TPU v7x, 32 devices: a whole 2x2x4 slice. The times are simulated.
32 devices in a mesh: dp: 16 (over z, y, x), tensor: 2 (over core).
Axes of the slice: x: 2, y: 2, z: 4, core: 2. Of those that a mesh axis runs over, the one named last changes fastest.
Arguments:
- residual_in: float32 [16, 2048, 640], P('dp'), may hold values from -6 to 6
- cotangent: float32 [16, 2048, 640], P('dp'), may hold values from -6 to 6
- segment_ids: int32 [16, 2048], P('dp'), may hold values from 0 to 15, never falling along the last dimension, each value on 1 to 512 neighbouring positions
- gain_attn_in: float32 [640], replicated, may hold values from 0.25 to 1.75
- w_query: bfloat16 [640, 1024], P(None, 'tensor'), may hold values from -0.25 to 0.25
- w_key: bfloat16 [640, 256], replicated, may hold values from -0.25 to 0.25
- w_value: bfloat16 [640, 256], replicated, may hold values from -0.25 to 0.25
- gain_query: float32 [256], replicated, may hold values from 0.5 to 4
- gain_key: float32 [256], replicated, may hold values from 0.5 to 4
- w_out: bfloat16 [1024, 640], P('tensor'), may hold values from -0.1875 to 0.1875
- gain_attn_out: float32 [640], replicated, may hold values from 0.25 to 1.75
- gain_ff_in: float32 [640], replicated, may hold values from 0.25 to 1.75
- w_gate: bfloat16 [640, 2048], P(None, 'tensor'), may hold values from -0.25 to 0.25
- w_up: bfloat16 [640, 2048], P(None, 'tensor'), may hold values from -0.25 to 0.25
- w_down: bfloat16 [2048, 640], P('tensor'), may hold values from -0.125 to 0.125
- gain_ff_out: float32 [640], replicated, may hold values from 0.25 to 1.75
Outputs:
- output: float32 [16, 2048, 640], P('dp', 'tensor')
- grad_input: float32 [16, 2048, 640], P('dp', 'tensor')
- grad_gain_attn_in: float32 [640], replicated
- grad_w_query: float32 [640, 1024], P(None, ('tensor', 'dp'))
- grad_w_key: float32 [640, 256], replicated
- grad_w_value: float32 [640, 256], replicated
- grad_gain_query: float32 [256], replicated
- grad_gain_key: float32 [256], replicated
- grad_w_out: float32 [1024, 640], P('tensor', 'dp')
- grad_gain_attn_out: float32 [640], replicated
- grad_gain_ff_in: float32 [640], replicated
- grad_w_gate: float32 [640, 2048], P(None, ('tensor', 'dp'))
- grad_w_up: float32 [640, 2048], P(None, ('tensor', 'dp'))
- grad_w_down: float32 [2048, 640], P('tensor', 'dp')
- grad_gain_ff_out: float32 [640], replicated
Inputs may be any that keep to these rules, and one draw needn't show every extreme that they name: `segment_ids`: each row holds 16 sequences numbered from 0 upward in order without gaps; each has 1 to 512 tokens and some sequence of each row has exactly 512.
All inputs are finite; a program needn't handle non-finite values.
Results may differ from a plain program's by a relative error of at most 0.015.
The roundings to bfloat16 on the way count: a program that leaves them out, or rounds other values in their place, can miss the bound.
Values may be sent and summed in bfloat16 or wider, within the bound.
A program may use at most 256 MiB of HBM per device.

v0:
```python
import jax
import jax.numpy as jnp
from jax import lax
from jax.sharding import PartitionSpec as P

D = 640
HEAD_WIDTH = 256
BLOCK = 512


EPS = 1e-06
THETA = 1000000.0
SCORE_SCALE = 0.0625
GELU_C = 0.7978845608028654
GELU_A = 0.044715


def product(left, right):
    return jnp.dot(left, right, preferred_element_type=jnp.float32)


def product_tn(left, right):
    return lax.dot_general(
        left, right, (((0,), (0,)), ((), ())), preferred_element_type=jnp.float32
    )


def product_nt(left, right):
    return lax.dot_general(
        left, right, (((1,), (1,)), ((), ())), preferred_element_type=jnp.float32
    )


def rms_forward(values, gain):
    inv_rms = lax.rsqrt(jnp.mean(values * values, axis=-1, keepdims=True) + EPS)
    normed = values * inv_rms
    return (normed * gain, normed, inv_rms)


def rms_backward(normed, inv_rms, gain, upstream):
    scaled = upstream * gain
    return inv_rms * (scaled - normed * jnp.mean(scaled * normed, axis=-1, keepdims=True))


def positions_of(segment_row):
    token_count = segment_row.shape[0]
    index_row = jnp.arange(token_count, dtype=jnp.int32)
    first_pos = jnp.concatenate([jnp.ones((1,), bool), segment_row[1:] != segment_row[:-1]])
    start_row = lax.cummax(jnp.where(first_pos, index_row, 0), axis=0)
    return index_row - start_row


def rope_tables(positions):
    freq_index = jnp.arange(HEAD_WIDTH // 2, dtype=jnp.float32)
    inv_freq = jnp.exp(freq_index * (-2.0 * jnp.log(THETA) / HEAD_WIDTH))
    angles = positions.astype(jnp.float32)[:, None] * inv_freq[None, :]
    return (jnp.cos(angles)[:, None, :], jnp.sin(angles)[:, None, :])


def rotate(values, cos_tab, sin_tab, direction):
    half_a = values[..., : HEAD_WIDTH // 2]
    half_b = values[..., HEAD_WIDTH // 2 :]
    return jnp.concatenate(
        [
            half_a * cos_tab - direction * half_b * sin_tab,
            half_b * cos_tab + direction * half_a * sin_tab,
        ],
        axis=-1,
    )


def windows(values, front):
    blocks = values.shape[0] // BLOCK
    padded = jnp.concatenate([front, values], axis=0)
    padded = padded.reshape((blocks + 1, BLOCK) + values.shape[1:])
    return jnp.concatenate([padded[:-1], padded[1:]], axis=1)


def window_restore(win_grad):
    own_part = win_grad[:, BLOCK:]
    next_part = jnp.concatenate(
        [win_grad[1:, :BLOCK], jnp.zeros_like(win_grad[:1, :BLOCK])], axis=0
    )
    total = own_part + next_part
    return (total.reshape((total.shape[0] * BLOCK,) + total.shape[2:]), win_grad[0, :BLOCK])


def block_mask(segment_row):
    token_count = segment_row.shape[0]
    blocks = token_count // BLOCK
    index_row = jnp.arange(token_count, dtype=jnp.int32)
    filler = jnp.full((BLOCK,), -1, jnp.int32)
    key_seg = windows(segment_row, filler)
    key_index = windows(index_row, filler)
    query_seg = segment_row.reshape(blocks, BLOCK)
    query_index = index_row.reshape(blocks, BLOCK)
    return (key_seg[:, None, :] == query_seg[:, :, None]) & (
        key_index[:, None, :] <= query_index[:, :, None]
    )


def attn_scores(query_rot, key_rot, key_front, seg_mask):
    token_count, head_total_count = (query_rot.shape[0], query_rot.shape[1])
    blocks = token_count // BLOCK
    query_block = query_rot.reshape(blocks, BLOCK, head_total_count, HEAD_WIDTH)
    key_window = windows(key_rot, key_front)
    logit_scores = (
        jnp.einsum("pjlu,pvu->pljv", query_block, key_window, preferred_element_type=jnp.float32)
        * SCORE_SCALE
    )
    return (jnp.where(seg_mask[:, None], logit_scores, -jnp.inf), query_block, key_window)


def attend_forward(query_rot, key_rot, value_b, key_front, value_front, seg_mask):
    token_count, head_total_count = (query_rot.shape[0], query_rot.shape[1])
    logit_scores, query_block, key_window = attn_scores(query_rot, key_rot, key_front, seg_mask)
    value_window = windows(value_b, value_front)
    row_max = jnp.max(logit_scores, axis=-1, keepdims=True)
    log_total = row_max + jnp.log(jnp.sum(jnp.exp(logit_scores - row_max), axis=-1, keepdims=True))
    attention_weights = jnp.exp(logit_scores - log_total).astype(jnp.bfloat16)
    attention_mixed = jnp.einsum(
        "ipjv,ivx->ijpx", attention_weights, value_window, preferred_element_type=jnp.float32
    )
    return (attention_mixed.reshape(token_count, head_total_count, HEAD_WIDTH), log_total)


def attend_backward(
    query_rot,
    key_rot,
    value_b,
    key_front,
    value_front,
    seg_mask,
    attention_mixed,
    log_total,
    grad_out,
):
    token_count, head_total_count = (query_rot.shape[0], query_rot.shape[1])
    blocks = token_count // BLOCK
    logit_scores, query_block, key_window = attn_scores(query_rot, key_rot, key_front, seg_mask)
    value_window = windows(value_b, value_front)
    attention_weights = jnp.exp(logit_scores - log_total)
    probability_rows = attention_weights.astype(jnp.bfloat16)
    gradient_block = grad_out.reshape(blocks, BLOCK, head_total_count, HEAD_WIDTH)
    probability_gradient = jnp.einsum(
        "pjlu,pvu->pljv", gradient_block, value_window, preferred_element_type=jnp.float32
    )
    row_delta = jnp.sum(grad_out.astype(jnp.float32) * attention_mixed, axis=-1)
    row_delta = row_delta.reshape(blocks, BLOCK, head_total_count).transpose(0, 2, 1)[..., None]
    score_gradient = (attention_weights * (probability_gradient - row_delta) * SCORE_SCALE).astype(
        jnp.bfloat16
    )
    query_gradient = jnp.einsum(
        "ipjv,ivx->ijpx", score_gradient, key_window, preferred_element_type=jnp.float32
    )
    key_gradient, key_back = window_restore(
        jnp.einsum(
            "vptl,vtpm->vlm", score_gradient, query_block, preferred_element_type=jnp.float32
        )
    )
    value_gradient, value_back = window_restore(
        jnp.einsum(
            "vptl,vtpm->vlm", probability_rows, gradient_block, preferred_element_type=jnp.float32
        )
    )
    return (
        query_gradient.reshape(token_count, head_total_count, HEAD_WIDTH),
        key_gradient,
        value_gradient,
        key_back,
        value_back,
    )


def on_device(
    residual_in,
    cotangent,
    segment_ids,
    gain_attn_in,
    w_query,
    w_key,
    w_value,
    gain_query,
    gain_key,
    w_out,
    gain_attn_out,
    gain_ff_in,
    w_gate,
    w_up,
    w_down,
    gain_ff_out,
):
    inputs_all = residual_in[0]
    upstream_all = cotangent[0]
    segment_row = segment_ids[0]
    tok_total = inputs_all.shape[0]
    row_share = tok_total // lax.axis_size("tensor")
    first_row = lax.axis_index("tensor") * row_share

    def own_rows(values):
        return lax.dynamic_slice_in_dim(values, first_row, row_share, 0)

    def mine(values):
        return own_rows(values)

    cos_full, sin_full = rope_tables(positions_of(segment_row))
    mask_full = block_mask(segment_row)
    inputs, upstream, cos_tab, sin_tab, seg_mask = (
        inputs_all,
        upstream_all,
        cos_full,
        sin_full,
        mask_full,
    )
    query_full, gate_full, up_full, out_full, down_full = (w_query, w_gate, w_up, w_out, w_down)
    token_count = inputs.shape[0]
    head_total_count = query_full.shape[1] // HEAD_WIDTH
    normed_in, hat_in, inv_in = rms_forward(inputs, gain_attn_in)
    normed_b = normed_in.astype(jnp.bfloat16)
    query_lin = product(normed_b, query_full).reshape(token_count, head_total_count, HEAD_WIDTH)
    key_lin = product(normed_b, w_key).reshape(token_count, 1, HEAD_WIDTH)
    value_b = product(normed_b, w_value).astype(jnp.bfloat16)
    query_n, query_hat, query_inv = rms_forward(query_lin, gain_query)
    key_n, key_hat, key_inv = rms_forward(key_lin, gain_key)
    query_b = rotate(query_n, cos_tab, sin_tab, 1.0).astype(jnp.bfloat16)
    key_b = rotate(key_n, cos_tab, sin_tab, 1.0).astype(jnp.bfloat16)[:, 0]
    key_front = jnp.zeros((BLOCK, HEAD_WIDTH), jnp.bfloat16)
    value_front = jnp.zeros((BLOCK, HEAD_WIDTH), jnp.bfloat16)
    attention_mixed, log_total = attend_forward(
        query_b, key_b, value_b, key_front, value_front, seg_mask
    )
    attn_flat = attention_mixed.reshape(token_count, head_total_count * HEAD_WIDTH).astype(
        jnp.bfloat16
    )
    attn_part = product(attn_flat, out_full)
    attn_sum = lax.psum(attn_part, "tensor")
    branch_attn, hat_attn, inv_attn = rms_forward(attn_sum, gain_attn_out)
    middle = inputs + branch_attn
    normed_mid, hat_mid, inv_mid = rms_forward(middle, gain_ff_in)
    mid_b = normed_mid.astype(jnp.bfloat16)
    gate_proj = product(mid_b, gate_full)
    up_proj = product(mid_b, up_full)
    tanh_part = jnp.tanh(GELU_C * (gate_proj + GELU_A * gate_proj * gate_proj * gate_proj))
    gelu_val = 0.5 * gate_proj * (1.0 + tanh_part)
    act_b = (gelu_val * up_proj).astype(jnp.bfloat16)
    ff_part = product(act_b, down_full)
    ff_sum = lax.psum(ff_part, "tensor")
    branch_ff, hat_ff, inv_ff = rms_forward(ff_sum, gain_ff_out)
    output = middle + branch_ff
    query_width = query_full.shape[1] // w_query.shape[1]
    unit_width = gate_full.shape[1] // w_gate.shape[1]
    grad_gain_ff_out = jnp.sum(mine(upstream) * mine(hat_ff), axis=0)
    grad_ff = rms_backward(hat_ff, inv_ff, gain_ff_out, upstream).astype(jnp.bfloat16)
    grad_w_down = product_tn(act_b, grad_ff)
    grad_act = product_nt(grad_ff, down_full)
    gelu_deriv = 0.5 * (1.0 + tanh_part) + 0.5 * gate_proj * (
        1.0 - tanh_part * tanh_part
    ) * GELU_C * (1.0 + 3.0 * GELU_A * gate_proj * gate_proj)
    grad_gate = (grad_act * up_proj * gelu_deriv).astype(jnp.bfloat16)
    grad_up = (grad_act * gelu_val).astype(jnp.bfloat16)
    grad_w_gate = product_tn(mid_b, grad_gate).reshape(D, unit_width, -1)
    grad_w_up = product_tn(mid_b, grad_up).reshape(D, unit_width, -1)
    grad_w_down = grad_w_down.reshape(grad_w_down.shape[0], 1, D)
    grad_mid_n = product_nt(grad_gate, gate_full) + product_nt(grad_up, up_full)
    grad_gain_ff_in = jnp.sum(grad_mid_n * hat_mid, axis=0)
    mid_term = rms_backward(hat_mid, inv_mid, gain_ff_in, grad_mid_n)
    grad_middle = upstream + lax.psum(mid_term, "tensor")
    grad_gain_attn_out = jnp.sum(mine(grad_middle) * mine(hat_attn), axis=0)
    grad_attn_sum = rms_backward(hat_attn, inv_attn, gain_attn_out, grad_middle).astype(
        jnp.bfloat16
    )
    grad_w_out = product_tn(attn_flat, grad_attn_sum)
    grad_attn = (
        product_nt(grad_attn_sum, out_full)
        .astype(jnp.bfloat16)
        .reshape(token_count, head_total_count, HEAD_WIDTH)
    )
    key_backs = []
    value_backs = []
    query_gradient, key_gradient, value_gradient, key_back, value_back = attend_backward(
        query_b,
        key_b,
        value_b,
        key_front,
        value_front,
        seg_mask,
        attention_mixed,
        log_total,
        grad_attn,
    )
    key_backs.append(key_back)
    value_backs.append(value_back)
    grad_gain_key = jnp.zeros((HEAD_WIDTH,), jnp.float32)
    key_grad_n = rotate(key_gradient[:, None], cos_tab, sin_tab, -1.0)
    grad_gain_key = grad_gain_key + jnp.sum(key_grad_n * key_hat, axis=(0, 1))
    key_raw = rms_backward(key_hat, key_inv, gain_key, key_grad_n).astype(jnp.bfloat16)[:, 0]
    value_raw = value_gradient.astype(jnp.bfloat16)
    grad_w_key = product_tn(normed_b, key_raw)
    grad_w_value = product_tn(normed_b, value_raw)
    grad_normed = product_nt(key_raw, w_key) + product_nt(value_raw, w_value)
    query_grad_n = rotate(query_gradient, cos_tab, sin_tab, -1.0)
    grad_gain_query = jnp.sum(query_grad_n * query_hat, axis=(0, 1))
    query_raw = (
        rms_backward(query_hat, query_inv, gain_query, query_grad_n)
        .astype(jnp.bfloat16)
        .reshape(token_count, head_total_count * HEAD_WIDTH)
    )
    grad_w_query = product_tn(normed_b, query_raw).reshape(D, query_width, -1)
    grad_w_out = grad_w_out.reshape(grad_w_out.shape[0], 1, D)
    grad_normed = grad_normed + product_nt(query_raw, query_full)
    grad_gain_attn_in = jnp.sum(grad_normed * hat_in, axis=0)
    in_term = rms_backward(hat_in, inv_in, gain_attn_in, grad_normed)
    grad_input = grad_middle + lax.psum(in_term, "tensor")
    share_query, share_out, share_gate, share_up, share_down = (
        lax.psum_scatter(grad_w_query, "dp", scatter_dimension=2, tiled=True),
        lax.psum_scatter(grad_w_out, "dp", scatter_dimension=2, tiled=True),
        lax.psum_scatter(grad_w_gate, "dp", scatter_dimension=2, tiled=True),
        lax.psum_scatter(grad_w_up, "dp", scatter_dimension=2, tiled=True),
        lax.psum_scatter(grad_w_down, "dp", scatter_dimension=2, tiled=True),
    )
    share_query = share_query.reshape(D, -1)
    share_gate = share_gate.reshape(D, -1)
    share_up = share_up.reshape(D, -1)
    share_out = share_out.reshape(share_out.shape[0], -1)
    share_down = share_down.reshape(share_down.shape[0], -1)
    shared_sums = lax.psum(
        (
            grad_gain_attn_in,
            grad_w_key,
            grad_w_value,
            grad_gain_query,
            grad_gain_key,
            grad_gain_attn_out,
            grad_gain_ff_in,
            grad_gain_ff_out,
        ),
        ("dp", "tensor"),
    )
    return (
        mine(output)[None],
        mine(grad_input)[None],
        shared_sums[0],
        share_query,
        shared_sums[1],
        shared_sums[2],
        shared_sums[3],
        shared_sums[4],
        share_out,
        shared_sums[5],
        shared_sums[6],
        share_gate,
        share_up,
        share_down,
        shared_sums[7],
    )


def solution(mesh):
    return jax.shard_map(
        on_device,
        mesh=mesh,
        in_specs=(
            P("dp", None, None),
            P("dp", None, None),
            P("dp", None),
            P(),
            P(None, "tensor"),
            P(),
            P(),
            P(),
            P(),
            P("tensor", None),
            P(),
            P(),
            P(None, "tensor"),
            P(None, "tensor"),
            P("tensor", None),
            P(),
        ),
        out_specs=(
            P("dp", "tensor", None),
            P("dp", "tensor", None),
            P(),
            P(None, ("tensor", "dp")),
            P(),
            P(),
            P(),
            P(),
            P("tensor", "dp"),
            P(),
            P(),
            P(None, ("tensor", "dp")),
            P(None, ("tensor", "dp")),
            P("tensor", "dp"),
            P(),
        ),
        check_vma=False,
    )
```

profile of v0, /device:TPU:1, one launch (start us, length us, event | category | flops | bytes accessed | tf_op | source)
XLA Modules:
  0.0 850.1 jit_solution(15098856227065348030)
XLA Ops:
  10.8 3.0 fusion.12
  14.8 2.0 multiply_convert_fusion.5
  18.8 6.2 broadcast_multiply_fusion.2
  25.4 5.5 fusion.44
  32.4 5.7 multiply_reduce_fusion.11
  42.1 2.6 compare_and_fusion
  44.7 2.4 fusion.51
  48.6 1.9 subtract_convert_fusion
  50.5 5.0 fusion.4
  55.6 3.9 exponential_reduce_fusion
  59.5 1.8 copy-done.11
  61.3 10.4 %bitcast_convert_fusion = (bf16[4,512,2,256]{1,3,2,0:T(8,128)(2,1)}, f32[4,256,2,512]{3,1,2,0:T(8,128)}) fusion(f32[4,1024,512,2]{2,1,3,0:T(8,128)} %copy-done.11, f32[4,2,512]{2,1,0:T(2,128)S(1)} %bitcast.255, pred[4,512,1024]{1,2,0:T(8,128)(4,1)S(1)} %compare_and_fusion, bf16[4,512,256]{1,2,0:T(8,128)(2,1)} %copy.69, bf16[4,512,256]{1,2,0:T(8,128)(2,1)} %copy.68), kind=kOutput, calls=%fused_computation.47 | convolution fusion | flops 2169503744 | bytes 27279360 | tf_op jit(solution)/shard_map/ipjv,ivx->ijpx/dot_general | solution.py:121
  71.8 5.0 copy.74
  78.6 4.2 fusion.60
  82.8 32.2 %all-reduce.20.cloned.1.call-done = f32[2048,640]{1,0:T(8,128)} async-done(((f32[2048,640]{1,0:T(8,128)}), f32[2048,640]{1,0:T(8,128)}) %all-reduce.20.cloned.1.call-update) | async-done | bytes 5242896 | tf_op jit(solution)/shard_map/psum | solution.py:236
  115.0 3.0 multiply_reduce_fusion.8
  119.1 4.8 multiply_reduce_fusion.7
  123.8 2.3 copy-done.3
  126.7 3.4 fusion.61
  130.2 7.2 multiply_convert_fusion.1
  137.3 2.0 copy-done.70
  139.3 5.1 fusion.62
  144.6 30.9 %all-reduce.22.cloned.1.call-done = f32[2048,640]{1,0:T(8,128)} async-done(((f32[2048,640]{1,0:T(8,128)}), f32[2048,640]{1,0:T(8,128)}) %all-reduce.22.cloned.1.call-update) | async-done | bytes 5242896 | tf_op jit(solution)/shard_map/psum | solution.py:247
  175.5 3.0 multiply_reduce_fusion.6
  178.6 4.9 multiply_reduce_fusion.5
  186.2 15.7 %multiply_convert_fusion = (bf16[2048,1024]{1,0:T(8,128)(2,1)}, bf16[2048,1024]{1,0:T(8,128)(2,1)}) fusion(f32[2048,1024]{1,0:T(8,128)} %copy-done.71, f32[2048,1024]{1,0:T(8,128)} %get-tuple-element.99, bf16[2048,640]{1,0:T(8,128)(2,1)S(1)} %multiply_convert_fusion.3, bf16[1024,640]{1,0:T(8,128)(2,1)S(1)} %copy-done.66), kind=kOutput, calls=%fused_computation.18 | convolution fusion | flops 2732589056 | bytes 29097984 | tf_op jit(solution)/shard_map/dot_general | solution.py:29
  201.9 5.3 fusion.63
  207.2 6.1 multiply_reduce_fusion
  213.3 2.9 subtract_multiply_fusion.1
  216.3 30.9 %all-reduce.24.cloned.1.call-done = f32[2048,640]{1,0:T(8,128)} async-done(((f32[2048,640]{1,0:T(8,128)}), f32[2048,640]{1,0:T(8,128)}) %all-reduce.24.cloned.1.call-update) | async-done | bytes 5242896 | tf_op jit(solution)/shard_map/psum | solution.py:267
  247.3 6.5 multiply_reduce_fusion.3
  257.6 1.8 convolution_convert_fusion
  259.5 2.1 reshape_reshape.4
  261.5 4.7 copy.77
  266.3 3.7 fusion.13
  270.5 12.1 %fusion.2 = bf16[4,2,512,1024]{2,3,1,0:T(8,128)(2,1)} fusion(f32[4,1024,512,2]{2,1,3,0:T(8,128)} %copy-done.11, bf16[4,512,2,256]{1,3,2,0:T(8,128)(2,1)S(1)} %copy.77, f32[4,2,512]{2,1,0:T(2,128)S(1)} %bitcast.254, f32[4,2,512]{2,1,0:T(2,128)S(1)} %bitcast.256, pred[4,512,1024]{1,2,0:T(8,128)(4,1)S(1)} %copy-done.16, ...), kind=kOutput, calls=%fused_computation.3 | convolution fusion | flops 2181038080 | bytes 31490048 | tf_op jit(solution)/shard_map/pjlu,pvu->pljv/dot_general | solution.py:145
  282.6 8.2 convolution_bitcast_fusion
  290.9 7.9 convolution_bitcast_fusion.2
  298.8 8.3 convolution_bitcast_fusion.1
  307.1 5.5 copy.81
  312.6 2.8 multiply_subtract_fusion
  317.7 2.7 multiply_convert_fusion.7
  320.4 3.0 copy.82
  323.4 1.9 fusion.65
  326.3 4.5 fusion.48
  336.4 2.6 multiply_reduce_fusion.1
  339.0 2.9 subtract_multiply_fusion
  342.0 7.4 convolution_bitcast_fusion.5
  349.4 6.8 copy.85
  356.3 7.5 convolution_bitcast_fusion.4
  363.8 6.7 copy.86
  370.5 8.3 convolution_bitcast_fusion.3
  378.8 6.5 copy.87
  385.3 3.3 fusion.39
  388.7 2.1 copy.83
  390.8 4.2 convolution_bitcast_fusion.6
  395.0 2.1 copy.84
  400.3 5.5 fusion.16
  409.4 5.3 multiply_reduce_fusion.12
  414.8 44.1 %all-reduce.10 = (f32[640]{0:T(1024)}, f32[256]{0:T(256)}, f32[256]{0:T(256)}, f32[640]{0:T(1024)}, f32[640]{0:T(1024)}, /*index=5*/f32[640]{0:T(1024)}) all-reduce(f32[640]{0:T(1024)S(1)} %get-tuple-element.47, f32[256]{0:T(256)S(1)} %get-tuple-element.49, ...), channel_id=1, replica_groups=mesh['dp'=16,'tensor'=2] {'dp','tensor'}, use_global_device_ids=true, to_apply=%region_22.23 | all-reduce | flops 3072 | bytes 24576 | tf_op jit(solution)/shard_map/psum | solution.py:326
  458.9 243.6 %all-reduce.30.cloned.1.call-done = (f32[640,1,512]{0,1,2:T(1,128)}, f32[512,1,640]{0,1,2:T(1,128)}, f32[640,1,1024]{0,1,2:T(1,128)}, f32[640,1,1024]{0,1,2:T(1,128)}, f32[1024,1,640]{0,1,2:T(1,128)}) async-done(((f32[640,1,512]{0,1,2:T(1,128)}, f32[512,1,640]{0,1,2:T(1,128)}, f32[640,1,1024]{0,1,2:T(1,128)}, f32[640,1,1024]{0,1,2:T(1,128)}, f32[1024,1,640]{0,1,2:T(1,128)}), (f32[640,1,512]{0,1,2:T(1,128)}, ...) | async-done | bytes 10485776
  710.5 128.5 %all-reduce.28.cloned.1.call-done = (f32[640,256]{1,0:T(8,128)}, f32[640,256]{1,0:T(8,128)}) async-done(((f32[640,256]{1,0:T(8,128)}, f32[640,256]{1,0:T(8,128)}), (f32[640,256]{1,0:T(8,128)}, f32[640,256]{1,0:T(8,128)})) %all-reduce.28.cloned.1.call-update) | async-done | bytes 1310736 | tf_op jit(solution)/shard_map/psum | solution.py:326
  839.0 2.0 copy.135
  840.9 2.0 copy.136
  (249 shorter events, 45.6 us)
Async XLA Ops:
  7.2 123.0 %copy-start = (bf16[640,1024]{1,0:T(8,128)(2,1)S(1)}, bf16[640,1024]{1,0:T(8,128)(2,1)}, u32[]{:S(2)}) copy-start(bf16[640,1024]{1,0:T(8,128)(2,1)} %param.29) | copy-start | bytes 3932164
  7.2 6.7 copy-start.52
  7.2 107.8 %all-reduce.20.cloned.1.call-start = ((), (), s32[]{:S(2)}) async-start(), calls=%async_computation | async-start | bytes 10485760 | tf_op jit(solution)/shard_map/psum | solution.py:236
  7.3 18.1 %copy-start.63 = (f32[128]{0:T(128)}, f32[128]{0:T(128)S(1)}, u32[]{:S(2)}) copy-start(f32[128]{0:T(128)S(1)} %multiply_exponential_fusion) | copy-start | bytes 1540
  10.8 4.0 copy-start.2
  14.8 23.3 %copy-start.44 = (f32[2048]{0:T(1024)}, f32[2048]{0:T(1024)S(1)}, u32[]{:S(2)}) copy-start(f32[2048]{0:T(1024)S(1)} %add_rsqrt_fusion.5) | copy-start | bytes 24580
  16.9 8.1 copy-start.60
  18.1 12.8 %copy-start.6 = (f32[2048,256]{1,0:T(8,128)}, f32[2048,256]{1,0:T(8,128)S(1)}, u32[]{:S(2)}) copy-start(f32[2048,256]{1,0:T(8,128)S(1)} %get-tuple-element.93) | copy-start | bytes 6291460
  18.1 12.8 %copy-start.48 = (f32[2048]{0:T(1024)}, f32[2048]{0:T(1024)S(1)}, u32[]{:S(2)}) copy-start(f32[2048]{0:T(1024)S(1)} %add_rsqrt_fusion.4) | copy-start | bytes 24580
  18.8 12.1 %copy-start.50 = (f32[2048]{0:T(1024)}, f32[2048]{0:T(1024)S(1)}, u32[]{:S(2)}) copy-start(f32[2048]{0:T(1024)S(1)} %fusion.52) | copy-start | bytes 24580
  30.9 7.3 slice-start
  32.4 5.8 slice-start.1
  32.4 5.8 copy-start.36
  38.2 8.9 %copy-start.46 = (f32[2048,2]{0,1:T(2,128)}, f32[2048,2]{0,1:T(2,128)S(1)}, u32[]{:S(2)}) copy-start(f32[2048,2]{0,1:T(2,128)S(1)} %add_rsqrt_fusion) | copy-start | bytes 49156
  39.4 7.7 copy-start.58
  40.7 4.0 copy-start.31
  42.1 5.1 copy-start.4
  44.7 16.6 %copy-start.15 = (pred[4,512,1024]{1,2,0:T(8,128)(4,1)}, pred[4,512,1024]{1,2,0:T(8,128)(4,1)S(1)}, u32[]{:S(2)}) copy-start(pred[4,512,1024]{1,2,0:T(8,128)(4,1)S(1)} %compare_and_fusion) | copy-start | bytes 6291460
  55.6 5.8 copy-start.11
  82.7 35.4 %copy-start.56 = (f32[640]{0:T(1024)S(1)}, f32[640]{0:T(1024)}, u32[]{:S(2)}) copy-start(f32[640]{0:T(1024)} %param.26) | copy-start | bytes 7684
  82.8 92.7 %all-reduce.22.cloned.1.call-start = ((), (), s32[]{:S(2)}) async-start(), calls=%async_computation.1 | async-start | bytes 10485760 | tf_op jit(solution)/shard_map/psum | solution.py:247
  115.0 4.0 copy-start.10
  119.1 7.1 copy-start.57
  126.7 3.5 copy-start.27
  130.2 7.2 copy-start.71
  130.2 9.2 %copy-start.65 = (bf16[1024,640]{1,0:T(8,128)(2,1)S(1)}, bf16[1024,640]{1,0:T(8,128)(2,1)}, u32[]{:S(2)}) copy-start(bf16[1024,640]{1,0:T(8,128)(2,1)} %param.30) | copy-start | bytes 3932164
  144.5 34.1 %copy-start.54 = (f32[640]{0:T(1024)S(1)}, f32[640]{0:T(1024)}, u32[]{:S(2)}) copy-start(f32[640]{0:T(1024)} %param.31) | copy-start | bytes 7684
  144.5 102.8 %all-reduce.24.cloned.1.call-start = ((), (), s32[]{:S(2)}) async-start(), calls=%async_computation.2 | async-start | bytes 10485760 | tf_op jit(solution)/shard_map/psum | solution.py:267
  175.5 8.1 slice-start.4
  178.6 5.0 slice-start.5
  183.6 23.6 %slice-start.6 = ((s8[5242880]{0:T(1024)(128)(4,1)}), s8[4194304]{0:T(1024)(128)(4,1)S(1)}, s32[]{:S(2)}) async-start(s8[5242880]{0:T(1024)(128)(4,1)} %bitcast.215), calls=%async_computation.12 | async-start | bytes 8388608
  186.2 15.7 %copy-start.28 = (bf16[2048,640]{1,0:T(8,128)(2,1)}, bf16[2048,640]{1,0:T(8,128)(2,1)S(1)}, u32[]{:S(2)}) copy-start(bf16[2048,640]{1,0:T(8,128)(2,1)S(1)} %multiply_convert_fusion.3) | copy-start | bytes 7864324
  186.2 15.7 %copy-start.68 = (bf16[640,1024]{1,0:T(8,128)(2,1)S(1)}, bf16[640,1024]{1,0:T(8,128)(2,1)}, u32[]{:S(2)}) copy-start(bf16[640,1024]{1,0:T(8,128)(2,1)} %param.28) | copy-start | bytes 3932164
  186.2 21.0 %slice-start.7 = ((s8[5242880]{0:T(1024)(128)(4,1)}), s8[1048576]{0:T(1024)(128)(4,1)S(1)}, s32[]{:S(2)}) async-start(s8[5242880]{0:T(1024)(128)(4,1)} %bitcast.215), calls=%async_computation.13 | async-start | bytes 2097152
  216.3 37.5 %slice-start.8 = ((s8[5242880]{0:T(1024)(128)(4,1)}), s8[1048576]{0:T(1024)(128)(4,1)S(1)}, s32[]{:S(2)}) async-start(s8[5242880]{0:T(1024)(128)(4,1)} %bitcast.217), calls=%async_computation.14 | async-start | bytes 2097152
  216.3 193.1 %all-reduce.26.cloned.1.call-start = ((), (), s32[]{:S(2)}) async-start(), calls=%async_computation.3 | async-start | bytes 10485760 | tf_op jit(solution)/shard_map/psum | solution.py:313
  247.3 6.7 slice-start.9
  254.0 3.7 copy-start.43
  266.3 16.3 %copy-start.17 = (bf16[4,512,2,256]{1,3,2,0:T(8,128)(2,1)}, bf16[4,512,2,256]{1,3,2,0:T(8,128)(2,1)S(1)}, u32[]{:S(2)}) copy-start(bf16[4,512,2,256]{1,3,2,0:T(8,128)(2,1)S(1)} %copy.77) | copy-start | bytes 6291460
  266.3 3.7 copy-start.16
  266.3 3.9 copy-start.38
  266.3 4.2 copy-start.39
  270.5 12.1 %copy-start.32 = (bf16[2048,1,128]{2,0,1:T(8,128)(2,1)S(1)}, bf16[2048,1,128]{2,0,1:T(8,128)(2,1)}, u32[]{:S(2)}) copy-start(bf16[2048,1,128]{2,0,1:T(8,128)(2,1)} %get-tuple-element.85) | copy-start | bytes 1572868
  270.5 12.1 %copy-start.33 = (bf16[2048,1,128]{2,0,1:T(8,128)(2,1)S(1)}, bf16[2048,1,128]{2,0,1:T(8,128)(2,1)}, u32[]{:S(2)}) copy-start(bf16[2048,1,128]{2,0,1:T(8,128)(2,1)} %get-tuple-element.86) | copy-start | bytes 1572868
  282.6 8.2 copy-start.40
  282.6 8.2 copy-start.41
  282.6 16.1 %slice-start.10 = ((s8[16777216]{0:T(1024)(128)(4,1)}), s8[4194304]{0:T(1024)(128)(4,1)S(1)}, s32[]{:S(2)}) async-start(s8[16777216]{0:T(1024)(128)(4,1)} %bitcast.219), calls=%async_computation.16 | async-start | bytes 8388608
  282.6 16.1 %slice-start.11 = ((s8[16777216]{0:T(1024)(128)(4,1)}), s8[4194304]{0:T(1024)(128)(4,1)S(1)}, s32[]{:S(2)}) async-start(s8[16777216]{0:T(1024)(128)(4,1)} %bitcast.219), calls=%async_computation.17 | async-start | bytes 8388608
  290.9 7.9 slice-start.12
  290.9 7.9 slice-start.13
  307.1 5.5 copy-start.14
  307.1 5.5 copy-start.20
  312.6 3.5 copy-start.5
  312.6 3.4 copy-start.47
  312.6 3.4 copy-start.59
  325.7 5.1 copy-start.7
  325.7 5.1 copy-start.49
  325.7 5.1 copy-start.61
  330.9 4.9 slice-start.2
  342.0 360.5 %all-reduce.30.cloned.1.call-start = ((), (), s32[]{:S(2)}) async-start(), calls=%async_computation.5 | async-start | bytes 20971520
  397.1 441.8 %all-reduce.28.cloned.1.call-start = ((), (), s32[]{:S(2)}) async-start(), calls=%async_computation.4 | async-start | bytes 2621440 | tf_op jit(solution)/shard_map/psum | solution.py:326
  400.3 5.6 copy-start.19
  400.3 5.6 copy-start.26
  409.4 433.5 %copy-start.1 = (bf16[640,1024]{1,0:T(8,128)(2,1)S(1)}, bf16[640,1024]{1,0:T(8,128)(2,1)}, u32[]{:S(2)}) copy-start(bf16[640,1024]{1,0:T(8,128)(2,1)} %param.29) | copy-start | bytes 3932164
  (28 other events, 55.0 us)
Sparse Core Ops, SparseCore 0:
  82.9 32.1 all-reduce.19
  144.6 30.8 all-reduce.21
  216.4 30.8 all-reduce.23
  342.1 30.8 all-reduce.25
  397.3 305.1 all-reduce.29
  708.5 130.4 all-reduce.27
where the time goes:
time: 856 us; the launch traced here: 850 us
  waiting for transfers between devices  466 us (54%)
  matrix products  148 us (17%)
  other arithmetic  91.3 us (11%)
  local copies, waits for them, and re-layouts  82 us (10%)
  blocking collectives  44.1 us (5%)
  between operations  17.5 us (2%)
    unnamed x7, waiting for transfers between devices  244 us
    psum x1, waiting for transfers between devices, on_device(): lax.psum((grad_gain_attn_in, grad_w_key, grad_w_value, grad_gain_query, g...  128 us
    psum x1, blocking collectives, on_device(): lax.psum((grad_gain_attn_in, grad_w_key, grad_w_value, grad_gain_query, g...  44.1 us
    dot_general x7, matrix products, product_nt(): lax.dot_general(left, right, (((1,), (1,)), ((), ())), preferred_element_...  34.4 us
    dot_general x7, matrix products, product_tn(): lax.dot_general(left, right, (((0,), (0,)), ((), ())), preferred_element_...  34.2 us
    psum x1, waiting for transfers between devices, on_device(): attn_sum = lax.psum(attn_part, 'tensor')  32.2 us
    unnamed x187, local copies, waits for them, and re-layouts  32.1 us
    psum x1, waiting for transfers between devices, on_device(): ff_sum = lax.psum(ff_part, 'tensor')  30.9 us
  transfers between devices with their start and end apart: 6, of which 5 were waited for; matrix products, arithmetic and copies ran while one was open for 9% of the time, Pallas kernels for 0%

commit v1 on v0

v1 whole, which is shorter than its diff:
```python
import functools
import jax
import jax.numpy as jnp
import numpy as np
from jax import lax
from jax.experimental import pallas as pl
from jax.experimental.pallas import tpu as pltpu
from jax.sharding import PartitionSpec as P

HEAD_WIDTH = 256
BLOCK = 512
EPS = 1e-06
THETA = 1000000.0
SCORE_SCALE = 0.0625
GELU_C = 0.7978845608028654
GELU_A = 0.044715
HALF = HEAD_WIDTH // 2
QB = 256
WIN = BLOCK + QB
LANES = 128
BF = jnp.bfloat16
F32 = jnp.float32
VMEM_LIMIT = 60 << 20


def nn(a, b):
    return lax.dot_general(a, b, (((1,), (0,)), ((), ())), preferred_element_type=F32)


def nt(a, b):
    return lax.dot_general(a, b, (((1,), (1,)), ((), ())), preferred_element_type=F32)


def tn(a, b):
    return lax.dot_general(a, b, (((0,), (0,)), ((), ())), preferred_element_type=F32)


def rms_stats(v):
    inv = lax.rsqrt(jnp.mean(v * v, axis=-1, keepdims=True) + EPS)
    return v * inv, inv


def rms_back(hat, inv, gain, up):
    scaled = up * gain
    return inv * (scaled - hat * jnp.mean(scaled * hat, axis=-1, keepdims=True))


def rotate(v, cos, sin, direction):
    a, b = v[:, :HALF], v[:, HALF:]
    if direction > 0:
        return jnp.concatenate([a * cos - b * sin, b * cos + a * sin], axis=-1)
    return jnp.concatenate([a * cos + b * sin, b * cos - a * sin], axis=-1)


def column_of(row):
    n = row.shape[1]
    return jnp.transpose(jnp.broadcast_to(row, (LANES, n)))


def rope_table():
    freq = np.arange(HALF, dtype=np.float32)
    inv_freq = np.exp(freq * np.float32(-2.0 * np.log(THETA) / HEAD_WIDTH)).astype(np.float32)
    angles = np.arange(BLOCK, dtype=np.float32)[:, None] * inv_freq[None, :]
    parts = []
    for tab in (np.cos(angles.astype(np.float64)), np.sin(angles.astype(np.float64))):
        tab = tab.astype(np.float32)
        hi = tab.astype(BF)
        lo = (tab - hi.astype(np.float32)).astype(BF)
        parts += [hi, lo]
    return np.concatenate(parts, axis=1)


def project_kernel(me, x, seg, starts, table, g_in, wq_o, wq_x, wk, wv, gq, gk,
                   q_o, q_x, ql_o, ql_x, k_out, v_out, kl_out, nb_out, cos_out, sin_out):
    i = pl.program_id(0)
    rows = x.shape[1]
    hat, _ = rms_stats(x[0])
    nb = (hat * g_in[...]).astype(BF)
    nb_out[...] = nb
    seg_col = column_of(seg[...])
    lane = lax.broadcasted_iota(jnp.int32, (rows, LANES), 1)
    start = jnp.sum(jnp.where(seg_col == lane, starts[...], 0.0), axis=1, keepdims=True)
    row = lax.broadcasted_iota(jnp.int32, (rows, 1), 0) + me[0] + (i - 1) * rows
    pos = row - start.astype(jnp.int32)
    hot = (lax.broadcasted_iota(jnp.int32, (rows, BLOCK), 1) == pos).astype(F32).astype(BF)
    cs = nn(hot, table[...])
    cos = cs[:, :LANES] + cs[:, LANES : 2 * LANES]
    sin = cs[:, 2 * LANES : 3 * LANES] + cs[:, 3 * LANES :]
    cos_out[...] = cos
    sin_out[...] = sin
    k_lin = nn(nb, wk[...])
    kl_out[...] = k_lin
    k_hat, _ = rms_stats(k_lin)
    k_out[...] = rotate(k_hat * gk[...], cos, sin, 1).astype(BF)
    v_out[...] = nn(nb, wv[...]).astype(BF)

    @pl.when(i > 0)
    def _():
        for w, lin_out, out in ((wq_o, ql_o, q_o), (wq_x, ql_x, q_x)):
            lin = nn(nb, w[...])
            lin_out[...] = lin
            for h in range(lin.shape[1] // HEAD_WIDTH):
                cols = slice(h * HEAD_WIDTH, (h + 1) * HEAD_WIDTH)
                q_hat, _ = rms_stats(lin[:, cols])
                out[:, cols] = rotate(q_hat * gq[...], cos, sin, 1).astype(BF)


def score_mask(seg_q, seg_k, rows, width):
    lane = lax.broadcasted_iota(jnp.int32, (rows, width), 1)
    sub = lax.broadcasted_iota(jnp.int32, (rows, width), 0)
    return (seg_q == seg_k) & (lane <= sub + (width - rows))


def block_kernel(x, up, seg, q_o, q_x, k, v, wo_o, wo_x, wg_o, wg_x, wu_o, wu_x, wd_o, wd_x,
                 g_ao, g_fi, g_fo,
                 out, gmid_out, ga_o, ga_x, af_o, af_x, lse_out, delta_out, mid_out, gff_out, gas_out,
                 act_o, act_x, gg_o, gg_x, gu_o, gu_x, gains,
                 mix, gate_s, up_s):
    i = pl.program_id(0)
    rows = x.shape[1]
    base = pl.multiple_of(i * rows, rows)
    k_win = k[pl.ds(base, WIN), :]
    v_win = v[pl.ds(base, WIN), :]
    seg_k = seg[:, pl.ds(base, WIN)]
    seg_q = column_of(seg[:, pl.ds(base + BLOCK, rows)])[:, :1]
    mask = score_mask(seg_q, seg_k, rows, WIN)
    heads_per = q_o.shape[1] // HEAD_WIDTH
    lses = []
    for part, (q, af) in enumerate(((q_o, af_o), (q_x, af_x))):
        for h in range(heads_per):
            cols = slice(h * HEAD_WIDTH, (h + 1) * HEAD_WIDTH)
            s = jnp.where(mask, nt(q[:, cols], k_win) * SCORE_SCALE, -jnp.inf)
            top = jnp.max(s, axis=-1, keepdims=True)
            lse = top + jnp.log(jnp.sum(jnp.exp(s - top), axis=-1, keepdims=True))
            lses.append(lse)
            p = jnp.exp(s - lse).astype(BF)
            m = nn(p, v_win)
            mix[part * heads_per + h] = m
            af[:, cols] = m.astype(BF)
    inputs = x[0]
    upstream = up[0]
    attn_sum = nn(af_o[...], wo_o[...]) + nn(af_x[...], wo_x[...])
    hat_attn, inv_attn = rms_stats(attn_sum)
    middle = inputs + hat_attn * g_ao[...]
    hat_mid, inv_mid = rms_stats(middle)
    mid_b = (hat_mid * g_fi[...]).astype(BF)
    mid_out[...] = mid_b
    ff_sum = None
    for part, (wg, wu, wd, act) in enumerate(((wg_o, wu_o, wd_o, act_o), (wg_x, wu_x, wd_x, act_x))):
        gate = nn(mid_b, wg[...])
        upp = nn(mid_b, wu[...])
        gate_s[part] = gate
        up_s[part] = upp
        th = jnp.tanh(GELU_C * (gate + GELU_A * gate * gate * gate))
        a = (0.5 * gate * (1.0 + th) * upp).astype(BF)
        act[...] = a
        f = nn(a, wd[...])
        ff_sum = f if ff_sum is None else ff_sum + f
    hat_ff, inv_ff = rms_stats(ff_sum)
    out[...] = middle + hat_ff * g_fo[...]
    gff = rms_back(hat_ff, inv_ff, g_fo[...], upstream).astype(BF)
    gff_out[...] = gff
    gmn = None
    for part, (wg, wu, wd, gg_out, gu_out) in enumerate(
        ((wg_o, wu_o, wd_o, gg_o, gu_o), (wg_x, wu_x, wd_x, gg_x, gu_x))
    ):
        gact = nt(gff, wd[...])
        gate = gate_s[part]
        upp = up_s[part]
        sq = gate * gate
        th = jnp.tanh(GELU_C * (gate + GELU_A * gate * sq))
        onep = 0.5 * (1.0 + th)
        deriv = onep + 0.5 * gate * (1.0 - th * th) * (GELU_C * (1.0 + 3.0 * GELU_A * sq))
        gg = (gact * upp * deriv).astype(BF)
        gu = (gact * (gate * onep)).astype(BF)
        gg_out[...] = gg
        gu_out[...] = gu
        t = nt(gg, wg[...]) + nt(gu, wu[...])
        gmn = t if gmn is None else gmn + t
    gmid = upstream + rms_back(hat_mid, inv_mid, g_fi[...], gmn)
    gmid_out[...] = gmid
    gas = rms_back(hat_attn, inv_attn, g_ao[...], gmid).astype(BF)
    gas_out[...] = gas
    deltas = []
    for part, (wo, ga) in enumerate(((wo_o, ga_o), (wo_x, ga_x))):
        g = nt(gas, wo[...]).astype(BF)
        ga[...] = g
        for h in range(heads_per):
            gh = g[:, h * HEAD_WIDTH : (h + 1) * HEAD_WIDTH].astype(F32)
            deltas.append(jnp.sum(gh * mix[part * heads_per + h], axis=-1, keepdims=True))
    lane = lax.broadcasted_iota(jnp.int32, (rows, LANES), 1)
    lse_all = jnp.zeros((rows, LANES), F32)
    delta_all = jnp.zeros((rows, LANES), F32)
    for n, (a, b) in enumerate(zip(lses, deltas)):
        lse_all = jnp.where(lane == n, a, lse_all)
        delta_all = jnp.where(lane == n, b, delta_all)
    lse_out[...] = lse_all
    delta_out[...] = delta_all

    @pl.when(i == 0)
    def _():
        gains[...] = jnp.zeros_like(gains)

    gains[0:1, :] += jnp.sum(upstream * hat_ff, axis=0, keepdims=True)
    gains[1:2, :] += jnp.sum(gmn * hat_mid, axis=0, keepdims=True)
    gains[2:3, :] += jnp.sum(gmid * hat_attn, axis=0, keepdims=True)


def attn_back_kernel(first, seg, q, k, v, ga, lse, delta, ql, cos, sin, gq, qraw, dk, dv, gain):
    i = pl.program_id(0)
    rows = q.shape[0]
    base = pl.multiple_of(i * rows, rows)

    @pl.when(i == 0)
    def _():
        dk[...] = jnp.zeros_like(dk)
        dv[...] = jnp.zeros_like(dv)
        gain[...] = jnp.zeros_like(gain)

    k_win = k[pl.ds(base, WIN), :]
    v_win = v[pl.ds(base, WIN), :]
    seg_k = seg[:, pl.ds(base, WIN)]
    seg_q = column_of(seg[:, pl.ds(base + BLOCK, rows)])[:, :1]
    mask = score_mask(seg_q, seg_k, rows, WIN)
    dk_sum = None
    dv_sum = None
    g_sum = None
    for h in range(q.shape[1] // HEAD_WIDTH):
        cols = slice(h * HEAD_WIDTH, (h + 1) * HEAD_WIDTH)
        qh = q[:, cols]
        gh = ga[:, cols]
        s = jnp.where(mask, nt(qh, k_win) * SCORE_SCALE, -jnp.inf)
        p = jnp.exp(s - lse[:, first + h : first + h + 1])
        dp = nt(gh, v_win)
        ds = (p * (dp - delta[:, first + h : first + h + 1]) * SCORE_SCALE).astype(BF)
        pb = p.astype(BF)
        dq = nn(ds, k_win)
        a = tn(ds, qh)
        b = tn(pb, gh)
        dk_sum = a if dk_sum is None else dk_sum + a
        dv_sum = b if dv_sum is None else dv_sum + b
        dqn = rotate(dq, cos[...], sin[...], -1)
        hat, inv = rms_stats(ql[:, cols])
        g = jnp.sum(dqn * hat, axis=0, keepdims=True)
        g_sum = g if g_sum is None else g_sum + g
        qraw[:, cols] = rms_back(hat, inv, gq[...], dqn).astype(BF)
    dk[pl.ds(base, WIN), :] += dk_sum
    dv[pl.ds(base, WIN), :] += dv_sum
    gain[...] += g_sum


def input_back_kernel(x, gmid, dk_o, dk_x, dv_o, dv_x, dk_r, dv_r, kl, cos, sin, gk, g_in,
                      qr_o, qr_x, wq_o, wq_x, wk, wv, gin_out, kraw_out, vraw_out, gains, gain_k):
    i = pl.program_id(0)
    last = pl.num_programs(0) - 1
    tail = (i == last).astype(F32)
    dk = dk_o[...] + dk_x[...] + tail * dk_r[...].astype(F32)
    dv = dv_o[...] + dv_x[...] + tail * dv_r[...].astype(F32)
    dkn = rotate(dk, cos[...], sin[...], -1)
    k_hat, k_inv = rms_stats(kl[...])
    kraw = rms_back(k_hat, k_inv, gk[...], dkn).astype(BF)
    vraw = dv.astype(BF)
    kraw_out[...] = kraw
    vraw_out[...] = vraw
    gn = nt(kraw, wk[...]) + nt(vraw, wv[...]) + nt(qr_o[...], wq_o[...]) + nt(qr_x[...], wq_x[...])
    hat, inv = rms_stats(x[0])
    gin_out[...] = gmid[...] + rms_back(hat, inv, g_in[...], gn)

    @pl.when(i == 0)
    def _():
        gains[...] = jnp.zeros_like(gains)
        gain_k[...] = jnp.zeros_like(gain_k)

    gains[...] += jnp.sum(gn * hat, axis=0, keepdims=True)
    gain_k[...] += jnp.sum(dkn * k_hat, axis=0, keepdims=True)


def whole(shape):
    return pl.BlockSpec(shape, lambda *_: (0,) * len(shape), pipeline_mode=pl.Buffered(1))


def rows_of(n, width, shift=0):
    if shift:
        return pl.BlockSpec((n, width), lambda i, *_: (jnp.maximum(i - shift, 0), 0))
    return pl.BlockSpec((n, width), lambda i, *_: (i, 0))


def params():
    return pltpu.CompilerParams(dimension_semantics=("arbitrary",), vmem_limit_bytes=VMEM_LIMIT)


def sds(shape, dtype):
    return jax.ShapeDtypeStruct(shape, dtype)


def project(first_row, x3, seg_ext, starts, table, g_in, wq_o, wq_x, wk, wv, gq, gk):
    depth = x3.shape[2]
    ext = seg_ext.shape[1]
    own = ext - BLOCK
    part = wq_o.shape[1]
    n = BLOCK
    me_block = lambda i, me: (0, jnp.maximum(me[0] // n + i - 1, 0), 0)
    return pl.pallas_call(
        project_kernel,
        grid_spec=pltpu.PrefetchScalarGridSpec(
            num_scalar_prefetch=1,
            grid=(ext // n,),
            in_specs=[
                pl.BlockSpec((1, n, depth), me_block),
                pl.BlockSpec((1, n), lambda i, *_: (0, i)),
                whole((1, LANES)),
                whole(table.shape),
                whole((1, depth)),
                whole(wq_o.shape), whole(wq_x.shape), whole(wk.shape), whole(wv.shape),
                whole((1, HEAD_WIDTH)), whole((1, HEAD_WIDTH)),
            ],
            out_specs=[
                rows_of(n, part, 1), rows_of(n, part, 1), rows_of(n, part, 1), rows_of(n, part, 1),
                rows_of(n, HEAD_WIDTH), rows_of(n, HEAD_WIDTH), rows_of(n, HEAD_WIDTH, 1),
                rows_of(n, depth, 1), rows_of(n, LANES, 1), rows_of(n, LANES, 1),
            ],
        ),
        out_shape=[
            sds((own, part), BF), sds((own, part), BF), sds((own, part), F32), sds((own, part), F32),
            sds((ext, HEAD_WIDTH), BF), sds((ext, HEAD_WIDTH), BF), sds((own, HEAD_WIDTH), F32),
            sds((own, depth), BF), sds((own, LANES), F32), sds((own, LANES), F32),
        ],
        compiler_params=params(),
        name="project",
    )(first_row, x3, seg_ext, starts, table, g_in, wq_o, wq_x, wk, wv, gq, gk)


def block_pass(first_row, x3, up3, seg_ext, q_o, q_x, k, v, weights, g_ao, g_fi, g_fo):
    depth = x3.shape[2]
    own, part = q_o.shape
    n = QB
    hidden = weights[2].shape[1]
    mine = pl.BlockSpec((1, n, depth), lambda i, me: (0, me[0] // n + i, 0))
    kern = lambda me, *refs: block_kernel(*refs)
    heads = 2 * part // HEAD_WIDTH
    return pl.pallas_call(
        kern,
        grid_spec=pltpu.PrefetchScalarGridSpec(
            num_scalar_prefetch=1,
            grid=(own // n,),
            in_specs=[mine, mine, whole(seg_ext.shape), rows_of(n, part), rows_of(n, part),
                      whole(k.shape), whole(v.shape)]
            + [whole(w.shape) for w in weights]
            + [whole((1, depth))] * 3,
            out_specs=[rows_of(n, depth)] * 2 + [rows_of(n, part)] * 4 + [rows_of(n, LANES)] * 2
            + [rows_of(n, depth)] * 3 + [rows_of(n, hidden)] * 6
            + [pl.BlockSpec((8, depth), lambda i, *_: (0, 0))],
            scratch_shapes=[
                pltpu.VMEM((heads, n, HEAD_WIDTH), F32),
                pltpu.VMEM((2, n, hidden), F32),
                pltpu.VMEM((2, n, hidden), F32),
            ],
        ),
        out_shape=[sds((own, depth), F32)] * 2 + [sds((own, part), BF)] * 4 + [sds((own, LANES), F32)] * 2
        + [sds((own, depth), BF)] * 3 + [sds((own, hidden), BF)] * 6 + [sds((8, depth), F32)],
        compiler_params=params(),
        name="block",
    )(first_row, x3, up3, seg_ext, q_o, q_x, k, v, *weights, g_ao, g_fi, g_fo)


def attn_back(first, seg_ext, q, k, v, ga, lse, delta, ql, cos, sin, gq):
    own, part = q.shape
    n = QB
    ext = k.shape[0]
    acc = pl.BlockSpec((ext, HEAD_WIDTH), lambda i: (0, 0))
    return pl.pallas_call(
        functools.partial(attn_back_kernel, first),
        grid=(own // n,),
        in_specs=[whole(seg_ext.shape), rows_of(n, part), whole(k.shape), whole(v.shape), rows_of(n, part),
                  rows_of(n, LANES), rows_of(n, LANES), rows_of(n, part), rows_of(n, LANES), rows_of(n, LANES),
                  whole((1, HEAD_WIDTH))],
        out_specs=[rows_of(n, part), acc, acc, pl.BlockSpec((1, HEAD_WIDTH), lambda i: (0, 0))],
        out_shape=[sds((own, part), BF), sds((ext, HEAD_WIDTH), F32), sds((ext, HEAD_WIDTH), F32),
                   sds((1, HEAD_WIDTH), F32)],
        compiler_params=params(),
        name="attn_back",
    )(seg_ext, q, k, v, ga, lse, delta, ql, cos, sin, gq)


def input_back(first_row, x3, gmid, dks, dvs, dk_r, dv_r, kl, cos, sin, gk, g_in, qr_o, qr_x, wq_o, wq_x, wk, wv):
    depth = x3.shape[2]
    own, part = qr_o.shape
    n = BLOCK
    kern = lambda me, *refs: input_back_kernel(*refs)
    later = pl.BlockSpec((n, HEAD_WIDTH), lambda i, *_: (i + 1, 0))
    return pl.pallas_call(
        kern,
        grid_spec=pltpu.PrefetchScalarGridSpec(
            num_scalar_prefetch=1,
            grid=(own // n,),
            in_specs=[pl.BlockSpec((1, n, depth), lambda i, me: (0, me[0] // n + i, 0)), rows_of(n, depth),
                      later, later, later, later, whole((n, HEAD_WIDTH)), whole((n, HEAD_WIDTH)),
                      rows_of(n, HEAD_WIDTH), rows_of(n, LANES), rows_of(n, LANES),
                      whole((1, HEAD_WIDTH)), whole((1, depth)), rows_of(n, part), rows_of(n, part),
                      whole(wq_o.shape), whole(wq_x.shape), whole(wk.shape), whole(wv.shape)],
            out_specs=[rows_of(n, depth), rows_of(n, HEAD_WIDTH), rows_of(n, HEAD_WIDTH),
                       pl.BlockSpec((1, depth), lambda i, *_: (0, 0)),
                       pl.BlockSpec((1, HEAD_WIDTH), lambda i, *_: (0, 0))],
        ),
        out_shape=[sds((own, depth), F32), sds((own, HEAD_WIDTH), BF), sds((own, HEAD_WIDTH), BF),
                   sds((1, depth), F32), sds((1, HEAD_WIDTH), F32)],
        compiler_params=params(),
        name="input_back",
    )(first_row, x3, gmid, dks[0], dks[1], dvs[0], dvs[1], dk_r, dv_r, kl, cos, sin, gk, g_in,
      qr_o, qr_x, wq_o, wq_x, wk, wv)


def swap(value, n_tensor):
    return lax.ppermute(value, "tensor", [(t, n_tensor - 1 - t) for t in range(n_tensor)])


def pair_sum(left_x, left_o, right, n_tensor):
    sent = tn(left_x, right).astype(BF)
    got = swap(sent, n_tensor)
    return (tn(left_o, right) + got.astype(F32)).astype(BF)


def bit_of(index, b):
    return lax.rem(lax.div(index, 2**b), 2)


def bit_orders(n_bits):
    plain = tuple(range(n_bits))
    turned = plain[1:] + plain[:1]
    lead = (plain[2],) + plain[:2] + plain[3:] if n_bits > 2 else plain[::-1]
    return plain, turned, lead


def natural_index(me, j, fixed, free):
    index = 0
    for b, flip in fixed:
        mine = bit_of(me, b)
        index = index + (1 - mine if flip else mine) * 2**b
    for k, b in enumerate(free):
        index = index + lax.rem(lax.div(j, 2 ** (len(free) - 1 - k)), 2) * 2**b
    return index


def reduce_kernel(items, kv_order, n_gain, *refs):
    n_items = len(items)
    refs = list(refs)
    take = lambda count: [refs.pop(0) for _ in range(count)]
    ins = []
    for order, given in items:
        ins.append(take(2 if given else 1))
    kv_in, g_block, g_in, gq_o, gq_x, g_k = take(6)
    outs = take(n_items)
    kv_out, gain_out = take(2)
    recvs, curs = [], []
    for order, given in items:
        n = len(order)
        first = 1 if given else 0
        recvs.append({s: refs.pop(0) for s in range(first, n)})
        curs.append({s: refs.pop(0) for s in range(1, n)})
    n_bits = len(kv_order)
    kv_core = refs.pop(0)
    kv_recv = take(n_bits)
    kv_cur = take(n_bits)
    kv_all = refs.pop(0)
    gain_own = take(n_gain)
    gain_got = take(n_gain)
    send_sems, recv_sems = take(2)

    me = lax.axis_index("dp")
    core = lax.axis_index("tensor")
    partner = lambda b: me + (1 - 2 * bit_of(me, b)) * 2**b
    barrier = pltpu.get_barrier_semaphore()
    for b in range(n_bits):
        pl.semaphore_signal(barrier, inc=1, device_id={"dp": partner(b)}, device_id_type=pl.DeviceIdType.MESH)
    pl.semaphore_signal(barrier, inc=1, device_id={"tensor": 1 - core}, device_id_type=pl.DeviceIdType.MESH)
    pl.semaphore_wait(barrier, n_bits + 1)

    counter = [0]
    sent = []

    def send(src, dst, device):
        k = counter[0]
        counter[0] += 1
        copy = pltpu.make_async_remote_copy(
            src_ref=src, dst_ref=dst, send_sem=send_sems.at[k], recv_sem=recv_sems.at[k],
            device_id=device, device_id_type=pl.DeviceIdType.MESH)
        copy.start()
        sent.append(copy)
        return copy

    flying = {}

    def start(n, s):
        order, given = items[n]
        total = len(order)
        half = 2 ** (total - s - 1)
        device = {"dp": partner(order[s])}
        if s == 0:
            copies = []
            for j in range(half):
                index = natural_index(me, j, ((order[0], True),), order[1:])
                copies.append(send(ins[n][0].at[index], recvs[n][0].at[j], device))
            flying[n] = copies
        else:
            away = (1 - bit_of(me, order[s])) * half
            flying[n] = [send(curs[n][s].at[pl.ds(away, half)], recvs[n][s], device)]

    def finish(n, s):
        order, given = items[n]
        total = len(order)
        half = 2 ** (total - s - 1)
        for copy in flying.pop(n, ()):
            copy.wait_recv()
        got = ins[n][1] if given and s == 0 else recvs[n][s]

        def keep_index(j):
            if s == 0:
                return natural_index(me, j, ((order[0], False),), order[1:])
            return bit_of(me, order[s]) * half + j

        held = ins[n][0] if s == 0 else curs[n][s]
        if s == total - 1:
            outs[n][...] = held[keep_index(0)].astype(F32) + got[0].astype(F32)
            return

        def body(j, carry):
            curs[n][s + 1][j] = (held[keep_index(j)].astype(F32) + got[j].astype(F32)).astype(BF)
            return carry

        lax.fori_loop(0, half, body, 0)
        start(n, s + 1)

    gain_own[0][...] = jnp.zeros_like(gain_own[0])
    gain_own[0][0:3, :] = g_block[0:3, :]
    gain_own[0][3:4, :] = g_in[...]
    gain_own[0][4:5, :HEAD_WIDTH] = gq_o[...] + gq_x[...]
    gain_own[0][5:6, :HEAD_WIDTH] = g_k[...]

    def gain_start(s):
        device = {"tensor": 1 - core} if s == 0 else {"dp": partner(s - 1)}
        return send(gain_own[s], gain_got[s], device)

    kv_copy = send(kv_in.at[1 - core], kv_core, {"tensor": 1 - core})
    for n, (order, given) in enumerate(items):
        if given:
            finish(n, 0)
        else:
            start(n, 0)
    gain_copy = gain_start(0)
    kv_copy.wait_recv()

    def kv_first(j, carry):
        index = natural_index(me, j, (), kv_order)
        kv_cur[0][j] = (kv_in[core, index].astype(F32) + kv_core[index].astype(F32)).astype(BF)
        return carry

    lax.fori_loop(0, 2**n_bits, kv_first, 0)

    def kv_start(s):
        half = 2 ** (n_bits - s - 1)
        away = (1 - bit_of(me, kv_order[s])) * half
        return send(kv_cur[s].at[pl.ds(away, half)], kv_recv[s], {"dp": partner(kv_order[s])})

    spot = 0
    for k, b in enumerate(kv_order):
        spot = spot + bit_of(me, b) * 2 ** (n_bits - 1 - k)
    kv_copy = kv_start(0)
    depth_of = [len(order) for order, _ in items]
    for step in range(n_bits):
        half = 2 ** (n_bits - step - 1)
        kv_copy.wait_recv()
        base = bit_of(me, kv_order[step]) * half
        if step < n_bits - 1:

            def kv_body(j, carry, step=step, base=base):
                kv_cur[step + 1][j] = (kv_cur[step][base + j].astype(F32) + kv_recv[step][j].astype(F32)).astype(BF)
                return carry

            lax.fori_loop(0, half, kv_body, 0)
            kv_copy = kv_start(step + 1)
        else:
            kv_all[core, spot] = (kv_cur[step][base].astype(F32) + kv_recv[step][0].astype(F32)).astype(BF)
        gain_copy.wait_recv()
        gain_own[step + 1][...] = gain_own[step][...] + gain_got[step][...]
        gain_copy = gain_start(step + 1)
        for n in range(n_items):
            s = step + (1 if items[n][1] else 0)
            if s < depth_of[n]:
                finish(n, s)
    gain_copy.wait_recv()
    gain_out[...] = gain_own[n_bits][...] + gain_got[n_bits][...]
    for s in reversed(range(n_bits)):
        size = 2 ** (n_bits - 1 - s)
        begin = 0
        for k in range(s + 1):
            begin = begin + bit_of(me, kv_order[k]) * 2 ** (n_bits - 1 - k)
        region = kv_all.at[core, pl.ds(begin, size)]
        copy = send(region, region, {"dp": partner(kv_order[s])})
        copy.wait_recv()
    copy = send(kv_all.at[core], kv_all.at[core], {"tensor": 1 - core})
    copy.wait_recv()

    def unpack(j, carry):
        index = natural_index(me, j, (), kv_order)
        for t in range(2):
            kv_out[t, index] = kv_all[t, j].astype(F32)
        return carry

    lax.fori_loop(0, 2**n_bits, unpack, 0)
    for copy in sent:
        copy.wait_send()


def reduce_all(n_dp, items, kv, kv_order, g_block, g_in, gq_o, gq_x, g_k):
    n_bits = len(kv_order)
    spec = []
    operands = []
    scratch = []
    outs = []
    copies = 0
    for value, got, order in items:
        n, c, width = value.shape
        given = got is not None
        spec.append((tuple(order), given))
        operands += [value, got] if given else [value]
        outs.append(sds((c, width), F32))
        first = 1 if given else 0
        scratch += [pltpu.VMEM((2 ** (n_bits - s - 1), c, width), BF) for s in range(first, n_bits)]
        scratch += [pltpu.VMEM((2 ** (n_bits - s), c, width), BF) for s in range(1, n_bits)]
        copies += n_bits - 1 + (0 if given else n // 2)
    _, n, c, width = kv.shape
    scratch += [pltpu.VMEM((n, c, width), BF)]
    scratch += [pltpu.VMEM((2 ** (n_bits - s - 1), c, width), BF) for s in range(n_bits)]
    scratch += [pltpu.VMEM((2 ** (n_bits - s), c, width), BF) for s in range(n_bits)]
    scratch += [pltpu.VMEM((2, n, c, width), BF)]
    scratch += [pltpu.VMEM((8, width), F32) for _ in range(2 * (n_bits + 1))]
    copies += 2 * n_bits + 2 + n_bits + 1
    scratch += [pltpu.SemaphoreType.DMA((copies,)), pltpu.SemaphoreType.DMA((copies,))]
    outs += [sds(kv.shape, F32), sds((8, width), F32)]
    vmem = pl.BlockSpec(memory_space=pltpu.VMEM)
    operands += [kv, g_block, g_in, gq_o, gq_x, g_k]
    return pl.pallas_call(
        functools.partial(reduce_kernel, tuple(spec), tuple(kv_order), n_bits + 1),
        out_shape=outs,
        in_specs=[vmem] * len(operands),
        out_specs=[vmem] * len(outs),
        scratch_shapes=scratch,
        compiler_params=pltpu.CompilerParams(collective_id=0, has_side_effects=True, vmem_limit_bytes=VMEM_LIMIT),
        name="reduce_all",
    )(*operands)


def first_hop(value, order, n_dp):
    n, c, width = value.shape
    b = order[0]
    me = lax.axis_index("dp")
    away = 1 - bit_of(me, b)
    view = value.reshape(n // 2 ** (b + 1), 2, 2**b, c, width)
    sent = lax.dynamic_index_in_dim(view, away, 1, keepdims=False)
    n_bits = len(order)
    high = n_bits - 1 - b
    sent = sent.reshape((2,) * (n_bits - 1) + (c, width))
    remaining = [k for k in reversed(range(n_bits)) if k != b]
    axes = [remaining.index(k) for k in order[1:]]
    sent = sent.transpose(axes + [n_bits - 1, n_bits]).reshape(n // 2, c, width)
    return lax.ppermute(sent, "dp", [(i, i ^ 2**b) for i in range(n_dp)])


def on_device(n_dp, n_tensor, residual_in, cotangent, segment_ids, gain_attn_in, w_query, w_key, w_value,
              gain_query, gain_key, w_out, gain_attn_out, gain_ff_in, w_gate, w_up, w_down, gain_ff_out):
    tokens, depth = residual_in.shape[1:]
    own = tokens // n_tensor
    me = lax.axis_index("tensor")
    first_row = (me * own).astype(jnp.int32).reshape(1)
    seg = segment_ids[0]
    seg_pad = jnp.concatenate([jnp.full((BLOCK,), -1, jnp.int32), seg])
    seg_ext = lax.dynamic_slice_in_dim(seg_pad, me * own, own + BLOCK, 0)[None]
    starts = jnp.sum((seg[None, :] < jnp.arange(LANES, dtype=jnp.int32)[:, None]).astype(F32), axis=1)[None]
    row = lambda g: g[None]
    wq_x, wo_x, wg_x, wu_x, wd_x = (swap(w, n_tensor) for w in (w_query, w_out, w_gate, w_up, w_down))
    table = jnp.asarray(rope_table())
    q_o, q_x, ql_o, ql_x, k, v, kl, nb, cos, sin = project(
        first_row, residual_in, seg_ext, starts, table, row(gain_attn_in), w_query, wq_x, w_key, w_value,
        row(gain_query), row(gain_key))
    weights = (w_out, wo_x, w_gate, wg_x, w_up, wu_x, w_down, wd_x)
    (output, gmid, ga_o, ga_x, af_o, af_x, lse, delta, mid_b, gff, gas,
     act_o, act_x, gg_o, gg_x, gu_o, gu_x, gains) = block_pass(
        first_row, residual_in, cotangent, seg_ext, q_o, q_x, k, v, weights,
        row(gain_attn_out), row(gain_ff_in), row(gain_ff_out))

    n_bits = n_dp.bit_length() - 1
    plain, turned, lead = bit_orders(n_bits)
    chunks = lambda value: value.reshape(n_dp, value.shape[0] // n_dp, value.shape[1])

    def down_pair():
        sent = tn(gff, act_x).astype(BF)
        got = swap(sent, n_tensor)
        return (tn(gff, act_o) + got.astype(F32)).astype(BF)

    down = chunks(down_pair())
    down_got = first_hop(down, plain, n_dp)
    gate = chunks(pair_sum(gg_x, gg_o, mid_b, n_tensor))
    gate_got = first_hop(gate, turned, n_dp)
    upw = chunks(pair_sum(gu_x, gu_o, mid_b, n_tensor))
    upw_got = first_hop(upw, lead, n_dp)
    out_sent = swap(tn(gas, af_x).astype(BF), n_tensor)
    out_w = chunks((tn(gas, af_o) + out_sent.astype(F32)).astype(BF))

    heads = q_o.shape[1] // HEAD_WIDTH
    qr_o, dk_o, dv_o, gq_o = attn_back(0, seg_ext, q_o, k, v, ga_o, lse, delta, ql_o, cos, sin, row(gain_query))
    qr_x, dk_x, dv_x, gq_x = attn_back(heads, seg_ext, q_x, k, v, ga_x, lse, delta, ql_x, cos, sin, row(gain_query))
    front = jnp.concatenate([dk_o[:BLOCK] + dk_x[:BLOCK], dv_o[:BLOCK] + dv_x[:BLOCK]], axis=1).astype(BF)
    back = lax.ppermute(front, "tensor", [(t, t - 1) for t in range(1, n_tensor)])
    grad_input, kraw, vraw, gain_in, gain_k = input_back(
        first_row, residual_in, gmid, (dk_o, dk_x), (dv_o, dv_x), back[:, :HEAD_WIDTH], back[:, HEAD_WIDTH:],
        kl, cos, sin, row(gain_key), row(gain_attn_in), qr_o, qr_x, w_query, wq_x, w_key, w_value)
    query = chunks(pair_sum(qr_x, qr_o, nb, n_tensor))
    kv = jnp.stack([tn(kraw, nb), tn(vraw, nb)]).astype(BF)
    kv = kv.reshape(2, n_dp, kv.shape[1] // n_dp, depth)
    s_down, s_gate, s_up, s_out, s_query, kv_sum, gain_sum = reduce_all(
        n_dp,
        [(down, down_got, plain), (gate, gate_got, turned), (upw, upw_got, lead), (out_w, None, plain),
         (query, None, turned)],
        kv, lead, gains, gain_in, gq_o, gq_x, gain_k)
    kv_sum = kv_sum.reshape(2, HEAD_WIDTH, depth)
    return (
        output[None], grad_input[None], gain_sum[3], s_query.T, kv_sum[0].T, kv_sum[1].T,
        gain_sum[4, :HEAD_WIDTH], gain_sum[5, :HEAD_WIDTH],
        s_out.T, gain_sum[2], gain_sum[1], s_gate.T, s_up.T, s_down.T, gain_sum[0],
    )


def solution(mesh):
    n_dp, n_tensor = mesh.shape["dp"], mesh.shape["tensor"]
    return jax.shard_map(
        functools.partial(on_device, n_dp, n_tensor),
        mesh=mesh,
        in_specs=(
            P("dp", None, None), P("dp", None, None), P("dp", None), P(), P(None, "tensor"), P(), P(), P(), P(),
            P("tensor", None), P(), P(), P(None, "tensor"), P(None, "tensor"), P("tensor", None), P(),
        ),
        out_specs=(
            P("dp", "tensor", None), P("dp", "tensor", None), P(), P(None, ("tensor", "dp")), P(), P(), P(), P(),
            P("tensor", "dp"), P(), P(), P(None, ("tensor", "dp")), P(None, ("tensor", "dp")), P("tensor", "dp"),
            P(),
        ),
        check_vma=False,
    )
```

time: 856 us -> 231 us (0.27)
  waiting for transfers between devices: 466 us -> 7.6 us
  Pallas kernels: 0 us -> 156 us
  matrix products: 148 us -> 27.3 us
  other arithmetic: 91.3 us -> 4.13 us
  local copies, waits for them, and re-layouts: 82 us -> 24.4 us
  blocking collectives: 44.1 us -> 0 us
  between operations: 17.5 us -> 1.07 us
  starting transfers between devices: 0.54 us -> 9.87 us
    unnamed x7 -> x0, waiting for transfers between devices: 244 us -> none
    psum x5 -> x0, waiting for transfers between devices: 223 us -> none  [the longest x1 128 us: on_device(): lax.psum((grad_gain_attn_in, grad_w_key, grad_w_value, grad_gain_query, g...]
    pallas_call x0 -> x6, Pallas kernels: none -> 156 us  [the longest x1 62.6 us: reduce_all(): pl.pallas_call(functools.partial(reduce_kernel, tuple(spec), tuple(kv_ord...]
    dot_general x27 -> x12, matrix products: 148 us -> 27.3 us  [tn(): lax.dot_general(a, b, (((0,), (0,)), ((), ())), preferred_element_type=F32)]
    reduce_sum x12 -> x1, other arithmetic: 46.3 us -> 1.4 us  [on_device(): jnp.sum((seg[None, :] < jnp.arange(LANES, dtype=jnp.int32)[:, None]).asty...]
    psum x1 -> x0, blocking collectives: 44.1 us -> none  [on_device(): lax.psum((grad_gain_attn_in, grad_w_key, grad_w_value, grad_gain_query, g...]
    reshape x5 -> x0, local copies, waits for them, and re-layouts: 24.3 us -> none  [the longest x1 6.84 us: on_device(): grad_w_gate = product_tn(mid_b, grad_gate).reshape(D, unit_width, -1)]
    unnamed x187 -> x69, local copies, waits for them, and re-layouts: 32.1 us -> 10.4 us
  transfers between devices with their start and end apart: 6 -> 14, of which waited for: 5 -> 2; matrix products, arithmetic and copies ran while one was open for 9% -> 16% of each run, Pallas kernels for 0% -> 9%
where the time goes in v1:
time: 231 us; the launch traced here: 230 us
  Pallas kernels  156 us (68%)
  matrix products  27.3 us (12%)
  local copies, waits for them, and re-layouts  24.4 us (11%)
  starting transfers between devices  9.87 us (4%)
  waiting for transfers between devices  7.6 us (3%)
  other arithmetic  4.13 us (2%)
    pallas_call x1, Pallas kernels, reduce_all(): pl.pallas_call(functools.partial(reduce_kernel, tuple(spec), tuple(kv_ord...  62.6 us
    pallas_call x1, Pallas kernels, block_pass(): pl.pallas_call(kern, grid_spec=pltpu.PrefetchScalarGridSpec(num_scalar_pr...  50.2 us
    dot_general x12, matrix products, tn(): lax.dot_general(a, b, (((0,), (0,)), ((), ())), preferred_element_type=F32)  27.3 us
    pallas_call x2, Pallas kernels, attn_back(): pl.pallas_call(functools.partial(attn_back_kernel, first), grid=(own // n...  23.2 us
    pallas_call x1, Pallas kernels, project(): pl.pallas_call(project_kernel, grid_spec=pltpu.PrefetchScalarGridSpec(num...  10.9 us
    unnamed x69, local copies, waits for them, and re-layouts  10.4 us
    pallas_call x1, Pallas kernels, input_back(): pl.pallas_call(kern, grid_spec=pltpu.PrefetchScalarGridSpec(num_scalar_pr...  9.17 us
    ppermute x3, waiting for transfers between devices, first_hop(): return lax.ppermute(sent, 'dp', [(i, i ^ 2 ** b) for i in range(n_dp)])  7.57 us
  transfers between devices with their start and end apart: 14, of which 2 were waited for; matrix products, arithmetic and copies ran while one was open for 16% of the time, Pallas kernels for 9%

profile of v1, /device:TPU:1, one launch (start us, length us, event | category | flops | bytes accessed | tf_op | source)
XLA Modules:
  0.0 230.4 jit_solution(16141579883092548231)
XLA Ops:
  0.6 0.1 collective-permute-start.2
  0.7 0.5 collective-permute-start.3
  1.2 0.1 collective-permute-start.4
  1.3 0.4 collective-permute-start
  1.7 0.1 collective-permute-start.1
  1.8 0.8 pad_dynamic-slice_fusion
  2.6 0.6 broadcast_in_dim.36.seg.refs_2_
  3.2 1.3 broadcast_in_dim.38.g_in.refs_12_
  4.5 1.3 broadcast_in_dim.41.refs_15_
  5.7 1.3 broadcast_in_dim.42.refs_16_
  7.0 1.3 broadcast_in_dim.43.refs_17_
  8.2 1.4 convert_reduce_fusion
  9.7 0.8 copy-done.3
  10.5 10.9 %project.1 = (bf16[1024,512]{1,0:T(8,128)(2,1)}, bf16[1024,512]{1,0:T(8,128)(2,1)}, f32[1024,512]{1,0:T(8,128)}, f32[1024,512]{1,0:T(8,128)}, bf16[1536,256]{1,0...) custom-call(s32[1]{0:T(128)} %bitcast.me, ...), custom_call_target="tpu_custom_call" | custom-call | tf_op jit(solution)/shard_map/project/pallas_call | solution.py:303
  21.5 1.1 copy-done.4
  22.5 0.4 copy-done.5
  23.0 50.2 %block.1 = (f32[1024,640]{1,0:T(8,128)}, f32[1024,640]{1,0:T(8,128)}, bf16[1024,512]{1,0:T(8,128)(2,1)}, bf16[1024,512]{1,0:T(8,128)(2,1)}, bf16[1024,512]{1,0:T...) custom-call(s32[1]{0:T(128)} %bitcast.me, ...), custom_call_target="tpu_custom_call" | custom-call | tf_op jit(solution)/shard_map/block/pallas_call | solution.py:341
  73.2 11.7 %attn_back.3 = (bf16[1024,512]{1,0:T(8,128)(2,1)}, f32[1536,256]{1,0:T(8,128)}, f32[1536,256]{1,0:T(8,128)}, f32[1,256]{1,0:T(1,128)}) custom-call(s32[1,1536]{1,0:T(1,128)} %broadcast_in_dim.36.seg.refs_2_, bf16[1024,512]{1,0:T(8,128)(2,1)} %get-tuple-element.64.refs_4_.q, bf16[1536,256]{1,0:T(8,128)(2,1)} %get-tuple-element.65.refs_5_.k, ...), custom_call_target="tpu_custom_call" | custom-call | tf_op jit(solution)/shard_map/attn_back/pallas_call | solution.py:371
  84.8 11.5 %attn_back.2 = (bf16[1024,512]{1,0:T(8,128)(2,1)}, f32[1536,256]{1,0:T(8,128)}, f32[1536,256]{1,0:T(8,128)}, f32[1,256]{1,0:T(1,128)}) custom-call(s32[1,1536]{1,0:T(1,128)} %broadcast_in_dim.36.seg.refs_2_, bf16[1024,512]{1,0:T(8,128)(2,1)} %get-tuple-element.63.refs_3_.q, bf16[1536,256]{1,0:T(8,128)(2,1)} %get-tuple-element.65.refs_5_.k, ...), custom_call_target="tpu_custom_call" | custom-call | tf_op jit(solution)/shard_map/attn_back/pallas_call | solution.py:371
  96.4 1.8 add_convert_fusion.3
  98.2 2.4 %collective-permute-start.5 = (bf16[512,512]{1,0:T(8,128)(2,1)S(1)}, bf16[512,512]{1,0:T(8,128)(2,1)S(1)}, u32[]{:S(2)}, u32[]{:S(2)}) collective-permute-start(bf16[512,512]{1,0:T(8,128)(2,1)S(1)} %pad_maximum_fusion.1), channel_id=1, source_target_pairs={{1,0},{3,2},{5,4},{7,6},{9,8},{11,10},{13,12},{15,14},{17,16},{19,... | collective-permute-start | bytes 1572872 | tf_op jit(solution)/shard_map/ppermute | solution.py:713
  100.6 1.9 convolution_convert_fusion.3
  102.5 1.7 convolution_convert_fusion.4
  104.3 0.5 collective-permute-start.12
  104.8 1.9 convolution_convert_fusion
  106.6 0.5 collective-permute-start.10
  107.1 2.9 %convolution_convert_fusion.1 = bf16[1024,640]{1,0:T(8,128)(2,1)} fusion(bf16[1024,1024]{1,0:T(8,128)(2,1)S(1)} %copy-done.20, bf16[1024,640]{1,0:T(8,128)(2,1)S(1)} %copy-done.27), kind=kOutput, calls=%fused_computation.4 | convolution fusion | flops 1342832640 | bytes 4718592 | tf_op jit(solution)/shard_map/dot_general | solution.py:35
  110.1 0.1 collective-permute-start.8
  110.2 2.6 %convolution_convert_fusion.2 = bf16[640,1024]{1,0:T(8,128)(2,1)} fusion(bf16[1024,640]{1,0:T(8,128)(2,1)S(1)} %copy-done.25, bf16[1024,1024]{1,0:T(8,128)(2,1)S(1)} %copy-done.19), kind=kOutput, calls=%fused_computation.5 | convolution fusion | flops 1342832640 | bytes 4718592 | tf_op jit(solution)/shard_map/dot_general | solution.py:35
  112.8 0.4 collective-permute-start.6
  113.2 0.8 fusion.3
  114.1 9.2 %input_back.1 = (f32[1024,640]{1,0:T(8,128)}, bf16[1024,256]{1,0:T(8,128)(2,1)}, bf16[1024,256]{1,0:T(8,128)(2,1)}, f32[1,640]{1,0:T(1,128)}, f32[1,256]{1,0:T(1,128)}) custom-call(s32[1]{0:T(128)} %bitcast.me, f32[1,2048,640]{2,1,0:T(8,128)} %refs_0_.3, f32[1024,640]{1,0:T(8,128)} %get-tuple-element.68.refs_1_, f32[1536,256]{1,0:T(8,128)} %get-tuple-element.75.refs_2_, ...), custom_call_target="tpu_custom_call" | custom-call | tf_op jit(solution)/shard_map/input_back/pallas_call | solution.py:391
  123.3 1.8 convolution_convert_fusion.6
  125.1 0.6 convolution_convert_fusion.5
  125.7 0.9 copy-done.18
  126.6 1.9 add_convert_fusion
  128.5 0.1 constant_dynamic-slice_fusion
  128.6 1.0 copy-done
  129.6 2.4 %collective-permute-start.11 = (bf16[8,64,640]{2,1,0:T(8,128)(2,1)S(1)}, bf16[8,64,640]{2,1,0:T(8,128)(2,1)S(1)}, u32[]{:S(2)}, u32[]{:S(2)}) collective-permute-start(bf16[8,64,640]{2,1,0:T(8,128)(2,1)S(1)} %bitcast.83), channel_id=1, source_target_pairs={{0,8},{2,10},{4,12},{6,14},{8,0},{10,2},{12,4},{14,6},{16,24},{18,... | collective-permute-start | bytes 1966088 | tf_op jit(solution)/shard_map/ppermute | solution.py:666
  132.0 3.3 %add_convert_fusion.1 = bf16[1024,640]{1,0:T(8,128)(2,1)S(1)} fusion(bf16[1024,640]{1,0:T(8,128)(2,1)} %collective-permute-done.8, bf16[1024,1024]{1,0:T(8,128)(2,1)S(1)} %copy-done.17, bf16[1024,640]{1,0:T(8,128)(2,1)S(1)} %copy-done.28), kind=kOutput, calls=%fused_computation.1 | convolution fusion | flops 1344143360 | bytes 6029312 | tf_op jit(solution)/shard_map/dot_general | solution.py:35
  135.3 0.1 constant_dynamic-slice_fusion.1
  135.5 0.9 copy-done.1
  136.4 1.3 collective-permute-start.9
  137.7 2.9 %add_convert_fusion.2 = bf16[640,1024]{1,0:T(8,128)(2,1)S(1)} fusion(bf16[640,1024]{1,0:T(8,128)(2,1)} %collective-permute-done.6, bf16[1024,640]{1,0:T(8,128)(2,1)S(1)} %copy-done.26, bf16[1024,1024]{1,0:T(8,128)(2,1)S(1)} %copy-done.16), kind=kOutput, calls=%fused_computation.2 | convolution fusion | flops 1344143360 | bytes 6029312 | tf_op jit(solution)/shard_map/dot_general | solution.py:35
  140.5 0.1 constant_dynamic-slice_fusion.2
  140.7 1.0 copy-done.2
  141.6 1.2 collective-permute-start.7
  142.9 0.9 pad_maximum_fusion.refs_8_
  143.8 3.1 %fusion.1 = bf16[512,640]{1,0:T(8,128)(2,1)} fusion(bf16[1024,512]{1,0:T(8,128)(2,1)S(1)} %copy-done.6, bf16[1024,640]{1,0:T(8,128)(2,1)S(1)} %copy-done.22, bf16[512,640]{1,0:T(8,128)(2,1)} %collective-permute-done.13), kind=kOutput, calls=%fused_computation.9 | convolution fusion | flops 672071680 | bytes 3670016 | tf_op jit(solution)/shard_map/dot_general | solution.py:35
  146.9 2.8 %fusion = bf16[640,512]{1,0:T(8,128)(2,1)} fusion(bf16[1024,640]{1,0:T(8,128)(2,1)S(1)} %copy-done.24, bf16[1024,512]{1,0:T(8,128)(2,1)S(1)} %copy-done.29, bf16[640,512]{1,0:T(8,128)(2,1)} %collective-permute-done.12), kind=kOutput, calls=%fused_computation.8 | convolution fusion | flops 672071680 | bytes 3670016 | tf_op jit(solution)/shard_map/dot_general | solution.py:35
  149.7 2.6 %collective-permute-done.9.refs_3_ = bf16[8,64,640]{2,1,0:T(8,128)(2,1)S(1)} collective-permute-done((bf16[8,64,640]{2,1,0:T(8,128)(2,1)S(1)}, bf16[8,64,640]{2,1,0:T(8,128)(2,1)S(1)}, u32[]{:S(2)}, u32[]{:S(2)}) %collective-permute-start.9) | collective-permute-done | bytes 655392 | tf_op jit(solution)/shard_map/ppermute | solution.py:666
  152.3 5.0 %collective-permute-done.7.refs_1_ = bf16[8,40,1024]{2,1,0:T(8,128)(2,1)S(1)} collective-permute-done((bf16[8,40,1024]{2,1,0:T(8,128)(2,1)S(1)}, bf16[8,40,1024]{2,1,0:T(8,128)(2,1)S(1)}, u32[]{:S(2)}, u32[]{:S(2)}) %collective-permute-start.7) | collective-permute-done | bytes 655392 | tf_op jit(solution)/shard_map/ppermute | solution.py:666
  157.3 0.8 copy-done.10
  158.1 62.6 %reduce_all.1 = (f32[40,1024]{1,0:T(8,128)}, f32[64,640]{1,0:T(8,128)}, f32[64,640]{1,0:T(8,128)}, f32[40,512]{1,0:T(8,128)}, f32[32,640]{1,0:T(8,128)}, /*index=5*/f32[2,16,16,640]{3,2,1,0:T(8,128)}, f32[8,640]{1,0:T(8,128)}) custom-call(bf16[16,40,1024]{2,1,0:T(8,128)(2,1)} %bitcast.75, bf16[8,40,1024]{2,1,0:T(8,128)(2,1)} %copy-done.10, ...), custom_call_target="tpu_custom_call" | custom-call | tf_op jit(solution)/shard_map/reduce_all/pallas_call | solution.py:642
  220.7 1.5 slice_reduce_fusion
  222.2 1.3 fusion.4
  223.6 1.4 fusion.2
  225.0 1.1 copy.48
  226.1 1.1 copy.49
  227.1 0.6 copy.58
  227.8 0.6 copy.59
  228.4 0.7 copy.60
  229.1 0.7 copy.61
  229.8 0.7 copy.62
  (73 shorter events, 0.3 us)
Async XLA Ops:
  0.6 20.8 %collective-permute-start.2 = (bf16[640,1024]{1,0:T(8,128)(2,1)}, bf16[640,1024]{1,0:T(8,128)(2,1)S(1)}, u32[]{:S(2)}, u32[]{:S(2)}) collective-permute-start(bf16[640,1024]{1,0:T(8,128)(2,1)} %refs_9_.1), channel_id=1, source_target_pairs={{0,1},{1,0},{2,3},{3,2},{4,5},{5,4},{6,7},{7,6},{8,9},{9,8},{10,11... | collective-permute-start | bytes 3932168 | tf_op jit(solution)/shard_map/ppermute | solution.py:414
  0.7 20.7 %collective-permute-start.3 = (bf16[640,1024]{1,0:T(8,128)(2,1)}, bf16[640,1024]{1,0:T(8,128)(2,1)S(1)}, u32[]{:S(2)}, u32[]{:S(2)}) collective-permute-start(bf16[640,1024]{1,0:T(8,128)(2,1)} %refs_11_.1), channel_id=1, source_target_pairs={{0,1},{1,0},{2,3},{3,2},{4,5},{5,4},{6,7},{7,6},{8,9},{9,8},{10,11... | collective-permute-start | bytes 3932168 | tf_op jit(solution)/shard_map/ppermute | solution.py:414
  1.2 20.2 %collective-permute-start.4 = (bf16[1024,640]{1,0:T(8,128)(2,1)}, bf16[1024,640]{1,0:T(8,128)(2,1)}, u32[]{:S(2)}, u32[]{:S(2)}) collective-permute-start(bf16[1024,640]{1,0:T(8,128)(2,1)} %refs_13_.1), channel_id=1, source_target_pairs={{0,1},{1,0},{2,3},{3,2},{4,5},{5,4},{6,7},{7,6},{8,9},{9,8},{10,11... | collective-permute-start | bytes 3932168 | tf_op jit(solution)/shard_map/ppermute | solution.py:414
  1.3 8.3 %collective-permute-start = (bf16[640,512]{1,0:T(8,128)(2,1)}, bf16[640,512]{1,0:T(8,128)(2,1)S(1)}, u32[]{:S(2)}, u32[]{:S(2)}) collective-permute-start(bf16[640,512]{1,0:T(8,128)(2,1)} %refs_15_.1), channel_id=1, source_target_pairs={{0,1},{1,0},{2,3},{3,2},{4,5},{5,4},{6,7},{7,6},{8,9},{9,8},{10,11... | collective-permute-start | bytes 1966088 | tf_op jit(solution)/shard_map/ppermute | solution.py:414
  1.7 19.7 %collective-permute-start.1 = (bf16[512,640]{1,0:T(8,128)(2,1)}, bf16[512,640]{1,0:T(8,128)(2,1)}, u32[]{:S(2)}, u32[]{:S(2)}) collective-permute-start(bf16[512,640]{1,0:T(8,128)(2,1)} %refs_7_.1), channel_id=1, source_target_pairs={{0,1},{1,0},{2,3},{3,2},{4,5},{5,4},{6,7},{7,6},{8,9},{9,8},{10,11... | collective-permute-start | bytes 1966088 | tf_op jit(solution)/shard_map/ppermute | solution.py:414
  9.6 0.8 copy-start.3
  21.4 1.1 copy-start.4
  21.5 1.5 copy-start.5
  96.4 4.2 %copy-start.7 = (bf16[1024,512]{1,0:T(8,128)(2,1)S(1)}, bf16[1024,512]{1,0:T(8,128)(2,1)}, u32[]{:S(2)}) copy-start(bf16[1024,512]{1,0:T(8,128)(2,1)} %get-tuple-element.83.refs_14_) | copy-start | bytes 3145732
  96.4 4.2 %copy-start.22 = (bf16[1024,640]{1,0:T(8,128)(2,1)S(1)}, bf16[1024,640]{1,0:T(8,128)(2,1)}, u32[]{:S(2)}) copy-start(bf16[1024,640]{1,0:T(8,128)(2,1)} %get-tuple-element.96) | copy-start | bytes 3932164
  98.2 14.6 %collective-permute-start.5 = (bf16[512,512]{1,0:T(8,128)(2,1)S(1)}, bf16[512,512]{1,0:T(8,128)(2,1)S(1)}, u32[]{:S(2)}, u32[]{:S(2)}) collective-permute-start(bf16[512,512]{1,0:T(8,128)(2,1)S(1)} %pad_maximum_fusion.1), channel_id=1, source_target_pairs={{1,0},{3,2},{5,4},{7,6},{9,8},{11,10},{13,12},{15,14},{17,16},{19,... | collective-permute-start | bytes 1572872 | tf_op jit(solution)/shard_map/ppermute | solution.py:713
  100.6 1.9 copy-start.23
  100.6 1.9 copy-start.30
  102.5 41.3 %collective-permute-start.13 = (bf16[512,640]{1,0:T(8,128)(2,1)}, bf16[512,640]{1,0:T(8,128)(2,1)}, u32[]{:S(2)}, u32[]{:S(2)}) collective-permute-start(bf16[512,640]{1,0:T(8,128)(2,1)} %convolution_convert_fusion.3), channel_id=1, source_target_pairs={{0,1},{1,0},{2,3},{3,2},{4,5},{5,4},{6,7},{7,6},{8,9},{9,8},{10,11... | collective-permute-start | bytes 1966088 | tf_op jit(solution)/shard_map/ppermute | solution.py:414
  102.5 2.2 copy-start.21
  102.5 2.2 copy-start.27
  104.3 42.7 %collective-permute-start.12 = (bf16[640,512]{1,0:T(8,128)(2,1)}, bf16[640,512]{1,0:T(8,128)(2,1)}, u32[]{:S(2)}, u32[]{:S(2)}) collective-permute-start(bf16[640,512]{1,0:T(8,128)(2,1)} %convolution_convert_fusion.4), channel_id=1, source_target_pairs={{0,1},{1,0},{2,3},{3,2},{4,5},{5,4},{6,7},{7,6},{8,9},{9,8},{10,11... | collective-permute-start | bytes 1966088 | tf_op jit(solution)/shard_map/ppermute | solution.py:414
  104.8 2.4 %copy-start.20 = (bf16[1024,1024]{1,0:T(8,128)(2,1)S(1)}, bf16[1024,1024]{1,0:T(8,128)(2,1)}, u32[]{:S(2)}) copy-start(bf16[1024,1024]{1,0:T(8,128)(2,1)} %get-tuple-element.90) | copy-start | bytes 6291460
  106.6 19.0 %collective-permute-start.10 = (bf16[1024,640]{1,0:T(8,128)(2,1)S(1)}, bf16[1024,640]{1,0:T(8,128)(2,1)S(1)}, u32[]{:S(2)}, u32[]{:S(2)}) collective-permute-start(bf16[1024,640]{1,0:T(8,128)(2,1)S(1)} %convolution_convert_fusion), channel_id=1, source_target_pairs={{0,1},{1,0},{2,3},{3,2},{4,5},{5,4},{6,7},{7,6},{8,9},{9,8},{10,11... | collective-permute-start | bytes 3932168 | tf_op jit(solution)/shard_map/ppermute | solution.py:414
  107.1 3.0 %copy-start.19 = (bf16[1024,1024]{1,0:T(8,128)(2,1)S(1)}, bf16[1024,1024]{1,0:T(8,128)(2,1)}, u32[]{:S(2)}) copy-start(bf16[1024,1024]{1,0:T(8,128)(2,1)} %get-tuple-element.87) | copy-start | bytes 6291460
  107.1 3.0 %copy-start.25 = (bf16[1024,640]{1,0:T(8,128)(2,1)S(1)}, bf16[1024,640]{1,0:T(8,128)(2,1)}, u32[]{:S(2)}) copy-start(bf16[1024,640]{1,0:T(8,128)(2,1)} %get-tuple-element.85) | copy-start | bytes 3932164
  110.1 21.9 %collective-permute-start.8 = (bf16[1024,640]{1,0:T(8,128)(2,1)}, bf16[1024,640]{1,0:T(8,128)(2,1)}, u32[]{:S(2)}, u32[]{:S(2)}) collective-permute-start(bf16[1024,640]{1,0:T(8,128)(2,1)} %convolution_convert_fusion.1), channel_id=1, source_target_pairs={{0,1},{1,0},{2,3},{3,2},{4,5},{5,4},{6,7},{7,6},{8,9},{9,8},{10,11... | collective-permute-start | bytes 3932168 | tf_op jit(solution)/shard_map/ppermute | solution.py:414
  112.8 24.9 %collective-permute-start.6 = (bf16[640,1024]{1,0:T(8,128)(2,1)}, bf16[640,1024]{1,0:T(8,128)(2,1)}, u32[]{:S(2)}, u32[]{:S(2)}) collective-permute-start(bf16[640,1024]{1,0:T(8,128)(2,1)} %convolution_convert_fusion.2), channel_id=1, source_target_pairs={{0,1},{1,0},{2,3},{3,2},{4,5},{5,4},{6,7},{7,6},{8,9},{9,8},{10,11... | collective-permute-start | bytes 3932168 | tf_op jit(solution)/shard_map/ppermute | solution.py:414
  123.2 1.8 copy-start.31
  123.2 2.4 %copy-start.28 = (bf16[1024,640]{1,0:T(8,128)(2,1)S(1)}, bf16[1024,640]{1,0:T(8,128)(2,1)}, u32[]{:S(2)}) copy-start(bf16[1024,640]{1,0:T(8,128)(2,1)} %get-tuple-element.89) | copy-start | bytes 3932164
  125.0 1.6 copy-start.18
  128.5 1.2 copy-start
  128.5 3.5 %copy-start.17 = (bf16[1024,1024]{1,0:T(8,128)(2,1)S(1)}, bf16[1024,1024]{1,0:T(8,128)(2,1)}, u32[]{:S(2)}) copy-start(bf16[1024,1024]{1,0:T(8,128)(2,1)} %get-tuple-element.88) | copy-start | bytes 6291460
  129.6 20.1 %collective-permute-start.11 = (bf16[8,64,640]{2,1,0:T(8,128)(2,1)S(1)}, bf16[8,64,640]{2,1,0:T(8,128)(2,1)S(1)}, u32[]{:S(2)}, u32[]{:S(2)}) collective-permute-start(bf16[8,64,640]{2,1,0:T(8,128)(2,1)S(1)} %bitcast.83), channel_id=1, source_target_pairs={{0,8},{2,10},{4,12},{6,14},{8,0},{10,2},{12,4},{14,6},{16,24},{18,... | collective-permute-start | bytes 1966088 | tf_op jit(solution)/shard_map/ppermute | solution.py:666
  132.0 5.6 %copy-start.26 = (bf16[1024,640]{1,0:T(8,128)(2,1)S(1)}, bf16[1024,640]{1,0:T(8,128)(2,1)}, u32[]{:S(2)}) copy-start(bf16[1024,640]{1,0:T(8,128)(2,1)} %get-tuple-element.85) | copy-start | bytes 3932164
  135.3 1.1 copy-start.1
  135.3 2.4 %copy-start.16 = (bf16[1024,1024]{1,0:T(8,128)(2,1)S(1)}, bf16[1024,1024]{1,0:T(8,128)(2,1)}, u32[]{:S(2)}) copy-start(bf16[1024,1024]{1,0:T(8,128)(2,1)} %get-tuple-element.86) | copy-start | bytes 6291460
  136.4 15.9 %collective-permute-start.9 = (bf16[8,64,640]{2,1,0:T(8,128)(2,1)S(1)}, bf16[8,64,640]{2,1,0:T(8,128)(2,1)S(1)}, u32[]{:S(2)}, u32[]{:S(2)}) collective-permute-start(bf16[8,64,640]{2,1,0:T(8,128)(2,1)S(1)} %bitcast.84), channel_id=1, source_target_pairs={{0,4},{2,6},{4,0},{6,2},{8,12},{10,14},{12,8},{14,10},{16,20},{18,... | collective-permute-start | bytes 1966088 | tf_op jit(solution)/shard_map/ppermute | solution.py:666
  140.5 1.1 copy-start.2
  140.6 3.2 %copy-start.6 = (bf16[1024,512]{1,0:T(8,128)(2,1)S(1)}, bf16[1024,512]{1,0:T(8,128)(2,1)}, u32[]{:S(2)}) copy-start(bf16[1024,512]{1,0:T(8,128)(2,1)} %get-tuple-element.82.refs_13_) | copy-start | bytes 3145732
  141.6 15.7 %collective-permute-start.7 = (bf16[8,40,1024]{2,1,0:T(8,128)(2,1)S(1)}, bf16[8,40,1024]{2,1,0:T(8,128)(2,1)S(1)}, u32[]{:S(2)}, u32[]{:S(2)}) collective-permute-start(bf16[8,40,1024]{2,1,0:T(8,128)(2,1)S(1)} %bitcast.87), channel_id=1, source_target_pairs={{0,2},{2,0},{4,6},{6,4},{8,10},{10,8},{12,14},{14,12},{16,18},{18,... | collective-permute-start | bytes 1966088 | tf_op jit(solution)/shard_map/ppermute | solution.py:666
  143.8 3.1 %copy-start.24 = (bf16[1024,640]{1,0:T(8,128)(2,1)S(1)}, bf16[1024,640]{1,0:T(8,128)(2,1)}, u32[]{:S(2)}) copy-start(bf16[1024,640]{1,0:T(8,128)(2,1)} %get-tuple-element.93) | copy-start | bytes 3932164
  143.8 3.1 %copy-start.29 = (bf16[1024,512]{1,0:T(8,128)(2,1)S(1)}, bf16[1024,512]{1,0:T(8,128)(2,1)}, u32[]{:S(2)}) copy-start(bf16[1024,512]{1,0:T(8,128)(2,1)} %get-tuple-element.94) | copy-start | bytes 3145732
  149.7 7.6 %copy-start.8 = (bf16[8,64,640]{2,1,0:T(8,128)(2,1)}, bf16[8,64,640]{2,1,0:T(8,128)(2,1)S(1)}, u32[]{:S(2)}) copy-start(bf16[8,64,640]{2,1,0:T(8,128)(2,1)S(1)} %collective-permute-done.11.refs_5_) | copy-start | bytes 1966084
  152.3 5.0 %copy-start.9 = (bf16[8,64,640]{2,1,0:T(8,128)(2,1)}, bf16[8,64,640]{2,1,0:T(8,128)(2,1)S(1)}, u32[]{:S(2)}) copy-start(bf16[8,64,640]{2,1,0:T(8,128)(2,1)S(1)} %collective-permute-done.9.refs_3_) | copy-start | bytes 1966084
  157.3 0.8 copy-start.10
  225.0 2.2 copy-start.15
  225.0 2.8 %copy-start.14 = (f32[40,512]{1,0:T(8,128)S(1)}, f32[40,512]{1,0:T(8,128)}, u32[]{:S(2)}) copy-start(f32[40,512]{1,0:T(8,128)} %get-tuple-element.107) | copy-start | bytes 245764
  225.0 3.4 %copy-start.13 = (f32[64,640]{1,0:T(8,128)S(1)}, f32[64,640]{1,0:T(8,128)}, u32[]{:S(2)}) copy-start(f32[64,640]{1,0:T(8,128)} %get-tuple-element.108) | copy-start | bytes 491524
  226.1 3.0 %copy-start.12 = (f32[64,640]{1,0:T(8,128)S(1)}, f32[64,640]{1,0:T(8,128)}, u32[]{:S(2)}) copy-start(f32[64,640]{1,0:T(8,128)} %get-tuple-element.109) | copy-start | bytes 491524
  226.1 3.7 %copy-start.11 = (f32[40,1024]{1,0:T(8,128)S(1)}, f32[40,1024]{1,0:T(8,128)}, u32[]{:S(2)}) copy-start(f32[40,1024]{1,0:T(8,128)} %get-tuple-element.110) | copy-start | bytes 491524

commit v2 on v1

--- a/solution.py
+++ b/solution.py
@@ -70,8 +70,9 @@
     return np.concatenate(parts, axis=1)
 
 
-def project_kernel(me, x, seg, starts, table, g_in, wq_o, wq_x, wk, wv, gq, gk,
+def project_kernel(me, x, seg, starts, table, rows8, wq_o, wq_x, wk, wv,
                    q_o, q_x, ql_o, ql_x, k_out, v_out, kl_out, nb_out, cos_out, sin_out):
+    g_in, gq, gk = gain_refs(rows8, 0, 4, 5)
     i = pl.program_id(0)
     rows = x.shape[1]
     hat, _ = rms_stats(x[0])
@@ -102,7 +103,12 @@
             for h in range(lin.shape[1] // HEAD_WIDTH):
                 cols = slice(h * HEAD_WIDTH, (h + 1) * HEAD_WIDTH)
                 q_hat, _ = rms_stats(lin[:, cols])
-                out[:, cols] = rotate(q_hat * gq[...], cos, sin, 1).astype(BF)
+                out[:, cols] = (rotate(q_hat * gq[...], cos, sin, 1) * SCORE_SCALE).astype(BF)
+
+
+def gain_refs(rows8, *which):
+    width = rows8.shape[1]
+    return [rows8.at[r : r + 1, : (width if r < 4 else HEAD_WIDTH)] for r in which]
 
 
 def score_mask(seg_q, seg_k, rows, width):
@@ -112,10 +118,11 @@
 
 
 def block_kernel(x, up, seg, q_o, q_x, k, v, wo_o, wo_x, wg_o, wg_x, wu_o, wu_x, wd_o, wd_x,
-                 g_ao, g_fi, g_fo,
+                 rows8,
                  out, gmid_out, ga_o, ga_x, af_o, af_x, lse_out, delta_out, mid_out, gff_out, gas_out,
                  act_o, act_x, gg_o, gg_x, gu_o, gu_x, gains,
                  mix, gate_s, up_s):
+    g_ao, g_fi, g_fo = gain_refs(rows8, 1, 2, 3)
     i = pl.program_id(0)
     rows = x.shape[1]
     base = pl.multiple_of(i * rows, rows)
@@ -129,11 +136,12 @@
     for part, (q, af) in enumerate(((q_o, af_o), (q_x, af_x))):
         for h in range(heads_per):
             cols = slice(h * HEAD_WIDTH, (h + 1) * HEAD_WIDTH)
-            s = jnp.where(mask, nt(q[:, cols], k_win) * SCORE_SCALE, -jnp.inf)
+            s = jnp.where(mask, nt(q[:, cols], k_win), -jnp.inf)
             top = jnp.max(s, axis=-1, keepdims=True)
-            lse = top + jnp.log(jnp.sum(jnp.exp(s - top), axis=-1, keepdims=True))
-            lses.append(lse)
-            p = jnp.exp(s - lse).astype(BF)
+            e = jnp.exp(s - top)
+            mass = jnp.sum(e, axis=-1, keepdims=True)
+            lses.append(top + jnp.log(mass))
+            p = (e * (1.0 / mass)).astype(BF)
             m = nn(p, v_win)
             mix[part * heads_per + h] = m
             af[:, cols] = m.astype(BF)
@@ -149,10 +157,14 @@
     for part, (wg, wu, wd, act) in enumerate(((wg_o, wu_o, wd_o, act_o), (wg_x, wu_x, wd_x, act_x))):
         gate = nn(mid_b, wg[...])
         upp = nn(mid_b, wu[...])
-        gate_s[part] = gate
-        up_s[part] = upp
-        th = jnp.tanh(GELU_C * (gate + GELU_A * gate * gate * gate))
-        a = (0.5 * gate * (1.0 + th) * upp).astype(BF)
+        sq = gate * gate
+        th = jnp.tanh(gate * (GELU_C + (GELU_C * GELU_A) * sq))
+        onep = 0.5 + 0.5 * th
+        gelu = gate * onep
+        deriv = onep + gate * (1.0 - th * th) * (0.5 * GELU_C + (1.5 * GELU_C * GELU_A) * sq)
+        gate_s[part] = gelu
+        up_s[part] = upp * deriv
+        a = (gelu * upp).astype(BF)
         act[...] = a
         f = nn(a, wd[...])
         ff_sum = f if ff_sum is None else ff_sum + f
@@ -165,14 +177,8 @@
         ((wg_o, wu_o, wd_o, gg_o, gu_o), (wg_x, wu_x, wd_x, gg_x, gu_x))
     ):
         gact = nt(gff, wd[...])
-        gate = gate_s[part]
-        upp = up_s[part]
-        sq = gate * gate
-        th = jnp.tanh(GELU_C * (gate + GELU_A * gate * sq))
-        onep = 0.5 * (1.0 + th)
-        deriv = onep + 0.5 * gate * (1.0 - th * th) * (GELU_C * (1.0 + 3.0 * GELU_A * sq))
-        gg = (gact * upp * deriv).astype(BF)
-        gu = (gact * (gate * onep)).astype(BF)
+        gg = (gact * up_s[part]).astype(BF)
+        gu = (gact * gate_s[part]).astype(BF)
         gg_out[...] = gg
         gu_out[...] = gu
         t = nt(gg, wg[...]) + nt(gu, wu[...])
@@ -194,8 +200,8 @@
     for n, (a, b) in enumerate(zip(lses, deltas)):
         lse_all = jnp.where(lane == n, a, lse_all)
         delta_all = jnp.where(lane == n, b, delta_all)
-    lse_out[...] = lse_all
-    delta_out[...] = delta_all
+    lse_out[...] = jnp.transpose(lse_all)[:8]
+    delta_out[...] = jnp.transpose(delta_all)[:8]
 
     @pl.when(i == 0)
     def _():
@@ -206,7 +212,8 @@
     gains[2:3, :] += jnp.sum(gmid * hat_attn, axis=0, keepdims=True)
 
 
-def attn_back_kernel(first, seg, q, k, v, ga, lse, delta, ql, cos, sin, gq, qraw, dk, dv, gain):
+def attn_back_kernel(first, seg, q, k, v, ga, lse, delta, ql, cos, sin, rows8, qraw, dk, dv, gain):
+    (gq,) = gain_refs(rows8, 4)
     i = pl.program_id(0)
     rows = q.shape[0]
     base = pl.multiple_of(i * rows, rows)
@@ -219,24 +226,25 @@
 
     k_win = k[pl.ds(base, WIN), :]
     v_win = v[pl.ds(base, WIN), :]
-    seg_k = seg[:, pl.ds(base, WIN)]
-    seg_q = column_of(seg[:, pl.ds(base + BLOCK, rows)])[:, :1]
-    mask = score_mask(seg_q, seg_k, rows, WIN)
+    seg_k = column_of(seg[:, pl.ds(base, WIN)])[:, :1]
+    seg_q = seg[:, pl.ds(base + BLOCK, rows)]
+    lane = lax.broadcasted_iota(jnp.int32, (WIN, rows), 1)
+    sub = lax.broadcasted_iota(jnp.int32, (WIN, rows), 0)
+    mask = (seg_q == seg_k) & (sub <= lane + (WIN - rows))
     dk_sum = None
     dv_sum = None
     g_sum = None
     for h in range(q.shape[1] // HEAD_WIDTH):
         cols = slice(h * HEAD_WIDTH, (h + 1) * HEAD_WIDTH)
+        at = slice(first + h, first + h + 1)
         qh = q[:, cols]
         gh = ga[:, cols]
-        s = jnp.where(mask, nt(qh, k_win) * SCORE_SCALE, -jnp.inf)
-        p = jnp.exp(s - lse[:, first + h : first + h + 1])
-        dp = nt(gh, v_win)
-        ds = (p * (dp - delta[:, first + h : first + h + 1]) * SCORE_SCALE).astype(BF)
-        pb = p.astype(BF)
-        dq = nn(ds, k_win)
-        a = tn(ds, qh)
-        b = tn(pb, gh)
+        s = jnp.where(mask, nt(k_win, qh), -jnp.inf)
+        p = jnp.exp(s - lse[at, :])
+        ds = (p * (nt(v_win, gh) - delta[at, :])).astype(BF)
+        dq = tn(ds, k_win) * SCORE_SCALE
+        a = nn(ds, qh)
+        b = nn(p.astype(BF), gh)
         dk_sum = a if dk_sum is None else dk_sum + a
         dv_sum = b if dv_sum is None else dv_sum + b
         dqn = rotate(dq, cos[...], sin[...], -1)
@@ -249,8 +257,9 @@
     gain[...] += g_sum
 
 
-def input_back_kernel(x, gmid, dk_o, dk_x, dv_o, dv_x, dk_r, dv_r, kl, cos, sin, gk, g_in,
-                      qr_o, qr_x, wq_o, wq_x, wk, wv, gin_out, kraw_out, vraw_out, gains, gain_k):
+def input_back_kernel(x, gmid, dk_o, dk_x, dv_o, dv_x, dk_r, dv_r, kl, cos, sin, rows8,
+                      qr_o, qr_x, wq_o, wq_x, wk, wv, nb, gin_out, kv_out, gains, gain_k, kv_acc):
+    g_in, gk = gain_refs(rows8, 0, 5)
     i = pl.program_id(0)
     last = pl.num_programs(0) - 1
     tail = (i == last).astype(F32)
@@ -260,8 +269,14 @@
     k_hat, k_inv = rms_stats(kl[...])
     kraw = rms_back(k_hat, k_inv, gk[...], dkn).astype(BF)
     vraw = dv.astype(BF)
-    kraw_out[...] = kraw
-    vraw_out[...] = vraw
+    kv_w = tn(jnp.concatenate([kraw, vraw], axis=1), nb[...])
+
+    @pl.when(i == 0)
+    def _():
+        kv_acc[...] = jnp.zeros_like(kv_acc)
+
+    kv_acc[...] += kv_w
+    kv_out[...] = kv_acc[...].astype(BF)
     gn = nt(kraw, wk[...]) + nt(vraw, wv[...]) + nt(qr_o[...], wq_o[...]) + nt(qr_x[...], wq_x[...])
     hat, inv = rms_stats(x[0])
     gin_out[...] = gmid[...] + rms_back(hat, inv, g_in[...], gn)
@@ -289,11 +304,15 @@
     return pltpu.CompilerParams(dimension_semantics=("arbitrary",), vmem_limit_bytes=VMEM_LIMIT)
 
 
+def cost(us):
+    return pl.CostEstimate(flops=us * 10**9, bytes_accessed=us * 10**6, transcendentals=0)
+
+
 def sds(shape, dtype):
     return jax.ShapeDtypeStruct(shape, dtype)
 
 
-def project(first_row, x3, seg_ext, starts, table, g_in, wq_o, wq_x, wk, wv, gq, gk):
+def project(first_row, x3, seg_ext, starts, table, rows8, wq_o, wq_x, wk, wv):
     depth = x3.shape[2]
     ext = seg_ext.shape[1]
     own = ext - BLOCK
@@ -310,9 +329,8 @@
                 pl.BlockSpec((1, n), lambda i, *_: (0, i)),
                 whole((1, LANES)),
                 whole(table.shape),
-                whole((1, depth)),
+                whole(rows8.shape),
                 whole(wq_o.shape), whole(wq_x.shape), whole(wk.shape), whole(wv.shape),
-                whole((1, HEAD_WIDTH)), whole((1, HEAD_WIDTH)),
             ],
             out_specs=[
                 rows_of(n, part, 1), rows_of(n, part, 1), rows_of(n, part, 1), rows_of(n, part, 1),
@@ -326,11 +344,12 @@
             sds((own, depth), BF), sds((own, LANES), F32), sds((own, LANES), F32),
         ],
         compiler_params=params(),
+        cost_estimate=cost(6),
         name="project",
-    )(first_row, x3, seg_ext, starts, table, g_in, wq_o, wq_x, wk, wv, gq, gk)
-
-
-def block_pass(first_row, x3, up3, seg_ext, q_o, q_x, k, v, weights, g_ao, g_fi, g_fo):
+    )(first_row, x3, seg_ext, starts, table, rows8, wq_o, wq_x, wk, wv)
+
+
+def block_pass(first_row, x3, up3, seg_ext, q_o, q_x, k, v, weights, rows8):
     depth = x3.shape[2]
     own, part = q_o.shape
     n = QB
@@ -346,8 +365,8 @@
             in_specs=[mine, mine, whole(seg_ext.shape), rows_of(n, part), rows_of(n, part),
                       whole(k.shape), whole(v.shape)]
             + [whole(w.shape) for w in weights]
-            + [whole((1, depth))] * 3,
-            out_specs=[rows_of(n, depth)] * 2 + [rows_of(n, part)] * 4 + [rows_of(n, LANES)] * 2
+            + [whole(rows8.shape)],
+            out_specs=[rows_of(n, depth)] * 2 + [rows_of(n, part)] * 4 + [pl.BlockSpec((8, n), lambda i, *_: (0, i))] * 2
             + [rows_of(n, depth)] * 3 + [rows_of(n, hidden)] * 6
             + [pl.BlockSpec((8, depth), lambda i, *_: (0, 0))],
             scratch_shapes=[
@@ -356,14 +375,15 @@
                 pltpu.VMEM((2, n, hidden), F32),
             ],
         ),
-        out_shape=[sds((own, depth), F32)] * 2 + [sds((own, part), BF)] * 4 + [sds((own, LANES), F32)] * 2
+        out_shape=[sds((own, depth), F32)] * 2 + [sds((own, part), BF)] * 4 + [sds((8, own), F32)] * 2
         + [sds((own, depth), BF)] * 3 + [sds((own, hidden), BF)] * 6 + [sds((8, depth), F32)],
         compiler_params=params(),
+        cost_estimate=cost(40),
         name="block",
-    )(first_row, x3, up3, seg_ext, q_o, q_x, k, v, *weights, g_ao, g_fi, g_fo)
-
-
-def attn_back(first, seg_ext, q, k, v, ga, lse, delta, ql, cos, sin, gq):
+    )(first_row, x3, up3, seg_ext, q_o, q_x, k, v, *weights, rows8)
+
+
+def attn_back(first, seg_ext, q, k, v, ga, lse, delta, ql, cos, sin, rows8):
     own, part = q.shape
     n = QB
     ext = k.shape[0]
@@ -372,17 +392,19 @@
         functools.partial(attn_back_kernel, first),
         grid=(own // n,),
         in_specs=[whole(seg_ext.shape), rows_of(n, part), whole(k.shape), whole(v.shape), rows_of(n, part),
-                  rows_of(n, LANES), rows_of(n, LANES), rows_of(n, part), rows_of(n, LANES), rows_of(n, LANES),
-                  whole((1, HEAD_WIDTH))],
+                  pl.BlockSpec((8, n), lambda i: (0, i)), pl.BlockSpec((8, n), lambda i: (0, i)), rows_of(n, part),
+                  rows_of(n, LANES), rows_of(n, LANES),
+                  whole(rows8.shape)],
         out_specs=[rows_of(n, part), acc, acc, pl.BlockSpec((1, HEAD_WIDTH), lambda i: (0, 0))],
         out_shape=[sds((own, part), BF), sds((ext, HEAD_WIDTH), F32), sds((ext, HEAD_WIDTH), F32),
                    sds((1, HEAD_WIDTH), F32)],
         compiler_params=params(),
+        cost_estimate=cost(10),
         name="attn_back",
-    )(seg_ext, q, k, v, ga, lse, delta, ql, cos, sin, gq)
-
-
-def input_back(first_row, x3, gmid, dks, dvs, dk_r, dv_r, kl, cos, sin, gk, g_in, qr_o, qr_x, wq_o, wq_x, wk, wv):
+    )(seg_ext, q, k, v, ga, lse, delta, ql, cos, sin, rows8)
+
+
+def input_back(first_row, x3, gmid, dks, dvs, dk_r, dv_r, kl, cos, sin, rows8, qr_o, qr_x, wq_o, wq_x, wk, wv, nb):
     depth = x3.shape[2]
     own, part = qr_o.shape
     n = BLOCK
@@ -396,28 +418,24 @@
             in_specs=[pl.BlockSpec((1, n, depth), lambda i, me: (0, me[0] // n + i, 0)), rows_of(n, depth),
                       later, later, later, later, whole((n, HEAD_WIDTH)), whole((n, HEAD_WIDTH)),
                       rows_of(n, HEAD_WIDTH), rows_of(n, LANES), rows_of(n, LANES),
-                      whole((1, HEAD_WIDTH)), whole((1, depth)), rows_of(n, part), rows_of(n, part),
-                      whole(wq_o.shape), whole(wq_x.shape), whole(wk.shape), whole(wv.shape)],
-            out_specs=[rows_of(n, depth), rows_of(n, HEAD_WIDTH), rows_of(n, HEAD_WIDTH),
+                      whole(rows8.shape), rows_of(n, part), rows_of(n, part),
+                      whole(wq_o.shape), whole(wq_x.shape), whole(wk.shape), whole(wv.shape), rows_of(n, depth)],
+            out_specs=[rows_of(n, depth), pl.BlockSpec((2 * HEAD_WIDTH, depth), lambda i, *_: (0, 0)),
                        pl.BlockSpec((1, depth), lambda i, *_: (0, 0)),
                        pl.BlockSpec((1, HEAD_WIDTH), lambda i, *_: (0, 0))],
+            scratch_shapes=[pltpu.VMEM((2 * HEAD_WIDTH, depth), F32)],
         ),
-        out_shape=[sds((own, depth), F32), sds((own, HEAD_WIDTH), BF), sds((own, HEAD_WIDTH), BF),
+        out_shape=[sds((own, depth), F32), sds((2 * HEAD_WIDTH, depth), BF),
                    sds((1, depth), F32), sds((1, HEAD_WIDTH), F32)],
+        cost_estimate=cost(8),
         compiler_params=params(),
         name="input_back",
-    )(first_row, x3, gmid, dks[0], dks[1], dvs[0], dvs[1], dk_r, dv_r, kl, cos, sin, gk, g_in,
-      qr_o, qr_x, wq_o, wq_x, wk, wv)
+    )(first_row, x3, gmid, dks[0], dks[1], dvs[0], dvs[1], dk_r, dv_r, kl, cos, sin, rows8,
+      qr_o, qr_x, wq_o, wq_x, wk, wv, nb)
 
 
 def swap(value, n_tensor):
     return lax.ppermute(value, "tensor", [(t, n_tensor - 1 - t) for t in range(n_tensor)])
-
-
-def pair_sum(left_x, left_o, right, n_tensor):
-    sent = tn(left_x, right).astype(BF)
-    got = swap(sent, n_tensor)
-    return (tn(left_o, right) + got.astype(F32)).astype(BF)
 
 
 def bit_of(index, b):
@@ -429,6 +447,10 @@
     turned = plain[1:] + plain[:1]
     lead = (plain[2],) + plain[:2] + plain[3:] if n_bits > 2 else plain[::-1]
     return plain, turned, lead
+
+
+def drop_bit(index, b):
+    return lax.div(index, 2 ** (b + 1)) * 2**b + lax.rem(index, 2**b)
 
 
 def natural_index(me, j, fixed, free):
@@ -445,17 +467,14 @@
     n_items = len(items)
     refs = list(refs)
     take = lambda count: [refs.pop(0) for _ in range(count)]
-    ins = []
-    for order, given in items:
-        ins.append(take(2 if given else 1))
+    ins = [take(2) for _ in items]
     kv_in, g_block, g_in, gq_o, gq_x, g_k = take(6)
     outs = take(n_items)
     kv_out, gain_out = take(2)
     recvs, curs = [], []
-    for order, given in items:
+    for order in items:
         n = len(order)
-        first = 1 if given else 0
-        recvs.append({s: refs.pop(0) for s in range(first, n)})
+        recvs.append({s: refs.pop(0) for s in range(1, n)})
         curs.append({s: refs.pop(0) for s in range(1, n)})
     n_bits = len(kv_order)
     kv_core = refs.pop(0)
@@ -491,45 +510,41 @@
     flying = {}
 
     def start(n, s):
-        order, given = items[n]
+        order = items[n]
+        half = 2 ** (len(order) - s - 1)
+        away = (1 - bit_of(me, order[s])) * half
+        flying[n] = send(curs[n][s].at[pl.ds(away, half)], recvs[n][s], {"dp": partner(order[s])})
+
+    def finish(n, s):
+        order = items[n]
         total = len(order)
         half = 2 ** (total - s - 1)
-        device = {"dp": partner(order[s])}
-        if s == 0:
-            copies = []
-            for j in range(half):
-                index = natural_index(me, j, ((order[0], True),), order[1:])
-                copies.append(send(ins[n][0].at[index], recvs[n][0].at[j], device))
-            flying[n] = copies
-        else:
-            away = (1 - bit_of(me, order[s])) * half
-            flying[n] = [send(curs[n][s].at[pl.ds(away, half)], recvs[n][s], device)]
-
-    def finish(n, s):
-        order, given = items[n]
-        total = len(order)
-        half = 2 ** (total - s - 1)
-        for copy in flying.pop(n, ()):
-            copy.wait_recv()
-        got = ins[n][1] if given and s == 0 else recvs[n][s]
+        if s:
+            flying.pop(n).wait_recv()
+        got = recvs[n][s] if s else ins[n][1]
+        held = curs[n][s] if s else ins[n][0]
 
         def keep_index(j):
             if s == 0:
                 return natural_index(me, j, ((order[0], False),), order[1:])
             return bit_of(me, order[s]) * half + j
 
-        held = ins[n][0] if s == 0 else curs[n][s]
+        def total_at(j):
+            index = keep_index(j)
+            return held[index].astype(F32) + got[j if s else drop_bit(index, order[0])].astype(F32)
+
         if s == total - 1:
-            outs[n][...] = held[keep_index(0)].astype(F32) + got[0].astype(F32)
+            outs[n][...] = total_at(0)
             return
 
         def body(j, carry):
-            curs[n][s + 1][j] = (held[keep_index(j)].astype(F32) + got[j].astype(F32)).astype(BF)
+            curs[n][s + 1][j] = total_at(j).astype(BF)
             return carry
 
         lax.fori_loop(0, half, body, 0)
         start(n, s + 1)
 
+    kv_copy = send(kv_in.at[1 - core], kv_core, {"tensor": 1 - core})
     gain_own[0][...] = jnp.zeros_like(gain_own[0])
     gain_own[0][0:3, :] = g_block[0:3, :]
     gain_own[0][3:4, :] = g_in[...]
@@ -540,13 +555,9 @@
         device = {"tensor": 1 - core} if s == 0 else {"dp": partner(s - 1)}
         return send(gain_own[s], gain_got[s], device)
 
-    kv_copy = send(kv_in.at[1 - core], kv_core, {"tensor": 1 - core})
-    for n, (order, given) in enumerate(items):
-        if given:
-            finish(n, 0)
-        else:
-            start(n, 0)
     gain_copy = gain_start(0)
+    for n in range(n_items):
+        finish(n, 0)
     kv_copy.wait_recv()
 
     def kv_first(j, carry):
@@ -565,7 +576,6 @@
     for k, b in enumerate(kv_order):
         spot = spot + bit_of(me, b) * 2 ** (n_bits - 1 - k)
     kv_copy = kv_start(0)
-    depth_of = [len(order) for order, _ in items]
     for step in range(n_bits):
         half = 2 ** (n_bits - step - 1)
         kv_copy.wait_recv()
@@ -584,9 +594,8 @@
         gain_own[step + 1][...] = gain_own[step][...] + gain_got[step][...]
         gain_copy = gain_start(step + 1)
         for n in range(n_items):
-            s = step + (1 if items[n][1] else 0)
-            if s < depth_of[n]:
-                finish(n, s)
+            if step + 1 < len(items[n]):
+                finish(n, step + 1)
     gain_copy.wait_recv()
     gain_out[...] = gain_own[n_bits][...] + gain_got[n_bits][...]
     for s in reversed(range(n_bits)):
@@ -620,14 +629,12 @@
     copies = 0
     for value, got, order in items:
         n, c, width = value.shape
-        given = got is not None
-        spec.append((tuple(order), given))
-        operands += [value, got] if given else [value]
+        spec.append(tuple(order))
+        operands += [value, got]
         outs.append(sds((c, width), F32))
-        first = 1 if given else 0
-        scratch += [pltpu.VMEM((2 ** (n_bits - s - 1), c, width), BF) for s in range(first, n_bits)]
+        scratch += [pltpu.VMEM((2 ** (n_bits - s - 1), c, width), BF) for s in range(1, n_bits)]
         scratch += [pltpu.VMEM((2 ** (n_bits - s), c, width), BF) for s in range(1, n_bits)]
-        copies += n_bits - 1 + (0 if given else n // 2)
+        copies += n_bits - 1
     _, n, c, width = kv.shape
     scratch += [pltpu.VMEM((n, c, width), BF)]
     scratch += [pltpu.VMEM((2 ** (n_bits - s - 1), c, width), BF) for s in range(n_bits)]
@@ -650,20 +657,60 @@
     )(*operands)
 
 
-def first_hop(value, order, n_dp):
+def fold_kernel(specs, me_ref, *refs):
+    me = me_ref[0]
+    n = len(specs)
+    for k, (rest, done) in enumerate(specs):
+        held, got = refs[2 * k], refs[2 * k + 1]
+        keep, away = refs[2 * n + 2 * k], refs[2 * n + 2 * k + 1]
+        half = 2 ** (len(rest) - 1)
+        mine = bit_of(me, rest[0]) * half
+        other = half - mine
+
+        def body(j, carry, held=held, got=got, keep=keep, away=away, rest=rest, done=done, mine=mine, other=other):
+            for base, dst in ((other, away), (mine, keep)):
+                at = base + j
+                index = at if done is None else natural_index(me, at, ((done, False),), rest)
+                other_index = at if done is None else drop_bit(index, done)
+                dst[j] = (held[index].astype(F32) + got[other_index].astype(F32)).astype(BF)
+            return carry
+
+        lax.fori_loop(0, half, body, 0)
+
+
+def fold(me, items):
+    specs, operands, outs = [], [], []
+    for held, got, rest, done in items:
+        specs.append((tuple(rest), done))
+        operands += [held, got]
+        shape = (got.shape[0] // 2,) + got.shape[1:]
+        outs += [sds(shape, BF), sds(shape, BF)]
+    vmem = pl.BlockSpec(memory_space=pltpu.VMEM)
+    res = pl.pallas_call(
+        functools.partial(fold_kernel, tuple(specs)),
+        out_shape=outs,
+        in_specs=[pl.BlockSpec(memory_space=pltpu.SMEM)] + [vmem] * len(operands),
+        out_specs=[vmem] * len(outs),
+        compiler_params=pltpu.CompilerParams(vmem_limit_bytes=VMEM_LIMIT),
+        name="fold",
+    )(me, *operands)
+    return list(zip(res[0::2], res[1::2]))
+
+
+def hop(value, b, n_dp):
+    return lax.ppermute(value, "dp", [(i, i ^ 2**b) for i in range(n_dp)])
+
+
+def after(value, *others):
+    return lax.optimization_barrier((value,) + others)[0]
+
+
+def first_hop(value, b, n_dp):
     n, c, width = value.shape
-    b = order[0]
-    me = lax.axis_index("dp")
-    away = 1 - bit_of(me, b)
+    away = 1 - bit_of(lax.axis_index("dp"), b)
     view = value.reshape(n // 2 ** (b + 1), 2, 2**b, c, width)
-    sent = lax.dynamic_index_in_dim(view, away, 1, keepdims=False)
-    n_bits = len(order)
-    high = n_bits - 1 - b
-    sent = sent.reshape((2,) * (n_bits - 1) + (c, width))
-    remaining = [k for k in reversed(range(n_bits)) if k != b]
-    axes = [remaining.index(k) for k in order[1:]]
-    sent = sent.transpose(axes + [n_bits - 1, n_bits]).reshape(n // 2, c, width)
-    return lax.ppermute(sent, "dp", [(i, i ^ 2**b) for i in range(n_dp)])
+    sent = lax.dynamic_index_in_dim(view, away, 1, keepdims=False).reshape(n // 2, c, width)
+    return hop(sent, b, n_dp), sent
 
 
 def on_device(n_dp, n_tensor, residual_in, cotangent, segment_ids, gain_attn_in, w_query, w_key, w_value,
@@ -676,52 +723,71 @@
     seg_pad = jnp.concatenate([jnp.full((BLOCK,), -1, jnp.int32), seg])
     seg_ext = lax.dynamic_slice_in_dim(seg_pad, me * own, own + BLOCK, 0)[None]
     starts = jnp.sum((seg[None, :] < jnp.arange(LANES, dtype=jnp.int32)[:, None]).astype(F32), axis=1)[None]
-    row = lambda g: g[None]
+    fill = lambda g: jnp.pad(g, (0, depth - g.shape[0]))
+    rows8 = jnp.stack([gain_attn_in, gain_attn_out, gain_ff_in, gain_ff_out, fill(gain_query), fill(gain_key),
+                       jnp.zeros_like(gain_attn_in), jnp.zeros_like(gain_attn_in)])
     wq_x, wo_x, wg_x, wu_x, wd_x = (swap(w, n_tensor) for w in (w_query, w_out, w_gate, w_up, w_down))
     table = jnp.asarray(rope_table())
     q_o, q_x, ql_o, ql_x, k, v, kl, nb, cos, sin = project(
-        first_row, residual_in, seg_ext, starts, table, row(gain_attn_in), w_query, wq_x, w_key, w_value,
-        row(gain_query), row(gain_key))
+        first_row, residual_in, seg_ext, starts, table, rows8, w_query, wq_x, w_key, w_value)
     weights = (w_out, wo_x, w_gate, wg_x, w_up, wu_x, w_down, wd_x)
     (output, gmid, ga_o, ga_x, af_o, af_x, lse, delta, mid_b, gff, gas,
      act_o, act_x, gg_o, gg_x, gu_o, gu_x, gains) = block_pass(
-        first_row, residual_in, cotangent, seg_ext, q_o, q_x, k, v, weights,
-        row(gain_attn_out), row(gain_ff_in), row(gain_ff_out))
+        first_row, residual_in, cotangent, seg_ext, q_o, q_x, k, v, weights, rows8)
 
     n_bits = n_dp.bit_length() - 1
     plain, turned, lead = bit_orders(n_bits)
     chunks = lambda value: value.reshape(n_dp, value.shape[0] // n_dp, value.shape[1])
-
-    def down_pair():
-        sent = tn(gff, act_x).astype(BF)
-        got = swap(sent, n_tensor)
-        return (tn(gff, act_o) + got.astype(F32)).astype(BF)
-
-    down = chunks(down_pair())
-    down_got = first_hop(down, plain, n_dp)
-    gate = chunks(pair_sum(gg_x, gg_o, mid_b, n_tensor))
-    gate_got = first_hop(gate, turned, n_dp)
-    upw = chunks(pair_sum(gu_x, gu_o, mid_b, n_tensor))
-    upw_got = first_hop(upw, lead, n_dp)
-    out_sent = swap(tn(gas, af_x).astype(BF), n_tensor)
-    out_w = chunks((tn(gas, af_o) + out_sent.astype(F32)).astype(BF))
+    spot = lax.axis_index("dp").astype(jnp.int32).reshape(1)
+
+    pairs = [(gff, act_x, act_o, plain), (mid_b, gg_x, gg_o, turned), (mid_b, gu_x, gu_o, lead), (gas, af_x, af_o, plain)]
+    grad = lambda left, units: tn(left, units) if left is not mid_b else tn(units, left)
+    orders = [order for *_, order in pairs]
+    gots = []
+    last = ()
+    for left, units, _, _ in pairs:
+        sent = grad(left, after(units, *last)).astype(BF)
+        last = (sent,)
+        gots.append(swap(sent, n_tensor))
+    state = []
+    for (left, _, units, order), got in zip(pairs, gots):
+        value = chunks((grad(left, after(units, *last)) + got.astype(F32)).astype(BF))
+        arrived, away = first_hop(value, order[0], n_dp)
+        last = (away,)
+        state.append((value, arrived))
+
+    def advance(state, stage):
+        folded = fold(spot, [(held, got, order[stage:], order[0] if stage == 1 else None)
+                             for (held, got), order in zip(state, orders)])
+        return [(keep, hop(away, order[stage], n_dp)) for (keep, away), order in zip(folded, orders)], folded
 
     heads = q_o.shape[1] // HEAD_WIDTH
-    qr_o, dk_o, dv_o, gq_o = attn_back(0, seg_ext, q_o, k, v, ga_o, lse, delta, ql_o, cos, sin, row(gain_query))
-    qr_x, dk_x, dv_x, gq_x = attn_back(heads, seg_ext, q_x, k, v, ga_x, lse, delta, ql_x, cos, sin, row(gain_query))
+    ga_o = after(ga_o, *last)
+    qr_o, dk_o, dv_o, gq_o = attn_back(0, seg_ext, q_o, k, v, ga_o, lse, delta, ql_o, cos, sin, rows8)
+    state = [(after(value, dv_o), got) for value, got in state]
+    state, folded = advance(state, 1)
+    ga_x = after(ga_x, *(away for _, away in folded))
+    qr_x, dk_x, dv_x, gq_x = attn_back(heads, seg_ext, q_x, k, v, ga_x, lse, delta, ql_x, cos, sin, rows8)
+    state = [(after(value, qr_x), got) for value, got in state]
+    state, folded = advance(state, 2)
+    dk_x, dv_x, qr_x = lax.optimization_barrier((dk_x, dv_x, qr_x, *(away for _, away in folded)))[:3]
     front = jnp.concatenate([dk_o[:BLOCK] + dk_x[:BLOCK], dv_o[:BLOCK] + dv_x[:BLOCK]], axis=1).astype(BF)
     back = lax.ppermute(front, "tensor", [(t, t - 1) for t in range(1, n_tensor)])
-    grad_input, kraw, vraw, gain_in, gain_k = input_back(
+    query_sent = tn(qr_x, nb).astype(BF)
+    query_got = swap(query_sent, n_tensor)
+    query = chunks((tn(qr_o, nb) + query_got.astype(F32)).astype(BF))
+    query_hop, query_away = first_hop(query, turned[0], n_dp)
+    state = [(after(value, query_away), got) for value, got in state]
+    for stage in range(3, n_bits):
+        state, folded = advance(state, stage)
+    gmid = after(gmid, query_away, *(away for _, away in folded))
+    grad_input, kv, gain_in, gain_k = input_back(
         first_row, residual_in, gmid, (dk_o, dk_x), (dv_o, dv_x), back[:, :HEAD_WIDTH], back[:, HEAD_WIDTH:],
-        kl, cos, sin, row(gain_key), row(gain_attn_in), qr_o, qr_x, w_query, wq_x, w_key, w_value)
-    query = chunks(pair_sum(qr_x, qr_o, nb, n_tensor))
-    kv = jnp.stack([tn(kraw, nb), tn(vraw, nb)]).astype(BF)
-    kv = kv.reshape(2, n_dp, kv.shape[1] // n_dp, depth)
-    s_down, s_gate, s_up, s_out, s_query, kv_sum, gain_sum = reduce_all(
-        n_dp,
-        [(down, down_got, plain), (gate, gate_got, turned), (upw, upw_got, lead), (out_w, None, plain),
-         (query, None, turned)],
-        kv, lead, gains, gain_in, gq_o, gq_x, gain_k)
+        kl, cos, sin, rows8, qr_o, qr_x, w_query, wq_x, w_key, w_value, nb)
+    kv = kv.reshape(2, n_dp, HEAD_WIDTH // n_dp, depth)
+    s_query, kv_sum, gain_sum = reduce_all(
+        n_dp, [(query, query_hop, turned)], kv, lead, gains, gain_in, gq_o, gq_x, gain_k)
+    s_down, s_gate, s_up, s_out = [keep[0].astype(F32) + got[0].astype(F32) for keep, got in state]
     kv_sum = kv_sum.reshape(2, HEAD_WIDTH, depth)
     return (
         output[None], grad_input[None], gain_sum[3], s_query.T, kv_sum[0].T, kv_sum[1].T,

time: 231 us -> 228 us (0.987)
  starting transfers between devices: 9.87 us -> 26.3 us
  matrix products: 27.3 us -> 18.4 us
  Pallas kernels: 156 us -> 148 us
    pallas_call x1, Pallas kernels: 62.6 us -> 43.1 us  [reduce_all(): pl.pallas_call(functools.partial(reduce_kernel, tuple(spec), tuple(kv_ord...]
    ppermute x3 -> x17, starting transfers between devices: 4.82 us -> 19.5 us  [hop(): return lax.ppermute(value, 'dp', [(i, i ^ 2 ** b) for i in range(n_dp)])]
    pallas_call x0 -> x3, Pallas kernels: none -> 10.1 us  [fold(): pl.pallas_call(functools.partial(fold_kernel, tuple(specs)), out_shape=ou...]
    dot_general x12 -> x10, matrix products: 27.3 us -> 18.4 us  [tn(): lax.dot_general(a, b, (((0,), (0,)), ((), ())), preferred_element_type=F32)]
    broadcast_in_dim x4 -> x0, local copies, waits for them, and re-layouts: 5.06 us -> none  [on_device(): row = lambda g: g[None]]
    another operation x0 -> x8, local copies, waits for them, and re-layouts: none -> 3.4 us  [on_device(): jnp.stack([gain_attn_in, gain_attn_out, gain_ff_in, gain_ff_out, fill(gai...]
    pallas_call x1, Pallas kernels: 9.17 us -> 12.3 us  [input_back(): pl.pallas_call(kern, grid_spec=pltpu.PrefetchScalarGridSpec(num_scalar_pr...]
    transpose x0 -> x4, other arithmetic: none -> 2.71 us  [on_device(): return (output[None], grad_input[None], gain_sum[3], s_query.T, kv_sum[0]...]
  transfers between devices with their start and end apart: 14 -> 28, of which waited for: 2 -> 2; matrix products, arithmetic and copies ran while one was open for 16% -> 12% of each run, Pallas kernels for 9% -> 21%
where the time goes in v2:
time: 228 us
  Pallas kernels  148 us (65%)
  starting transfers between devices  26.3 us (12%)
  local copies, waits for them, and re-layouts  22.2 us (10%)
  matrix products  18.4 us (8%)
  other arithmetic  5.91 us (3%)
  waiting for transfers between devices  5.81 us (3%)
    pallas_call x1, Pallas kernels, block_pass(): pl.pallas_call(kern, grid_spec=pltpu.PrefetchScalarGridSpec(num_scalar_pr...  49.1 us
    pallas_call x1, Pallas kernels, reduce_all(): pl.pallas_call(functools.partial(reduce_kernel, tuple(spec), tuple(kv_ord...  43.1 us
    pallas_call x2, Pallas kernels, attn_back(): pl.pallas_call(functools.partial(attn_back_kernel, first), grid=(own // n...  22.2 us
    ppermute x17, starting transfers between devices, hop(): return lax.ppermute(value, 'dp', [(i, i ^ 2 ** b) for i in range(n_dp)])  19.5 us
    dot_general x10, matrix products, tn(): lax.dot_general(a, b, (((0,), (0,)), ((), ())), preferred_element_type=F32)  18.4 us
    pallas_call x1, Pallas kernels, input_back(): pl.pallas_call(kern, grid_spec=pltpu.PrefetchScalarGridSpec(num_scalar_pr...  12.3 us
    pallas_call x1, Pallas kernels, project(): pl.pallas_call(project_kernel, grid_spec=pltpu.PrefetchScalarGridSpec(num...  11 us
    pallas_call x3, Pallas kernels, fold(): pl.pallas_call(functools.partial(fold_kernel, tuple(specs)), out_shape=ou...  10.1 us
  transfers between devices with their start and end apart: 28, of which 2 were waited for; matrix products, arithmetic and copies ran while one was open for 12% of the time, Pallas kernels for 21%

profile of v2, /device:TPU:1, one launch (start us, length us, event | category | flops | bytes accessed | tf_op | source)
XLA Modules:
  0.0 227.8 jit_solution(6266934275074769563)
XLA Ops:
  1.8 0.8 pad_dynamic-slice_fusion
  2.6 0.6 broadcast_in_dim.14.seg.refs_2_
  3.2 0.7 pad.8
  3.9 0.7 pad.9
  4.6 0.7 stack.24
  5.2 0.7 stack.25
  5.9 0.7 stack.26
  6.6 0.7 stack.27
  7.3 0.6 stack.31.rows8.refs_15_.refs_11_
  8.0 1.4 convert_reduce_fusion
  9.4 0.8 copy-done.22
  10.2 11.0 %project.1 = (bf16[1024,512]{1,0:T(8,128)(2,1)}, bf16[1024,512]{1,0:T(8,128)(2,1)}, f32[1024,512]{1,0:T(8,128)}, f32[1024,512]{1,0:T(8,128)}, bf16[1536,256]{1,0...) custom-call(s32[1]{0:T(128)} %bitcast.me, ...), custom_call_target="tpu_custom_call" | custom-call | flops 6000000000 | bytes 6000000 | tf_op jit(solution)/shard_map/project/pallas_call | solution.py:322
  21.3 1.0 copy-done.20
  22.8 49.1 %block.1 = (f32[1024,640]{1,0:T(8,128)}, f32[1024,640]{1,0:T(8,128)}, bf16[1024,512]{1,0:T(8,128)(2,1)}, bf16[1024,512]{1,0:T(8,128)(2,1)}, bf16[1024,512]{1,0:T...) custom-call(s32[1]{0:T(128)} %bitcast.me, ...), custom_call_target="tpu_custom_call" | custom-call | flops 40000000000 | bytes 40000000 | tf_op jit(solution)/shard_map/block/pallas_call | solution.py:360
  71.9 3.5 %convolution_convert_fusion.2 = bf16[640,1024]{1,0:T(8,128)(2,1)S(1)} fusion(bf16[1024,640]{1,0:T(8,128)(2,1)} %get-tuple-element.118, bf16[1024,1024]{1,0:T(8,128)(2,1)} %get-tuple-element.123), kind=kOutput, calls=%fused_computation.5 | convolution fusion | flops 1342832640 | bytes 4718592 | tf_op jit(solution)/shard_map/dot_general | solution.py:35
  76.0 3.9 %convolution_convert_fusion.1 = bf16[1024,640]{1,0:T(8,128)(2,1)S(1)} fusion(bf16[1024,1024]{1,0:T(8,128)(2,1)} %get-tuple-element.124, bf16[1024,640]{1,0:T(8,128)(2,1)} %get-tuple-element.125), kind=kOutput, calls=%fused_computation.4 | convolution fusion | flops 1342832640 | bytes 4718592 | tf_op jit(solution)/shard_map/dot_general | solution.py:35
  80.1 1.9 convolution_convert_fusion
  82.5 0.9 convolution_convert_fusion.4
  83.5 0.6 copy-done.37
  84.4 1.6 add_convert_fusion.2
  86.1 2.3 %collective-permute-start.9 = (bf16[8,40,1024]{2,1,0:T(8,128)(2,1)S(1)}, bf16[8,40,1024]{2,1,0:T(8,128)(2,1)}, u32[]{:S(2)}, u32[]{:S(2)}) collective-permute-start(bf16[8,40,1024]{2,1,0:T(8,128)(2,1)S(1)} %dynamic-slice_bitcast_fusion), channel_id=1, source_target_pairs={{0,2},{2,0},{4,6},{6,4},{8,10},{10,8},{12,14},{14,12},{16,18},{18,... | collective-permute-start | bytes 1966088 | tf_op jit(solution)/shard_map/ppermute | solution.py:701
  88.4 1.9 add_convert_fusion.1
  90.4 1.3 collective-permute-start.10
  91.7 1.9 add_convert_fusion
  93.7 1.4 collective-permute-start.11
  95.3 0.9 fusion
  96.5 11.2 %attn_back.2 = (bf16[1024,512]{1,0:T(8,128)(2,1)}, f32[1536,256]{1,0:T(8,128)}, f32[1536,256]{1,0:T(8,128)}, f32[1,256]{1,0:T(1,128)}) custom-call(s32[1,1536]{1,0:T(1,128)} %broadcast_in_dim.14.seg.refs_2_, bf16[1024,512]{1,0:T(8,128)(2,1)} %get-tuple-element.107.refs_3_.q, bf16[1536,256]{1,0:T(8,128)(2,1)} %get-tuple-element.109.refs_5_.k, ...), custom_call_target="tpu_custom_call" | custom-call | flops 10000000000 | bytes 10000000 | tf_op jit(solution)/shard_map/attn_back/pallas_call | solution.py:391
  107.8 2.4 %collective-permute-done.12.refs_7_ = bf16[8,40,512]{2,1,0:T(8,128)(2,1)S(1)} collective-permute-done((bf16[8,40,512]{2,1,0:T(8,128)(2,1)S(1)}, bf16[8,40,512]{2,1,0:T(8,128)(2,1)S(1)}, u32[]{:S(2)}, u32[]{:S(2)}) %collective-permute-start.12) | collective-permute-done | bytes 327712 | tf_op jit(solution)/shard_map/ppermute | solution.py:701
  110.2 0.7 copy-done.5
  110.9 5.1 %fold.3 = (bf16[4,40,1024]{2,1,0:T(8,128)(2,1)}, bf16[4,40,1024]{2,1,0:T(8,128)(2,1)}, bf16[4,64,640]{2,1,0:T(8,128)(2,1)}, bf16[4,64,640]{2,1,0:T(8,128)(2,1)},...) custom-call(s32[1]{0:T(128)} %bitcast.12.me_ref, ...), custom_call_target="tpu_custom_call" | custom-call | tf_op jit(solution)/shard_map/fold/pallas_call | solution.py:689
  116.0 1.1 collective-permute-start.13
  117.1 1.3 collective-permute-start.14
  118.4 1.2 collective-permute-start.15
  119.8 11.0 %attn_back.3 = (bf16[1024,512]{1,0:T(8,128)(2,1)}, f32[1536,256]{1,0:T(8,128)}, f32[1536,256]{1,0:T(8,128)}, f32[1,256]{1,0:T(1,128)}) custom-call(s32[1,1536]{1,0:T(1,128)} %broadcast_in_dim.14.seg.refs_2_, bf16[1024,512]{1,0:T(8,128)(2,1)} %get-tuple-element.108.refs_4_.q, bf16[1536,256]{1,0:T(8,128)(2,1)} %get-tuple-element.109.refs_5_.k, ...), custom_call_target="tpu_custom_call" | custom-call | flops 10000000000 | bytes 10000000 | tf_op jit(solution)/shard_map/attn_back/pallas_call | solution.py:391
  130.9 0.6 copy-done.10
  131.7 0.7 copy-done.8
  132.4 2.8 %fold.4 = (bf16[2,40,1024]{2,1,0:T(8,128)(2,1)}, bf16[2,40,1024]{2,1,0:T(8,128)(2,1)}, bf16[2,64,640]{2,1,0:T(8,128)(2,1)}, bf16[2,64,640]{2,1,0:T(8,128)(2,1)},...) custom-call(s32[1]{0:T(128)} %bitcast.12.me_ref, ...), custom_call_target="tpu_custom_call" | custom-call | tf_op jit(solution)/shard_map/fold/pallas_call | solution.py:689
  135.3 1.8 add_convert_fusion.3
  137.1 4.4 %collective-permute-start.22 = (bf16[512,512]{1,0:T(8,128)(2,1)S(1)}, bf16[512,512]{1,0:T(8,128)(2,1)S(1)}, u32[]{:S(2)}, u32[]{:S(2)}) collective-permute-start(bf16[512,512]{1,0:T(8,128)(2,1)S(1)} %pad_maximum_fusion), channel_id=1, source_target_pairs={{1,0},{3,2},{5,4},{7,6},{9,8},{11,10},{13,12},{15,14},{17,16},{19,... | collective-permute-start | bytes 1572872 | tf_op jit(solution)/shard_map/ppermute | solution.py:775
  141.5 1.0 convolution_convert_fusion.3
  142.9 2.3 %collective-permute-start.19 = (bf16[2,64,640]{2,1,0:T(8,128)(2,1)S(1)}, bf16[2,64,640]{2,1,0:T(8,128)(2,1)S(1)}, u32[]{:S(2)}, u32[]{:S(2)}) collective-permute-start(bf16[2,64,640]{2,1,0:T(8,128)(2,1)S(1)} %copy-done.24), channel_id=1, source_target_pairs={{0,16},{2,18},{4,20},{6,22},{8,24},{10,26},{12,28},{14,30},{16,0},... | collective-permute-start | bytes 491528 | tf_op jit(solution)/shard_map/ppermute | solution.py:701
  145.2 1.2 collective-permute-start.20
  146.4 1.3 collective-permute-start.21
  147.7 0.9 fusion.3
  148.6 1.0 fusion.1
  150.0 3.3 %collective-permute-done.21.refs_7_ = bf16[2,40,512]{2,1,0:T(8,128)(2,1)S(1)} collective-permute-done((bf16[2,40,512]{2,1,0:T(8,128)(2,1)S(1)}, bf16[2,40,512]{2,1,0:T(8,128)(2,1)S(1)}, u32[]{:S(2)}, u32[]{:S(2)}) %collective-permute-start.21) | collective-permute-done | bytes 81952 | tf_op jit(solution)/shard_map/ppermute | solution.py:701
  153.3 0.6 copy-done.14
  154.1 0.7 copy-done.13
  154.7 2.2 fold.5
  156.9 2.3 %collective-permute-start.27 = (bf16[1,40,1024]{2,1,0:T(8,128)(2,1)}, bf16[1,40,1024]{2,1,0:T(8,128)(2,1)S(1)}, u32[]{:S(2)}, u32[]{:S(2)}) collective-permute-start(bf16[1,40,1024]{2,1,0:T(8,128)(2,1)} %get-tuple-element.176), channel_id=1, source_target_pairs={{0,16},{2,18},{4,20},{6,22},{8,24},{10,26},{12,28},{14,30},{16,0},... | collective-permute-start | bytes 245768 | tf_op jit(solution)/shard_map/ppermute | solution.py:701
  159.6 2.3 %collective-permute-start.24 = (bf16[1,40,512]{2,1,0:T(8,128)(2,1)}, bf16[1,40,512]{2,1,0:T(8,128)(2,1)S(1)}, u32[]{:S(2)}, u32[]{:S(2)}) collective-permute-start(bf16[1,40,512]{2,1,0:T(8,128)(2,1)} %get-tuple-element.179), channel_id=1, source_target_pairs={{0,16},{2,18},{4,20},{6,22},{8,24},{10,26},{12,28},{14,30},{16,0},... | collective-permute-start | bytes 122888 | tf_op jit(solution)/shard_map/ppermute | solution.py:701
  161.9 12.3 %input_back.1 = (f32[1024,640]{1,0:T(8,128)}, bf16[512,640]{1,0:T(8,128)(2,1)}, f32[1,640]{1,0:T(1,128)}, f32[1,256]{1,0:T(1,128)}) custom-call(s32[1]{0:T(128)} %bitcast.me, f32[1,2048,640]{2,1,0:T(8,128)} %refs_0_.3, f32[1024,640]{1,0:T(8,128)} %get-tuple-element.180.refs_1_, f32[1536,256]{1,0:T(8,128)} %get-tuple-element.181.refs_2_, ...), custom_call_target="tpu_custom_call" | custom-call | flops 8000000000 | bytes 8000000 | tf_op jit(solution)/shard_map/input_back/pallas_call | solution.py:413
  174.2 0.6 add_bitcast_fusion.3
  174.9 0.7 add_bitcast_fusion
  175.6 0.7 add_bitcast_fusion.1
  176.3 0.7 add_bitcast_fusion.2
  177.0 0.7 copy-done.9
  177.7 43.1 %reduce_all.1 = (f32[32,640]{1,0:T(8,128)}, f32[2,16,16,640]{3,2,1,0:T(8,128)}, f32[8,640]{1,0:T(8,128)}) custom-call(bf16[16,32,640]{2,1,0:T(8,128)(2,1)} %bitcast.86, bf16[8,32,640]{2,1,0:T(8,128)(2,1)} %copy-done.9, bf16[2,16,16,640]{3,2,1,0:T(8,128)(2,1)} %bitcast.89, f32[8,640]{1,0:T(8,128)} %get-tuple-element.187.refs_3_, ...), custom_call_target="tpu_custom_call" | custom-call | tf_op jit(solution)/shard_map/reduce_all/pallas_call | solution.py:649
  220.8 1.5 slice_reduce_fusion
  222.3 1.3 fusion.4
  223.6 1.4 fusion.2
  225.0 1.1 copy.44
  226.1 1.1 copy.45
  227.2 0.6 copy.52
  (120 shorter events, 5.8 us)
Async XLA Ops:
  0.6 20.6 %collective-permute-start.2 = (bf16[640,1024]{1,0:T(8,128)(2,1)}, bf16[640,1024]{1,0:T(8,128)(2,1)S(1)}, u32[]{:S(2)}, u32[]{:S(2)}) collective-permute-start(bf16[640,1024]{1,0:T(8,128)(2,1)} %refs_9_.1), channel_id=1, source_target_pairs={{0,1},{1,0},{2,3},{3,2},{4,5},{5,4},{6,7},{7,6},{8,9},{9,8},{10,11... | collective-permute-start | bytes 3932168 | tf_op jit(solution)/shard_map/ppermute | solution.py:438
  0.7 20.6 %collective-permute-start.3 = (bf16[640,1024]{1,0:T(8,128)(2,1)}, bf16[640,1024]{1,0:T(8,128)(2,1)S(1)}, u32[]{:S(2)}, u32[]{:S(2)}) collective-permute-start(bf16[640,1024]{1,0:T(8,128)(2,1)} %refs_11_.1), channel_id=1, source_target_pairs={{0,1},{1,0},{2,3},{3,2},{4,5},{5,4},{6,7},{7,6},{8,9},{9,8},{10,11... | collective-permute-start | bytes 3932168 | tf_op jit(solution)/shard_map/ppermute | solution.py:438
  1.2 20.1 %collective-permute-start.4 = (bf16[1024,640]{1,0:T(8,128)(2,1)}, bf16[1024,640]{1,0:T(8,128)(2,1)}, u32[]{:S(2)}, u32[]{:S(2)}) collective-permute-start(bf16[1024,640]{1,0:T(8,128)(2,1)} %refs_13_.1), channel_id=1, source_target_pairs={{0,1},{1,0},{2,3},{3,2},{4,5},{5,4},{6,7},{7,6},{8,9},{9,8},{10,11... | collective-permute-start | bytes 3932168 | tf_op jit(solution)/shard_map/ppermute | solution.py:438
  1.3 8.1 %collective-permute-start = (bf16[640,512]{1,0:T(8,128)(2,1)}, bf16[640,512]{1,0:T(8,128)(2,1)S(1)}, u32[]{:S(2)}, u32[]{:S(2)}) collective-permute-start(bf16[640,512]{1,0:T(8,128)(2,1)} %refs_14_.1), channel_id=1, source_target_pairs={{0,1},{1,0},{2,3},{3,2},{4,5},{5,4},{6,7},{7,6},{8,9},{9,8},{10,11... | collective-permute-start | bytes 1966088 | tf_op jit(solution)/shard_map/ppermute | solution.py:438
  1.7 19.5 %collective-permute-start.1 = (bf16[512,640]{1,0:T(8,128)(2,1)}, bf16[512,640]{1,0:T(8,128)(2,1)}, u32[]{:S(2)}, u32[]{:S(2)}) collective-permute-start(bf16[512,640]{1,0:T(8,128)(2,1)} %refs_7_.1), channel_id=1, source_target_pairs={{0,1},{1,0},{2,3},{3,2},{4,5},{5,4},{6,7},{7,6},{8,9},{9,8},{10,11... | collective-permute-start | bytes 1966088 | tf_op jit(solution)/shard_map/ppermute | solution.py:438
  9.4 0.8 copy-start.22
  21.3 1.1 copy-start.20
  21.3 1.5 copy-start.21
  75.5 8.0 %collective-permute-start.5 = (bf16[640,1024]{1,0:T(8,128)(2,1)S(1)}, bf16[640,1024]{1,0:T(8,128)(2,1)S(1)}, u32[]{:S(2)}, u32[]{:S(2)}) collective-permute-start(bf16[640,1024]{1,0:T(8,128)(2,1)S(1)} %convolution_convert_fusion.2), channel_id=1, source_target_pairs={{0,1},{1,0},{2,3},{3,2},{4,5},{5,4},{6,7},{7,6},{8,9},{9,8},{10,11... | collective-permute-start | bytes 3932168 | tf_op jit(solution)/shard_map/ppermute | solution.py:438
  76.0 4.1 %copy-start.35 = (bf16[1024,1024]{1,0:T(8,128)(2,1)S(1)}, bf16[1024,1024]{1,0:T(8,128)(2,1)}, u32[]{:S(2)}) copy-start(bf16[1024,1024]{1,0:T(8,128)(2,1)} %get-tuple-element.126) | copy-start | bytes 6291460
  76.0 4.1 %copy-start.36 = (bf16[1024,640]{1,0:T(8,128)(2,1)S(1)}, bf16[1024,640]{1,0:T(8,128)(2,1)}, u32[]{:S(2)}) copy-start(bf16[1024,640]{1,0:T(8,128)(2,1)} %get-tuple-element.125) | copy-start | bytes 3932164
  79.9 8.5 %collective-permute-start.6 = (bf16[1024,640]{1,0:T(8,128)(2,1)S(1)}, bf16[1024,640]{1,0:T(8,128)(2,1)S(1)}, u32[]{:S(2)}, u32[]{:S(2)}) collective-permute-start(bf16[1024,640]{1,0:T(8,128)(2,1)S(1)} %convolution_convert_fusion.1), channel_id=1, source_target_pairs={{0,1},{1,0},{2,3},{3,2},{4,5},{5,4},{6,7},{7,6},{8,9},{9,8},{10,11... | collective-permute-start | bytes 3932168 | tf_op jit(solution)/shard_map/ppermute | solution.py:438
  80.1 2.4 %copy-start.28 = (bf16[1024,640]{1,0:T(8,128)(2,1)S(1)}, bf16[1024,640]{1,0:T(8,128)(2,1)}, u32[]{:S(2)}) copy-start(bf16[1024,640]{1,0:T(8,128)(2,1)} %get-tuple-element.114) | copy-start | bytes 3932164
  80.1 2.4 %copy-start.32 = (bf16[1024,512]{1,0:T(8,128)(2,1)S(1)}, bf16[1024,512]{1,0:T(8,128)(2,1)}, u32[]{:S(2)}) copy-start(bf16[1024,512]{1,0:T(8,128)(2,1)} %get-tuple-element.127) | copy-start | bytes 3145732
  82.0 9.7 %collective-permute-start.7 = (bf16[1024,640]{1,0:T(8,128)(2,1)S(1)}, bf16[1024,640]{1,0:T(8,128)(2,1)S(1)}, u32[]{:S(2)}, u32[]{:S(2)}) collective-permute-start(bf16[1024,640]{1,0:T(8,128)(2,1)S(1)} %convolution_convert_fusion), channel_id=1, source_target_pairs={{0,1},{1,0},{2,3},{3,2},{4,5},{5,4},{6,7},{7,6},{8,9},{9,8},{10,11... | collective-permute-start | bytes 3932168 | tf_op jit(solution)/shard_map/ppermute | solution.py:438
  82.5 1.6 copy-start.37
  82.5 1.9 copy-start.38
  83.3 11.7 %collective-permute-start.8 = (bf16[640,512]{1,0:T(8,128)(2,1)S(1)}, bf16[640,512]{1,0:T(8,128)(2,1)S(1)}, u32[]{:S(2)}, u32[]{:S(2)}) collective-permute-start(bf16[640,512]{1,0:T(8,128)(2,1)S(1)} %convolution_convert_fusion.4), channel_id=1, source_target_pairs={{0,1},{1,0},{2,3},{3,2},{4,5},{5,4},{6,7},{7,6},{8,9},{9,8},{10,11... | collective-permute-start | bytes 1966088 | tf_op jit(solution)/shard_map/ppermute | solution.py:438
  84.4 4.0 %copy-start.34 = (bf16[1024,1024]{1,0:T(8,128)(2,1)S(1)}, bf16[1024,1024]{1,0:T(8,128)(2,1)}, u32[]{:S(2)}) copy-start(bf16[1024,1024]{1,0:T(8,128)(2,1)} %get-tuple-element.129) | copy-start | bytes 6291460
  86.0 4.3 %copy-start = (bf16[640,1024]{1,0:T(8,128)(2,1)}, bf16[640,1024]{1,0:T(8,128)(2,1)S(1)}, u32[]{:S(2)}) copy-start(bf16[640,1024]{1,0:T(8,128)(2,1)S(1)} %add_convert_fusion.2) | copy-start | bytes 3932164
  86.1 24.2 %collective-permute-start.9 = (bf16[8,40,1024]{2,1,0:T(8,128)(2,1)S(1)}, bf16[8,40,1024]{2,1,0:T(8,128)(2,1)}, u32[]{:S(2)}, u32[]{:S(2)}) collective-permute-start(bf16[8,40,1024]{2,1,0:T(8,128)(2,1)S(1)} %dynamic-slice_bitcast_fusion), channel_id=1, source_target_pairs={{0,2},{2,0},{4,6},{6,4},{8,10},{10,8},{12,14},{14,12},{16,18},{18,... | collective-permute-start | bytes 1966088 | tf_op jit(solution)/shard_map/ppermute | solution.py:701
  88.4 3.3 %copy-start.33 = (bf16[1024,1024]{1,0:T(8,128)(2,1)S(1)}, bf16[1024,1024]{1,0:T(8,128)(2,1)}, u32[]{:S(2)}) copy-start(bf16[1024,1024]{1,0:T(8,128)(2,1)} %get-tuple-element.130) | copy-start | bytes 6291460
  90.3 3.3 %copy-start.1 = (bf16[1024,640]{1,0:T(8,128)(2,1)}, bf16[1024,640]{1,0:T(8,128)(2,1)S(1)}, u32[]{:S(2)}) copy-start(bf16[1024,640]{1,0:T(8,128)(2,1)S(1)} %add_convert_fusion.1) | copy-start | bytes 3932164
  90.4 19.8 %collective-permute-start.10 = (bf16[8,64,640]{2,1,0:T(8,128)(2,1)S(1)}, bf16[8,64,640]{2,1,0:T(8,128)(2,1)}, u32[]{:S(2)}, u32[]{:S(2)}) collective-permute-start(bf16[8,64,640]{2,1,0:T(8,128)(2,1)S(1)} %bitcast.90), channel_id=1, source_target_pairs={{0,4},{2,6},{4,0},{6,2},{8,12},{10,14},{12,8},{14,10},{16,20},{18,... | collective-permute-start | bytes 1966088 | tf_op jit(solution)/shard_map/ppermute | solution.py:701
  93.6 2.6 %copy-start.2 = (bf16[1024,640]{1,0:T(8,128)(2,1)}, bf16[1024,640]{1,0:T(8,128)(2,1)S(1)}, u32[]{:S(2)}) copy-start(bf16[1024,640]{1,0:T(8,128)(2,1)S(1)} %add_convert_fusion) | copy-start | bytes 3932164
  93.6 1.7 copy-start.31
  93.7 16.5 %collective-permute-start.11 = (bf16[8,64,640]{2,1,0:T(8,128)(2,1)S(1)}, bf16[8,64,640]{2,1,0:T(8,128)(2,1)}, u32[]{:S(2)}, u32[]{:S(2)}) collective-permute-start(bf16[8,64,640]{2,1,0:T(8,128)(2,1)S(1)} %bitcast.93), channel_id=1, source_target_pairs={{0,8},{2,10},{4,12},{6,14},{8,0},{10,2},{12,4},{14,6},{16,24},{18,... | collective-permute-start | bytes 1966088 | tf_op jit(solution)/shard_map/ppermute | solution.py:701
  96.2 11.6 %copy-start.4 = (bf16[640,512]{1,0:T(8,128)(2,1)}, bf16[640,512]{1,0:T(8,128)(2,1)S(1)}, u32[]{:S(2)}) copy-start(bf16[640,512]{1,0:T(8,128)(2,1)S(1)} %fusion) | copy-start | bytes 1966084
  96.2 14.0 %collective-permute-start.12 = (bf16[8,40,512]{2,1,0:T(8,128)(2,1)S(1)}, bf16[8,40,512]{2,1,0:T(8,128)(2,1)S(1)}, u32[]{:S(2)}, u32[]{:S(2)}) collective-permute-start(bf16[8,40,512]{2,1,0:T(8,128)(2,1)S(1)} %dynamic-slice_bitcast_fusion.1), channel_id=1, source_target_pairs={{0,2},{2,0},{4,6},{6,4},{8,10},{10,8},{12,14},{14,12},{16,18},{18,... | collective-permute-start | bytes 983048 | tf_op jit(solution)/shard_map/ppermute | solution.py:701
  110.2 0.7 copy-start.5
  116.0 14.8 %collective-permute-start.13 = (bf16[4,40,1024]{2,1,0:T(8,128)(2,1)}, bf16[4,40,1024]{2,1,0:T(8,128)(2,1)S(1)}, u32[]{:S(2)}, u32[]{:S(2)}) collective-permute-start(bf16[4,40,1024]{2,1,0:T(8,128)(2,1)} %get-tuple-element.146), channel_id=1, source_target_pairs={{0,4},{2,6},{4,0},{6,2},{8,12},{10,14},{12,8},{14,10},{16,20},{18,... | collective-permute-start | bytes 983048 | tf_op jit(solution)/shard_map/ppermute | solution.py:701
  117.1 13.7 %collective-permute-start.14 = (bf16[4,64,640]{2,1,0:T(8,128)(2,1)}, bf16[4,64,640]{2,1,0:T(8,128)(2,1)S(1)}, u32[]{:S(2)}, u32[]{:S(2)}) collective-permute-start(bf16[4,64,640]{2,1,0:T(8,128)(2,1)} %get-tuple-element.147), channel_id=1, source_target_pairs={{0,8},{2,10},{4,12},{6,14},{8,0},{10,2},{12,4},{14,6},{16,24},{18,... | collective-permute-start | bytes 983048 | tf_op jit(solution)/shard_map/ppermute | solution.py:701
  118.4 12.5 %collective-permute-start.15 = (bf16[4,64,640]{2,1,0:T(8,128)(2,1)}, bf16[4,64,640]{2,1,0:T(8,128)(2,1)S(1)}, u32[]{:S(2)}, u32[]{:S(2)}) collective-permute-start(bf16[4,64,640]{2,1,0:T(8,128)(2,1)} %get-tuple-element.148), channel_id=1, source_target_pairs={{0,2},{2,0},{4,6},{6,4},{8,10},{10,8},{12,14},{14,12},{16,18},{18,... | collective-permute-start | bytes 983048 | tf_op jit(solution)/shard_map/ppermute | solution.py:701
  119.6 11.2 %collective-permute-start.16 = (bf16[4,40,512]{2,1,0:T(8,128)(2,1)}, bf16[4,40,512]{2,1,0:T(8,128)(2,1)S(1)}, u32[]{:S(2)}, u32[]{:S(2)}) collective-permute-start(bf16[4,40,512]{2,1,0:T(8,128)(2,1)} %get-tuple-element.149), channel_id=1, source_target_pairs={{0,4},{2,6},{4,0},{6,2},{8,12},{10,14},{12,8},{14,10},{16,20},{18,... | collective-permute-start | bytes 491528 | tf_op jit(solution)/shard_map/ppermute | solution.py:701
  130.8 0.8 copy-start.6
  130.8 0.8 copy-start.7
  131.7 0.7 copy-start.8
  135.3 6.2 %copy-start.27 = (bf16[1024,640]{1,0:T(8,128)(2,1)S(1)}, bf16[1024,640]{1,0:T(8,128)(2,1)}, u32[]{:S(2)}) copy-start(bf16[1024,640]{1,0:T(8,128)(2,1)} %get-tuple-element.139.refs_18_) | copy-start | bytes 3932164
  135.3 6.2 %copy-start.30 = (bf16[1024,512]{1,0:T(8,128)(2,1)S(1)}, bf16[1024,512]{1,0:T(8,128)(2,1)}, u32[]{:S(2)}) copy-start(bf16[1024,512]{1,0:T(8,128)(2,1)} %get-tuple-element.167.refs_13_) | copy-start | bytes 3145732
  137.1 9.3 %collective-permute-start.22 = (bf16[512,512]{1,0:T(8,128)(2,1)S(1)}, bf16[512,512]{1,0:T(8,128)(2,1)S(1)}, u32[]{:S(2)}, u32[]{:S(2)}) collective-permute-start(bf16[512,512]{1,0:T(8,128)(2,1)S(1)} %pad_maximum_fusion), channel_id=1, source_target_pairs={{1,0},{3,2},{5,4},{7,6},{9,8},{11,10},{13,12},{15,14},{17,16},{19,... | collective-permute-start | bytes 1572872 | tf_op jit(solution)/shard_map/ppermute | solution.py:775
  141.5 1.2 copy-start.25
  141.5 1.4 copy-start.24
  141.5 3.7 %copy-start.23 = (bf16[2,64,640]{2,1,0:T(8,128)(2,1)S(1)}, bf16[2,64,640]{2,1,0:T(8,128)(2,1)}, u32[]{:S(2)}) copy-start(bf16[2,64,640]{2,1,0:T(8,128)(2,1)} %get-tuple-element.165) | copy-start | bytes 491524
  141.5 4.9 %copy-start.26 = (bf16[2,40,512]{2,1,0:T(8,128)(2,1)S(1)}, bf16[2,40,512]{2,1,0:T(8,128)(2,1)}, u32[]{:S(2)}) copy-start(bf16[2,40,512]{2,1,0:T(8,128)(2,1)} %get-tuple-element.166) | copy-start | bytes 245764
  141.5 7.1 %copy-start.29 = (bf16[1024,512]{1,0:T(8,128)(2,1)S(1)}, bf16[1024,512]{1,0:T(8,128)(2,1)}, u32[]{:S(2)}) copy-start(bf16[1024,512]{1,0:T(8,128)(2,1)} %get-tuple-element.138.refs_12_) | copy-start | bytes 3145732
  142.6 6.0 %collective-permute-start.17 = (bf16[512,640]{1,0:T(8,128)(2,1)S(1)}, bf16[512,640]{1,0:T(8,128)(2,1)S(1)}, u32[]{:S(2)}, u32[]{:S(2)}) collective-permute-start(bf16[512,640]{1,0:T(8,128)(2,1)S(1)} %convolution_convert_fusion.3), channel_id=1, source_target_pairs={{0,1},{1,0},{2,3},{3,2},{4,5},{5,4},{6,7},{7,6},{8,9},{9,8},{10,11... | collective-permute-start | bytes 1966088 | tf_op jit(solution)/shard_map/ppermute | solution.py:438
  142.6 10.7 %collective-permute-start.18 = (bf16[2,40,1024]{2,1,0:T(8,128)(2,1)S(1)}, bf16[2,40,1024]{2,1,0:T(8,128)(2,1)S(1)}, u32[]{:S(2)}, u32[]{:S(2)}) collective-permute-start(bf16[2,40,1024]{2,1,0:T(8,128)(2,1)S(1)} %copy-done.25), channel_id=1, source_target_pairs={{0,8},{2,10},{4,12},{6,14},{8,0},{10,2},{12,4},{14,6},{16,24},{18,... | collective-permute-start | bytes 491528 | tf_op jit(solution)/shard_map/ppermute | solution.py:701
  142.9 10.4 %collective-permute-start.19 = (bf16[2,64,640]{2,1,0:T(8,128)(2,1)S(1)}, bf16[2,64,640]{2,1,0:T(8,128)(2,1)S(1)}, u32[]{:S(2)}, u32[]{:S(2)}) collective-permute-start(bf16[2,64,640]{2,1,0:T(8,128)(2,1)S(1)} %copy-done.24), channel_id=1, source_target_pairs={{0,16},{2,18},{4,20},{6,22},{8,24},{10,26},{12,28},{14,30},{16,0},... | collective-permute-start | bytes 491528 | tf_op jit(solution)/shard_map/ppermute | solution.py:701
  145.2 8.2 %collective-permute-start.20 = (bf16[2,64,640]{2,1,0:T(8,128)(2,1)S(1)}, bf16[2,64,640]{2,1,0:T(8,128)(2,1)S(1)}, u32[]{:S(2)}, u32[]{:S(2)}) collective-permute-start(bf16[2,64,640]{2,1,0:T(8,128)(2,1)S(1)} %copy-done.23), channel_id=1, source_target_pairs={{0,4},{2,6},{4,0},{6,2},{8,12},{10,14},{12,8},{14,10},{16,20},{18,... | collective-permute-start | bytes 491528 | tf_op jit(solution)/shard_map/ppermute | solution.py:701
  146.4 6.9 %collective-permute-start.21 = (bf16[2,40,512]{2,1,0:T(8,128)(2,1)S(1)}, bf16[2,40,512]{2,1,0:T(8,128)(2,1)S(1)}, u32[]{:S(2)}, u32[]{:S(2)}) collective-permute-start(bf16[2,40,512]{2,1,0:T(8,128)(2,1)S(1)} %copy-done.26), channel_id=1, source_target_pairs={{0,8},{2,10},{4,12},{6,14},{8,0},{10,2},{12,4},{14,6},{16,24},{18,... | collective-permute-start | bytes 245768 | tf_op jit(solution)/shard_map/ppermute | solution.py:701
  149.6 24.6 %copy-start.3 = (bf16[512,640]{1,0:T(8,128)(2,1)}, bf16[512,640]{1,0:T(8,128)(2,1)S(1)}, u32[]{:S(2)}) copy-start(bf16[512,640]{1,0:T(8,128)(2,1)S(1)} %fusion.1) | copy-start | bytes 1966084
  149.7 27.3 %collective-permute-start.23 = (bf16[8,32,640]{2,1,0:T(8,128)(2,1)S(1)}, bf16[8,32,640]{2,1,0:T(8,128)(2,1)S(1)}, u32[]{:S(2)}, u32[]{:S(2)}) collective-permute-start(bf16[8,32,640]{2,1,0:T(8,128)(2,1)S(1)} %bitcast.94), channel_id=1, source_target_pairs={{0,4},{2,6},{4,0},{6,2},{8,12},{10,14},{12,8},{14,10},{16,20},{18,... | collective-permute-start | bytes 983048 | tf_op jit(solution)/shard_map/ppermute | solution.py:701
  153.3 0.7 copy-start.11
  153.3 0.7 copy-start.12
  156.9 18.0 %collective-permute-start.27 = (bf16[1,40,1024]{2,1,0:T(8,128)(2,1)}, bf16[1,40,1024]{2,1,0:T(8,128)(2,1)S(1)}, u32[]{:S(2)}, u32[]{:S(2)}) collective-permute-start(bf16[1,40,1024]{2,1,0:T(8,128)(2,1)} %get-tuple-element.176), channel_id=1, source_target_pairs={{0,16},{2,18},{4,20},{6,22},{8,24},{10,26},{12,28},{14,30},{16,0},... | collective-permute-start | bytes 245768 | tf_op jit(solution)/shard_map/ppermute | solution.py:701
  159.2 16.3 %collective-permute-start.26 = (bf16[1,64,640]{2,1,0:T(8,128)(2,1)}, bf16[1,64,640]{2,1,0:T(8,128)(2,1)S(1)}, u32[]{:S(2)}, u32[]{:S(2)}) collective-permute-start(bf16[1,64,640]{2,1,0:T(8,128)(2,1)} %get-tuple-element.178), channel_id=1, source_target_pairs={{0,16},{2,18},{4,20},{6,22},{8,24},{10,26},{12,28},{14,30},{16,0},... | collective-permute-start | bytes 245768 | tf_op jit(solution)/shard_map/ppermute | solution.py:701
  159.3 17.0 %collective-permute-start.25 = (bf16[1,64,640]{2,1,0:T(8,128)(2,1)}, bf16[1,64,640]{2,1,0:T(8,128)(2,1)S(1)}, u32[]{:S(2)}, u32[]{:S(2)}) collective-permute-start(bf16[1,64,640]{2,1,0:T(8,128)(2,1)} %get-tuple-element.177), channel_id=1, source_target_pairs={{0,2},{2,0},{4,6},{6,4},{8,10},{10,8},{12,14},{14,12},{16,18},{18,... | collective-permute-start | bytes 245768 | tf_op jit(solution)/shard_map/ppermute | solution.py:701
  159.6 14.6 %collective-permute-start.24 = (bf16[1,40,512]{2,1,0:T(8,128)(2,1)}, bf16[1,40,512]{2,1,0:T(8,128)(2,1)S(1)}, u32[]{:S(2)}, u32[]{:S(2)}) collective-permute-start(bf16[1,40,512]{2,1,0:T(8,128)(2,1)} %get-tuple-element.179), channel_id=1, source_target_pairs={{0,16},{2,18},{4,20},{6,22},{8,24},{10,26},{12,28},{14,30},{16,0},... | collective-permute-start | bytes 122888 | tf_op jit(solution)/shard_map/ppermute | solution.py:701
  161.9 12.4 %copy-start.19 = (bf16[1,40,512]{2,1,0:T(8,128)(2,1)S(1)}, bf16[1,40,512]{2,1,0:T(8,128)(2,1)}, u32[]{:S(2)}) copy-start(bf16[1,40,512]{2,1,0:T(8,128)(2,1)} %get-tuple-element.195) | copy-start | bytes 122884
  161.9 13.0 %copy-start.17 = (bf16[1,40,1024]{2,1,0:T(8,128)(2,1)S(1)}, bf16[1,40,1024]{2,1,0:T(8,128)(2,1)}, u32[]{:S(2)}) copy-start(bf16[1,40,1024]{2,1,0:T(8,128)(2,1)} %get-tuple-element.198) | copy-start | bytes 245764
  161.9 13.7 %copy-start.16 = (bf16[1,64,640]{2,1,0:T(8,128)(2,1)S(1)}, bf16[1,64,640]{2,1,0:T(8,128)(2,1)}, u32[]{:S(2)}) copy-start(bf16[1,64,640]{2,1,0:T(8,128)(2,1)} %get-tuple-element.197) | copy-start | bytes 245764
  161.9 14.4 %copy-start.15 = (bf16[1,64,640]{2,1,0:T(8,128)(2,1)S(1)}, bf16[1,64,640]{2,1,0:T(8,128)(2,1)}, u32[]{:S(2)}) copy-start(bf16[1,64,640]{2,1,0:T(8,128)(2,1)} %get-tuple-element.196) | copy-start | bytes 245764
  177.0 0.7 copy-start.9
  225.0 2.2 copy-start.18
  (3 other events, 2.0 us)

commit v3 on v2

--- a/solution.py
+++ b/solution.py
@@ -212,10 +212,11 @@
     gains[2:3, :] += jnp.sum(gmid * hat_attn, axis=0, keepdims=True)
 
 
-def attn_back_kernel(first, seg, q, k, v, ga, lse, delta, ql, cos, sin, rows8, qraw, dk, dv, gain):
+def attn_back_kernel(seg, q_o, q_x, k, v, ga_o, ga_x, lse, delta, ql_o, ql_x, cos, sin, rows8,
+                     qr_o, qr_x, dk_out, dv_out, front, gain, dk, dv):
     (gq,) = gain_refs(rows8, 4)
     i = pl.program_id(0)
-    rows = q.shape[0]
+    rows = q_o.shape[0]
     base = pl.multiple_of(i * rows, rows)
 
     @pl.when(i == 0)
@@ -234,14 +235,16 @@
     dk_sum = None
     dv_sum = None
     g_sum = None
-    for h in range(q.shape[1] // HEAD_WIDTH):
+    heads = q_o.shape[1] // HEAD_WIDTH
+    for n in range(2 * heads):
+        q, ga, ql, qraw = ((q_o, ga_o, ql_o, qr_o), (q_x, ga_x, ql_x, qr_x))[n // heads]
+        h = n % heads
         cols = slice(h * HEAD_WIDTH, (h + 1) * HEAD_WIDTH)
-        at = slice(first + h, first + h + 1)
         qh = q[:, cols]
         gh = ga[:, cols]
         s = jnp.where(mask, nt(k_win, qh), -jnp.inf)
-        p = jnp.exp(s - lse[at, :])
-        ds = (p * (nt(v_win, gh) - delta[at, :])).astype(BF)
+        p = jnp.exp(s - lse[n : n + 1, :])
+        ds = (p * (nt(v_win, gh) - delta[n : n + 1, :])).astype(BF)
         dq = tn(ds, k_win) * SCORE_SCALE
         a = nn(ds, qh)
         b = nn(p.astype(BF), gh)
@@ -256,15 +259,22 @@
     dv[pl.ds(base, WIN), :] += dv_sum
     gain[...] += g_sum
 
-
-def input_back_kernel(x, gmid, dk_o, dk_x, dv_o, dv_x, dk_r, dv_r, kl, cos, sin, rows8,
+    @pl.when(i == pl.num_programs(0) - 1)
+    def _():
+        front[:, :HEAD_WIDTH] = dk[:BLOCK, :].astype(BF)
+        front[:, HEAD_WIDTH:] = dv[:BLOCK, :].astype(BF)
+        dk_out[...] = dk[BLOCK:, :]
+        dv_out[...] = dv[BLOCK:, :]
+
+
+def input_back_kernel(x, gmid, dk_own, dv_own, back, kl, cos, sin, rows8,
                       qr_o, qr_x, wq_o, wq_x, wk, wv, nb, gin_out, kv_out, gains, gain_k, kv_acc):
     g_in, gk = gain_refs(rows8, 0, 5)
     i = pl.program_id(0)
     last = pl.num_programs(0) - 1
     tail = (i == last).astype(F32)
-    dk = dk_o[...] + dk_x[...] + tail * dk_r[...].astype(F32)
-    dv = dv_o[...] + dv_x[...] + tail * dv_r[...].astype(F32)
+    dk = dk_own[...] + tail * back[:, :HEAD_WIDTH].astype(F32)
+    dv = dv_own[...] + tail * back[:, HEAD_WIDTH:].astype(F32)
     dkn = rotate(dk, cos[...], sin[...], -1)
     k_hat, k_inv = rms_stats(kl[...])
     kraw = rms_back(k_hat, k_inv, gk[...], dkn).astype(BF)
@@ -383,40 +393,41 @@
     )(first_row, x3, up3, seg_ext, q_o, q_x, k, v, *weights, rows8)
 
 
-def attn_back(first, seg_ext, q, k, v, ga, lse, delta, ql, cos, sin, rows8):
-    own, part = q.shape
+def attn_back(seg_ext, q_o, q_x, k, v, ga_o, ga_x, lse, delta, ql_o, ql_x, cos, sin, rows8):
+    own, part = q_o.shape
     n = QB
     ext = k.shape[0]
-    acc = pl.BlockSpec((ext, HEAD_WIDTH), lambda i: (0, 0))
+    fixed = lambda shape: pl.BlockSpec(shape, lambda i: (0, 0))
+    stat = pl.BlockSpec((8, n), lambda i: (0, i))
     return pl.pallas_call(
-        functools.partial(attn_back_kernel, first),
+        attn_back_kernel,
         grid=(own // n,),
-        in_specs=[whole(seg_ext.shape), rows_of(n, part), whole(k.shape), whole(v.shape), rows_of(n, part),
-                  pl.BlockSpec((8, n), lambda i: (0, i)), pl.BlockSpec((8, n), lambda i: (0, i)), rows_of(n, part),
-                  rows_of(n, LANES), rows_of(n, LANES),
-                  whole(rows8.shape)],
-        out_specs=[rows_of(n, part), acc, acc, pl.BlockSpec((1, HEAD_WIDTH), lambda i: (0, 0))],
-        out_shape=[sds((own, part), BF), sds((ext, HEAD_WIDTH), F32), sds((ext, HEAD_WIDTH), F32),
-                   sds((1, HEAD_WIDTH), F32)],
+        in_specs=[whole(seg_ext.shape), rows_of(n, part), rows_of(n, part), whole(k.shape), whole(v.shape),
+                  rows_of(n, part), rows_of(n, part), stat, stat, rows_of(n, part), rows_of(n, part),
+                  rows_of(n, LANES), rows_of(n, LANES), whole(rows8.shape)],
+        out_specs=[rows_of(n, part), rows_of(n, part), fixed((own, HEAD_WIDTH)), fixed((own, HEAD_WIDTH)),
+                   fixed((BLOCK, 2 * HEAD_WIDTH)), fixed((1, HEAD_WIDTH))],
+        out_shape=[sds((own, part), BF), sds((own, part), BF), sds((own, HEAD_WIDTH), F32),
+                   sds((own, HEAD_WIDTH), F32), sds((BLOCK, 2 * HEAD_WIDTH), BF), sds((1, HEAD_WIDTH), F32)],
+        scratch_shapes=[pltpu.VMEM((ext, HEAD_WIDTH), F32), pltpu.VMEM((ext, HEAD_WIDTH), F32)],
         compiler_params=params(),
-        cost_estimate=cost(10),
+        cost_estimate=cost(20),
         name="attn_back",
-    )(seg_ext, q, k, v, ga, lse, delta, ql, cos, sin, rows8)
-
-
-def input_back(first_row, x3, gmid, dks, dvs, dk_r, dv_r, kl, cos, sin, rows8, qr_o, qr_x, wq_o, wq_x, wk, wv, nb):
+    )(seg_ext, q_o, q_x, k, v, ga_o, ga_x, lse, delta, ql_o, ql_x, cos, sin, rows8)
+
+
+def input_back(first_row, x3, gmid, dk, dv, back, kl, cos, sin, rows8, qr_o, qr_x, wq_o, wq_x, wk, wv, nb):
     depth = x3.shape[2]
     own, part = qr_o.shape
     n = BLOCK
     kern = lambda me, *refs: input_back_kernel(*refs)
-    later = pl.BlockSpec((n, HEAD_WIDTH), lambda i, *_: (i + 1, 0))
     return pl.pallas_call(
         kern,
         grid_spec=pltpu.PrefetchScalarGridSpec(
             num_scalar_prefetch=1,
             grid=(own // n,),
             in_specs=[pl.BlockSpec((1, n, depth), lambda i, me: (0, me[0] // n + i, 0)), rows_of(n, depth),
-                      later, later, later, later, whole((n, HEAD_WIDTH)), whole((n, HEAD_WIDTH)),
+                      rows_of(n, HEAD_WIDTH), rows_of(n, HEAD_WIDTH), whole(back.shape),
                       rows_of(n, HEAD_WIDTH), rows_of(n, LANES), rows_of(n, LANES),
                       whole(rows8.shape), rows_of(n, part), rows_of(n, part),
                       whole(wq_o.shape), whole(wq_x.shape), whole(wk.shape), whole(wv.shape), rows_of(n, depth)],
@@ -430,7 +441,7 @@
         cost_estimate=cost(8),
         compiler_params=params(),
         name="input_back",
-    )(first_row, x3, gmid, dks[0], dks[1], dvs[0], dvs[1], dk_r, dv_r, kl, cos, sin, rows8,
+    )(first_row, x3, gmid, dk, dv, back, kl, cos, sin, rows8,
       qr_o, qr_x, wq_o, wq_x, wk, wv, nb)
 
 
@@ -463,43 +474,48 @@
     return index
 
 
-def reduce_kernel(items, kv_order, n_gain, *refs):
+def reduce_kernel(items, kv_groups, n_bits, *refs):
     n_items = len(items)
+    kv_order = sum(kv_groups, ())
     refs = list(refs)
     take = lambda count: [refs.pop(0) for _ in range(count)]
-    ins = [take(2) for _ in items]
-    kv_in, g_block, g_in, gq_o, gq_x, g_k = take(6)
+    ins = [take(2 if given else 1) for _, given in items]
+    kv_in, g_block, g_in, g_q, g_k = take(5)
     outs = take(n_items)
-    kv_out, gain_out = take(2)
+    k_out, v_out, gain_out = take(3)
     recvs, curs = [], []
-    for order in items:
-        n = len(order)
-        recvs.append({s: refs.pop(0) for s in range(1, n)})
-        curs.append({s: refs.pop(0) for s in range(1, n)})
-    n_bits = len(kv_order)
+    for order, given in items:
+        first = 1 if given else 0
+        recvs.append({s: refs.pop(0) for s in range(first, n_bits)})
+        curs.append({s: refs.pop(0) for s in range(1, n_bits)})
     kv_core = refs.pop(0)
-    kv_recv = take(n_bits)
-    kv_cur = take(n_bits)
+    kv_recv = take(len(kv_groups))
+    kv_cur = take(len(kv_groups))
     kv_all = refs.pop(0)
-    gain_own = take(n_gain)
-    gain_got = take(n_gain)
+    gain_own = take(n_bits + 1)
+    gain_got = take(n_bits + 1)
     send_sems, recv_sems = take(2)
 
     me = lax.axis_index("dp")
     core = lax.axis_index("tensor")
-    partner = lambda b: me + (1 - 2 * bit_of(me, b)) * 2**b
+
+    def flipped(bits):
+        return me + sum((1 - 2 * bit_of(me, b)) * 2**b for b in bits)
+
+    def subsets(group):
+        return [tuple(b for k, b in enumerate(group) if m >> k & 1) for m in range(1, 2 ** len(group))]
+
+    peers = {(b,) for b in range(n_bits)} | {tuple(sorted(m)) for g in kv_groups for m in subsets(g)}
     barrier = pltpu.get_barrier_semaphore()
-    for b in range(n_bits):
-        pl.semaphore_signal(barrier, inc=1, device_id={"dp": partner(b)}, device_id_type=pl.DeviceIdType.MESH)
+    for bits in sorted(peers):
+        pl.semaphore_signal(barrier, inc=1, device_id={"dp": flipped(bits)}, device_id_type=pl.DeviceIdType.MESH)
     pl.semaphore_signal(barrier, inc=1, device_id={"tensor": 1 - core}, device_id_type=pl.DeviceIdType.MESH)
-    pl.semaphore_wait(barrier, n_bits + 1)
-
-    counter = [0]
+    pl.semaphore_wait(barrier, len(peers) + 1)
+
     sent = []
 
     def send(src, dst, device):
-        k = counter[0]
-        counter[0] += 1
+        k = len(sent)
         copy = pltpu.make_async_remote_copy(
             src_ref=src, dst_ref=dst, send_sem=send_sems.at[k], recv_sem=recv_sems.at[k],
             device_id=device, device_id_type=pl.DeviceIdType.MESH)
@@ -510,30 +526,35 @@
     flying = {}
 
     def start(n, s):
-        order = items[n]
-        half = 2 ** (len(order) - s - 1)
-        away = (1 - bit_of(me, order[s])) * half
-        flying[n] = send(curs[n][s].at[pl.ds(away, half)], recvs[n][s], {"dp": partner(order[s])})
+        order, _ = items[n]
+        half = 2 ** (n_bits - s - 1)
+        device = {"dp": flipped((order[s],))}
+        if s == 0:
+            flying[n] = [
+                send(ins[n][0].at[natural_index(me, j, ((order[0], True),), order[1:])], recvs[n][0].at[j], device)
+                for j in range(half)
+            ]
+        else:
+            away = (1 - bit_of(me, order[s])) * half
+            flying[n] = [send(curs[n][s].at[pl.ds(away, half)], recvs[n][s], device)]
 
     def finish(n, s):
-        order = items[n]
-        total = len(order)
-        half = 2 ** (total - s - 1)
-        if s:
-            flying.pop(n).wait_recv()
-        got = recvs[n][s] if s else ins[n][1]
+        order, given = items[n]
+        half = 2 ** (n_bits - s - 1)
+        for copy in flying.pop(n, ()):
+            copy.wait_recv()
+        outside = given and s == 0
+        got = ins[n][1] if outside else recvs[n][s]
         held = curs[n][s] if s else ins[n][0]
 
-        def keep_index(j):
-            if s == 0:
-                return natural_index(me, j, ((order[0], False),), order[1:])
-            return bit_of(me, order[s]) * half + j
-
         def total_at(j):
-            index = keep_index(j)
-            return held[index].astype(F32) + got[j if s else drop_bit(index, order[0])].astype(F32)
-
-        if s == total - 1:
+            if s:
+                index = bit_of(me, order[s]) * half + j
+            else:
+                index = natural_index(me, j, ((order[0], False),), order[1:])
+            return held[index].astype(F32) + got[drop_bit(index, order[0]) if outside else j].astype(F32)
+
+        if s == n_bits - 1:
             outs[n][...] = total_at(0)
             return
 
@@ -544,21 +565,22 @@
         lax.fori_loop(0, half, body, 0)
         start(n, s + 1)
 
-    kv_copy = send(kv_in.at[1 - core], kv_core, {"tensor": 1 - core})
+    kv_copies = [send(kv_in.at[1 - core], kv_core, {"tensor": 1 - core})]
+    for n in range(n_items):
+        if not items[n][1]:
+            start(n, 0)
     gain_own[0][...] = jnp.zeros_like(gain_own[0])
     gain_own[0][0:3, :] = g_block[0:3, :]
     gain_own[0][3:4, :] = g_in[...]
-    gain_own[0][4:5, :HEAD_WIDTH] = gq_o[...] + gq_x[...]
+    gain_own[0][4:5, :HEAD_WIDTH] = g_q[...]
     gain_own[0][5:6, :HEAD_WIDTH] = g_k[...]
 
     def gain_start(s):
-        device = {"tensor": 1 - core} if s == 0 else {"dp": partner(s - 1)}
+        device = {"tensor": 1 - core} if s == 0 else {"dp": flipped((s - 1,))}
         return send(gain_own[s], gain_got[s], device)
 
-    gain_copy = gain_start(0)
-    for n in range(n_items):
-        finish(n, 0)
-    kv_copy.wait_recv()
+    gain_copies = [gain_start(0)]
+    kv_copies[0].wait_recv()
 
     def kv_first(j, carry):
         index = natural_index(me, j, (), kv_order)
@@ -567,52 +589,89 @@
 
     lax.fori_loop(0, 2**n_bits, kv_first, 0)
 
-    def kv_start(s):
-        half = 2 ** (n_bits - s - 1)
-        away = (1 - bit_of(me, kv_order[s])) * half
-        return send(kv_cur[s].at[pl.ds(away, half)], kv_recv[s], {"dp": partner(kv_order[s])})
+    def rest_of(g):
+        return 2 ** (n_bits - sum(len(x) for x in kv_groups[: g + 1]))
+
+    def block_index(group, bits):
+        index = 0
+        for k, b in enumerate(group):
+            mine = bit_of(me, b)
+            index = index + (1 - mine if b in bits else mine) * 2 ** (len(group) - 1 - k)
+        return index
+
+    def kv_start(g):
+        rest = rest_of(g)
+        return [send(kv_cur[g].at[pl.ds(block_index(kv_groups[g], m) * rest, rest)], kv_recv[g].at[c],
+                     {"dp": flipped(m)}) for c, m in enumerate(subsets(kv_groups[g]))]
 
     spot = 0
     for k, b in enumerate(kv_order):
         spot = spot + bit_of(me, b) * 2 ** (n_bits - 1 - k)
-    kv_copy = kv_start(0)
-    for step in range(n_bits):
-        half = 2 ** (n_bits - step - 1)
-        kv_copy.wait_recv()
-        base = bit_of(me, kv_order[step]) * half
-        if step < n_bits - 1:
-
-            def kv_body(j, carry, step=step, base=base):
-                kv_cur[step + 1][j] = (kv_cur[step][base + j].astype(F32) + kv_recv[step][j].astype(F32)).astype(BF)
+    kv_copies = kv_start(0)
+    for n in range(n_items):
+        if items[n][1]:
+            finish(n, 0)
+    todo = [(n, s) for s in range(n_bits) for n in range(-1, n_items) if s or n < 0 or not items[n][1]]
+    todo = todo + [(-1, n_bits)]
+    todo.sort(key=lambda e: e[1] - (1 if e[0] >= 0 and items[e[0]][1] else 0))
+
+    def advance():
+        rank = lambda e: e[1] - (1 if e[0] >= 0 and items[e[0]][1] else 0)
+        now = rank(todo[0]) if todo else 0
+        while todo and rank(todo[0]) == now:
+            n, s = todo.pop(0)
+            if n >= 0:
+                finish(n, s)
+                continue
+            gain_copies[s].wait_recv()
+            if s == n_bits:
+                gain_out[...] = gain_own[s][...] + gain_got[s][...]
+            else:
+                gain_own[s + 1][...] = gain_own[s][...] + gain_got[s][...]
+                gain_copies.append(gain_start(s + 1))
+
+    for g in range(len(kv_groups)):
+        rest = rest_of(g)
+        for copy in kv_copies:
+            copy.wait_recv()
+        base = block_index(kv_groups[g], ()) * rest
+
+        def kv_total(j, g=g, base=base):
+            total = kv_cur[g][base + j].astype(F32)
+            for c in range(2 ** len(kv_groups[g]) - 1):
+                total = total + kv_recv[g][c, j].astype(F32)
+            return total.astype(BF)
+
+        if g < len(kv_groups) - 1:
+
+            def kv_body(j, carry, g=g, kv_total=kv_total):
+                kv_cur[g + 1][j] = kv_total(j)
                 return carry
 
-            lax.fori_loop(0, half, kv_body, 0)
-            kv_copy = kv_start(step + 1)
+            lax.fori_loop(0, rest, kv_body, 0)
+            kv_copies = kv_start(g + 1)
         else:
-            kv_all[core, spot] = (kv_cur[step][base].astype(F32) + kv_recv[step][0].astype(F32)).astype(BF)
-        gain_copy.wait_recv()
-        gain_own[step + 1][...] = gain_own[step][...] + gain_got[step][...]
-        gain_copy = gain_start(step + 1)
-        for n in range(n_items):
-            if step + 1 < len(items[n]):
-                finish(n, step + 1)
-    gain_copy.wait_recv()
-    gain_out[...] = gain_own[n_bits][...] + gain_got[n_bits][...]
-    for s in reversed(range(n_bits)):
-        size = 2 ** (n_bits - 1 - s)
+            kv_all[core, spot] = kv_total(0)
+        advance()
+    for g in reversed(range(len(kv_groups))):
+        size = rest_of(g)
         begin = 0
-        for k in range(s + 1):
-            begin = begin + bit_of(me, kv_order[k]) * 2 ** (n_bits - 1 - k)
+        for k, b in enumerate(sum(kv_groups[: g + 1], ())):
+            begin = begin + bit_of(me, b) * 2 ** (n_bits - 1 - k)
         region = kv_all.at[core, pl.ds(begin, size)]
-        copy = send(region, region, {"dp": partner(kv_order[s])})
-        copy.wait_recv()
+        copies = [send(region, region, {"dp": flipped(m)}) for m in subsets(kv_groups[g])]
+        advance()
+        for copy in copies:
+            copy.wait_recv()
     copy = send(kv_all.at[core], kv_all.at[core], {"tensor": 1 - core})
+    while todo:
+        advance()
     copy.wait_recv()
 
     def unpack(j, carry):
         index = natural_index(me, j, (), kv_order)
-        for t in range(2):
-            kv_out[t, index] = kv_all[t, j].astype(F32)
+        k_out[index] = kv_all[0, j].astype(F32)
+        v_out[index] = kv_all[1, j].astype(F32)
         return carry
 
     lax.fori_loop(0, 2**n_bits, unpack, 0)
@@ -620,8 +679,9 @@
         copy.wait_send()
 
 
-def reduce_all(n_dp, items, kv, kv_order, g_block, g_in, gq_o, gq_x, g_k):
+def reduce_all(n_dp, items, kv, kv_order, g_block, g_in, g_q, g_k):
     n_bits = len(kv_order)
+    groups = tuple(tuple(kv_order[k : k + 2]) for k in range(0, n_bits, 2))
     spec = []
     operands = []
     scratch = []
@@ -629,25 +689,28 @@
     copies = 0
     for value, got, order in items:
         n, c, width = value.shape
-        spec.append(tuple(order))
-        operands += [value, got]
+        given = got is not None
+        spec.append((tuple(order), given))
+        operands += [value, got] if given else [value]
         outs.append(sds((c, width), F32))
-        scratch += [pltpu.VMEM((2 ** (n_bits - s - 1), c, width), BF) for s in range(1, n_bits)]
+        first = 1 if given else 0
+        scratch += [pltpu.VMEM((2 ** (n_bits - s - 1), c, width), BF) for s in range(first, n_bits)]
         scratch += [pltpu.VMEM((2 ** (n_bits - s), c, width), BF) for s in range(1, n_bits)]
-        copies += n_bits - 1
+        copies += n_bits - 1 + (0 if given else n // 2)
     _, n, c, width = kv.shape
     scratch += [pltpu.VMEM((n, c, width), BF)]
-    scratch += [pltpu.VMEM((2 ** (n_bits - s - 1), c, width), BF) for s in range(n_bits)]
-    scratch += [pltpu.VMEM((2 ** (n_bits - s), c, width), BF) for s in range(n_bits)]
+    sizes = [2 ** (n_bits - sum(len(x) for x in groups[:g])) for g in range(len(groups) + 1)]
+    scratch += [pltpu.VMEM((2 ** len(groups[g]) - 1, sizes[g + 1], c, width), BF) for g in range(len(groups))]
+    scratch += [pltpu.VMEM((sizes[g], c, width), BF) for g in range(len(groups))]
     scratch += [pltpu.VMEM((2, n, c, width), BF)]
     scratch += [pltpu.VMEM((8, width), F32) for _ in range(2 * (n_bits + 1))]
-    copies += 2 * n_bits + 2 + n_bits + 1
+    copies += 2 + 2 * sum(2 ** len(g) - 1 for g in groups) + n_bits + 1
     scratch += [pltpu.SemaphoreType.DMA((copies,)), pltpu.SemaphoreType.DMA((copies,))]
-    outs += [sds(kv.shape, F32), sds((8, width), F32)]
+    outs += [sds(kv.shape[1:], F32), sds(kv.shape[1:], F32), sds((8, width), F32)]
     vmem = pl.BlockSpec(memory_space=pltpu.VMEM)
-    operands += [kv, g_block, g_in, gq_o, gq_x, g_k]
+    operands += [kv, g_block, g_in, g_q, g_k]
     return pl.pallas_call(
-        functools.partial(reduce_kernel, tuple(spec), tuple(kv_order), n_bits + 1),
+        functools.partial(reduce_kernel, tuple(spec), groups, n_bits),
         out_shape=outs,
         in_specs=[vmem] * len(operands),
         out_specs=[vmem] * len(outs),
@@ -655,46 +718,6 @@
         compiler_params=pltpu.CompilerParams(collective_id=0, has_side_effects=True, vmem_limit_bytes=VMEM_LIMIT),
         name="reduce_all",
     )(*operands)
-
-
-def fold_kernel(specs, me_ref, *refs):
-    me = me_ref[0]
-    n = len(specs)
-    for k, (rest, done) in enumerate(specs):
-        held, got = refs[2 * k], refs[2 * k + 1]
-        keep, away = refs[2 * n + 2 * k], refs[2 * n + 2 * k + 1]
-        half = 2 ** (len(rest) - 1)
-        mine = bit_of(me, rest[0]) * half
-        other = half - mine
-
-        def body(j, carry, held=held, got=got, keep=keep, away=away, rest=rest, done=done, mine=mine, other=other):
-            for base, dst in ((other, away), (mine, keep)):
-                at = base + j
-                index = at if done is None else natural_index(me, at, ((done, False),), rest)
-                other_index = at if done is None else drop_bit(index, done)
-                dst[j] = (held[index].astype(F32) + got[other_index].astype(F32)).astype(BF)
-            return carry
-
-        lax.fori_loop(0, half, body, 0)
-
-
-def fold(me, items):
-    specs, operands, outs = [], [], []
-    for held, got, rest, done in items:
-        specs.append((tuple(rest), done))
-        operands += [held, got]
-        shape = (got.shape[0] // 2,) + got.shape[1:]
-        outs += [sds(shape, BF), sds(shape, BF)]
-    vmem = pl.BlockSpec(memory_space=pltpu.VMEM)
-    res = pl.pallas_call(
-        functools.partial(fold_kernel, tuple(specs)),
-        out_shape=outs,
-        in_specs=[pl.BlockSpec(memory_space=pltpu.SMEM)] + [vmem] * len(operands),
-        out_specs=[vmem] * len(outs),
-        compiler_params=pltpu.CompilerParams(vmem_limit_bytes=VMEM_LIMIT),
-        name="fold",
-    )(me, *operands)
-    return list(zip(res[0::2], res[1::2]))
 
 
 def hop(value, b, n_dp):
@@ -756,41 +779,27 @@
         last = (away,)
         state.append((value, arrived))
 
-    def advance(state, stage):
-        folded = fold(spot, [(held, got, order[stage:], order[0] if stage == 1 else None)
-                             for (held, got), order in zip(state, orders)])
-        return [(keep, hop(away, order[stage], n_dp)) for (keep, away), order in zip(folded, orders)], folded
-
-    heads = q_o.shape[1] // HEAD_WIDTH
     ga_o = after(ga_o, *last)
-    qr_o, dk_o, dv_o, gq_o = attn_back(0, seg_ext, q_o, k, v, ga_o, lse, delta, ql_o, cos, sin, rows8)
-    state = [(after(value, dv_o), got) for value, got in state]
-    state, folded = advance(state, 1)
-    ga_x = after(ga_x, *(away for _, away in folded))
-    qr_x, dk_x, dv_x, gq_x = attn_back(heads, seg_ext, q_x, k, v, ga_x, lse, delta, ql_x, cos, sin, rows8)
-    state = [(after(value, qr_x), got) for value, got in state]
-    state, folded = advance(state, 2)
-    dk_x, dv_x, qr_x = lax.optimization_barrier((dk_x, dv_x, qr_x, *(away for _, away in folded)))[:3]
-    front = jnp.concatenate([dk_o[:BLOCK] + dk_x[:BLOCK], dv_o[:BLOCK] + dv_x[:BLOCK]], axis=1).astype(BF)
+    qr_o, qr_x, dk, dv, front, gain_q = attn_back(
+        seg_ext, q_o, q_x, k, v, ga_o, ga_x, lse, delta, ql_o, ql_x, cos, sin, rows8)
+    front, qr_x, *arrived = lax.optimization_barrier((front, qr_x, *(got for _, got in state)))
+    state = [(value, got) for (value, _), got in zip(state, arrived)]
     back = lax.ppermute(front, "tensor", [(t, t - 1) for t in range(1, n_tensor)])
     query_sent = tn(qr_x, nb).astype(BF)
     query_got = swap(query_sent, n_tensor)
-    query = chunks((tn(qr_o, nb) + query_got.astype(F32)).astype(BF))
-    query_hop, query_away = first_hop(query, turned[0], n_dp)
-    state = [(after(value, query_away), got) for value, got in state]
-    for stage in range(3, n_bits):
-        state, folded = advance(state, stage)
-    gmid = after(gmid, query_away, *(away for _, away in folded))
     grad_input, kv, gain_in, gain_k = input_back(
-        first_row, residual_in, gmid, (dk_o, dk_x), (dv_o, dv_x), back[:, :HEAD_WIDTH], back[:, HEAD_WIDTH:],
-        kl, cos, sin, rows8, qr_o, qr_x, w_query, wq_x, w_key, w_value, nb)
+        first_row, residual_in, after(gmid, query_sent), dk, dv, back, kl, cos, sin, rows8, qr_o, qr_x,
+        w_query, wq_x, w_key, w_value, nb)
+    query = chunks((tn(after(qr_o, gain_k), nb) + query_got.astype(F32)).astype(BF))
     kv = kv.reshape(2, n_dp, HEAD_WIDTH // n_dp, depth)
-    s_query, kv_sum, gain_sum = reduce_all(
-        n_dp, [(query, query_hop, turned)], kv, lead, gains, gain_in, gq_o, gq_x, gain_k)
-    s_down, s_gate, s_up, s_out = [keep[0].astype(F32) + got[0].astype(F32) for keep, got in state]
-    kv_sum = kv_sum.reshape(2, HEAD_WIDTH, depth)
+    items = [(value, got, order) for (value, got), order in zip(state, orders)]
+    *shares, k_sum, v_sum, gain_sum = reduce_all(
+        n_dp, items + [(query, None, plain)], kv, plain, gains, gain_in, gain_q, gain_k)
+    s_down, s_gate, s_up, s_out, s_query = shares
+    k_sum = k_sum.reshape(HEAD_WIDTH, depth)
+    v_sum = v_sum.reshape(HEAD_WIDTH, depth)
     return (
-        output[None], grad_input[None], gain_sum[3], s_query.T, kv_sum[0].T, kv_sum[1].T,
+        output[None], grad_input[None], gain_sum[3], s_query.T, k_sum.T, v_sum.T,
         gain_sum[4, :HEAD_WIDTH], gain_sum[5, :HEAD_WIDTH],
         s_out.T, gain_sum[2], gain_sum[1], s_gate.T, s_up.T, s_down.T, gain_sum[0],
     )

time: 228 us -> 201 us (0.88)
  starting transfers between devices: 26.3 us -> 11.9 us
  Pallas kernels: 148 us -> 142 us
  waiting for transfers between devices: 5.81 us -> 0.04 us
  other arithmetic: 5.91 us -> 1.4 us
  matrix products: 18.4 us -> 22.1 us
    ppermute x17 -> x4, starting transfers between devices: 19.5 us -> 5.14 us  [hop(): return lax.ppermute(value, 'dp', [(i, i ^ 2 ** b) for i in range(n_dp)])]
    pallas_call x6 -> x2, Pallas kernels: 75.4 us -> 69.3 us  [the longest x1 51.3 us: reduce_all(): pl.pallas_call(functools.partial(reduce_kernel, tuple(spec), groups, n_bi...]
    ppermute x17 -> x4, waiting for transfers between devices: 5.78 us -> 0.01 us  [hop(): return lax.ppermute(value, 'dp', [(i, i ^ 2 ** b) for i in range(n_dp)])]
    dot_general x10, matrix products: 18.4 us -> 22.1 us  [tn(): lax.dot_general(a, b, (((0,), (0,)), ((), ())), preferred_element_type=F32)]
    reshape x0 -> x2, local copies, waits for them, and re-layouts: none -> 3.28 us  [the longest x1 2.21 us: on_device(): k_sum = k_sum.reshape(HEAD_WIDTH, depth)]
    transpose x4 -> x0, other arithmetic: 2.71 us -> none  [on_device(): return (output[None], grad_input[None], gain_sum[3], s_query.T, kv_sum[0]...]
    unnamed x79 -> x59, local copies, waits for them, and re-layouts: 8.6 us -> 6.56 us
  transfers between devices with their start and end apart: 28 -> 15, of which waited for: 2 -> 0; matrix products, arithmetic and copies ran while one was open for 12% -> 13% of each run, Pallas kernels for 21% -> 21%
where the time goes in v3:
time: 201 us; the launch traced here: 200 us
  Pallas kernels  142 us (71%)
  matrix products  22.1 us (11%)
  local copies, waits for them, and re-layouts  21.8 us (11%)
  starting transfers between devices  11.9 us (6%)
    pallas_call x1, Pallas kernels, reduce_all(): pl.pallas_call(functools.partial(reduce_kernel, tuple(spec), groups, n_bi...  51.3 us
    pallas_call x1, Pallas kernels, block_pass(): pl.pallas_call(kern, grid_spec=pltpu.PrefetchScalarGridSpec(num_scalar_pr...  49.1 us
    dot_general x10, matrix products, tn(): lax.dot_general(a, b, (((0,), (0,)), ((), ())), preferred_element_type=F32)  22.1 us
    pallas_call x1, Pallas kernels, attn_back(): pl.pallas_call(attn_back_kernel, grid=(own // n,), in_specs=[whole(seg_ex...  18 us
    pallas_call x1, Pallas kernels, input_back(): pl.pallas_call(kern, grid_spec=pltpu.PrefetchScalarGridSpec(num_scalar_pr...  12.5 us
    pallas_call x1, Pallas kernels, project(): pl.pallas_call(project_kernel, grid_spec=pltpu.PrefetchScalarGridSpec(num...  11 us
    unnamed x59, local copies, waits for them, and re-layouts  6.56 us
    ppermute x4, starting transfers between devices, hop(): return lax.ppermute(value, 'dp', [(i, i ^ 2 ** b) for i in range(n_dp)])  5.14 us
  transfers between devices with their start and end apart: 15, of which 0 were waited for; matrix products, arithmetic and copies ran while one was open for 13% of the time, Pallas kernels for 21%

profile of v3, /device:TPU:1, one launch (start us, length us, event | category | flops | bytes accessed | tf_op | source)
XLA Modules:
  0.0 200.4 jit_solution(6731573580021343562)
XLA Ops:
  0.6 0.1 collective-permute-start.2
  0.7 0.5 collective-permute-start.3
  1.2 0.1 collective-permute-start.4
  1.3 0.4 collective-permute-start
  1.7 0.1 collective-permute-start.1
  1.8 0.8 pad_dynamic-slice_fusion
  2.6 0.6 broadcast_in_dim.14.seg.refs_2_
  3.2 0.7 pad.8
  3.9 0.7 pad.9
  4.6 0.7 stack.24
  5.2 0.7 stack.25
  5.9 0.7 stack.26
  6.6 0.7 stack.27
  7.3 0.6 stack.31.rows8.refs_15_.refs_8_
  8.0 1.4 convert_reduce_fusion
  9.4 0.8 copy-done.16
  10.2 11.0 %project.1 = (bf16[1024,512]{1,0:T(8,128)(2,1)}, bf16[1024,512]{1,0:T(8,128)(2,1)}, f32[1024,512]{1,0:T(8,128)}, f32[1024,512]{1,0:T(8,128)}, bf16[1536,256]{1,0...) custom-call(s32[1]{0:T(128)} %bitcast.me, ...), custom_call_target="tpu_custom_call" | custom-call | flops 6000000000 | bytes 6000000 | tf_op jit(solution)/shard_map/project/pallas_call | solution.py:332
  21.2 0.0 collective-permute-done.1.refs_8_
  21.3 0.0 collective-permute-done.3.refs_12_
  21.3 0.0 collective-permute-done.4.refs_14_
  21.3 1.0 copy-done.14
  22.3 0.4 copy-done.15
  22.7 49.1 %block.1 = (f32[1024,640]{1,0:T(8,128)}, f32[1024,640]{1,0:T(8,128)}, bf16[1024,512]{1,0:T(8,128)(2,1)}, bf16[1024,512]{1,0:T(8,128)(2,1)}, bf16[1024,512]{1,0:T...) custom-call(s32[1]{0:T(128)} %bitcast.me, ...), custom_call_target="tpu_custom_call" | custom-call | flops 40000000000 | bytes 40000000 | tf_op jit(solution)/shard_map/block/pallas_call | solution.py:370
  71.9 3.5 %convolution_convert_fusion.2 = bf16[640,1024]{1,0:T(8,128)(2,1)S(1)} fusion(bf16[1024,640]{1,0:T(8,128)(2,1)} %get-tuple-element.88, bf16[1024,1024]{1,0:T(8,128)(2,1)} %get-tuple-element.93), kind=kOutput, calls=%fused_computation.5 | convolution fusion | flops 1342832640 | bytes 4718592 | tf_op jit(solution)/shard_map/dot_general | solution.py:35
  75.4 0.5 collective-permute-start.5
  75.9 3.9 %convolution_convert_fusion.1 = bf16[1024,640]{1,0:T(8,128)(2,1)S(1)} fusion(bf16[1024,1024]{1,0:T(8,128)(2,1)} %get-tuple-element.94, bf16[1024,640]{1,0:T(8,128)(2,1)} %get-tuple-element.95), kind=kOutput, calls=%fused_computation.4 | convolution fusion | flops 1342832640 | bytes 4718592 | tf_op jit(solution)/shard_map/dot_general | solution.py:35
  79.9 0.1 collective-permute-start.6
  80.0 1.9 convolution_convert_fusion
  81.9 0.5 collective-permute-start.7
  82.4 0.9 convolution_convert_fusion.4
  83.3 0.1 collective-permute-start.8
  83.4 0.0 collective-permute-done.5
  83.4 0.6 copy-done.25
  84.0 0.4 copy-done.26
  84.4 1.6 add_convert_fusion.2
  85.9 1.0 dynamic-slice_bitcast_fusion
  86.9 2.3 %collective-permute-start.9 = (bf16[8,40,1024]{2,1,0:T(8,128)(2,1)}, bf16[8,40,1024]{2,1,0:T(8,128)(2,1)S(1)}, u32[]{:S(2)}, u32[]{:S(2)}) collective-permute-start(bf16[8,40,1024]{2,1,0:T(8,128)(2,1)} %dynamic-slice_bitcast_fusion), channel_id=1, source_target_pairs={{0,2},{2,0},{4,6},{6,4},{8,10},{10,8},{12,14},{14,12},{16,18},{18,... | collective-permute-start | bytes 1966088 | tf_op jit(solution)/shard_map/ppermute | solution.py:724
  89.2 0.0 collective-permute-done.6
  89.2 1.9 add_convert_fusion.1
  91.1 1.0 constant_dynamic-slice_fusion.1
  92.1 1.2 collective-permute-start.10
  93.4 1.9 add_convert_fusion
  95.3 1.0 constant_dynamic-slice_fusion
  96.3 1.3 collective-permute-start.11
  97.6 0.0 collective-permute-done.8
  97.6 0.9 fusion
  98.5 0.3 collective-permute-start.12
  98.8 18.0 %attn_back.1 = (bf16[1024,512]{1,0:T(8,128)(2,1)}, bf16[1024,512]{1,0:T(8,128)(2,1)}, f32[1024,256]{1,0:T(8,128)}, f32[1024,256]{1,0:T(8,128)}, bf16[512,512]{1,0:T(8,128)(2,1)}, /*index=5*/f32[1,256]{1,0:T(1,128)}) custom-call(s32[1,1536]{1,0:T(1,128)} %broadcast_in_dim.14.seg.refs_2_, bf16[1024,512]{1,0:T(8,128)(2,1)} %get-tuple-element.77.refs_3_.q_o, ...), custom_call_target="tpu_custom_call" | custom-call | flops 20000000000 | bytes 20000000 | tf_op jit(solution)/shard_map/attn_back/pallas_call | solution.py:402
  116.8 0.0 collective-permute-done.12.refs_7_
  116.9 4.3 %collective-permute-start.13 = (bf16[512,512]{1,0:T(8,128)(2,1)}, bf16[512,512]{1,0:T(8,128)(2,1)}, u32[]{:S(2)}, u32[]{:S(2)}) collective-permute-start(bf16[512,512]{1,0:T(8,128)(2,1)} %get-tuple-element.117), channel_id=1, source_target_pairs={{1,0},{3,2},{5,4},{7,6},{9,8},{11,10},{13,12},{15,14},{17,16},{19,... | collective-permute-start | bytes 1572872 | tf_op jit(solution)/shard_map/ppermute | solution.py:787
  121.2 2.7 %convolution_convert_fusion.3 = bf16[512,640]{1,0:T(8,128)(2,1)S(1)} fusion(bf16[1024,512]{1,0:T(8,128)(2,1)} %get-tuple-element.112.refs_10_, bf16[1024,640]{1,0:T(8,128)(2,1)} %get-tuple-element.113.refs_15_), kind=kOutput, calls=%fused_computation.10 | convolution fusion | flops 671416320 | bytes 3014656 | tf_op jit(solution)/shard_map/dot_general | solution.py:35
  123.9 0.1 collective-permute-start.14
  124.0 12.5 %input_back.1 = (f32[1024,640]{1,0:T(8,128)}, bf16[512,640]{1,0:T(8,128)(2,1)}, f32[1,640]{1,0:T(1,128)}, f32[1,256]{1,0:T(1,128)}) custom-call(s32[1]{0:T(128)} %bitcast.me, f32[1,2048,640]{2,1,0:T(8,128)} %refs_0_.3, f32[1024,640]{1,0:T(8,128)} %get-tuple-element.114.refs_1_, f32[1024,256]{1,0:T(8,128)} %get-tuple-element.115.refs_2_, ...), custom_call_target="tpu_custom_call" | custom-call | flops 8000000000 | bytes 8000000 | tf_op jit(solution)/shard_map/input_back/pallas_call | solution.py:424
  136.5 3.1 %fusion.1 = bf16[512,640]{1,0:T(8,128)(2,1)} fusion(bf16[1024,512]{1,0:T(8,128)(2,1)} %get-tuple-element.126.refs_9_, bf16[1024,640]{1,0:T(8,128)(2,1)S(1)} %copy-done.17, bf16[512,640]{1,0:T(8,128)(2,1)S(1)} %collective-permute-done.14), kind=kOutput, calls=%fused_computation.9 | convolution fusion | flops 672071680 | bytes 3670016 | tf_op jit(solution)/shard_map/dot_general | solution.py:35
  139.6 51.3 %reduce_all.1 = (f32[40,1024]{1,0:T(8,128)}, f32[64,640]{1,0:T(8,128)}, f32[64,640]{1,0:T(8,128)}, f32[40,512]{1,0:T(8,128)}, f32[32,640]{1,0:T(8,128)}, /*index...) custom-call(bf16[16,40,1024]{2,1,0:T(8,128)(2,1)} %bitcast.61, bf16[8,40,1024]{2,1,0:T(8,128)(2,1)} %copy-done.4, ...), custom_call_target="tpu_custom_call" | custom-call | tf_op jit(solution)/shard_map/reduce_all/pallas_call | solution.py:712
  191.0 1.5 slice_reduce_fusion
  192.5 1.3 fusion.2
  193.8 2.2 %copy.42 = f32[256,640]{0,1:T(8,128)} copy(f32[256,640]{1,0:T(8,128)} %bitcast.73) | data formatting | bytes 1310720 | tf_op jit(solution)/shard_map/reshape | solution.py:799
  196.0 1.1 copy.43
  197.1 0.6 copy.53
  197.7 0.6 copy.54
  198.4 0.7 copy.55
  199.0 0.7 copy.56
  199.7 0.7 copy.57
  (61 shorter events, 0.2 us)
Async XLA Ops:
  0.6 20.6 %collective-permute-start.2 = (bf16[640,1024]{1,0:T(8,128)(2,1)}, bf16[640,1024]{1,0:T(8,128)(2,1)S(1)}, u32[]{:S(2)}, u32[]{:S(2)}) collective-permute-start(bf16[640,1024]{1,0:T(8,128)(2,1)} %refs_9_.1), channel_id=1, source_target_pairs={{0,1},{1,0},{2,3},{3,2},{4,5},{5,4},{6,7},{7,6},{8,9},{9,8},{10,11... | collective-permute-start | bytes 3932168 | tf_op jit(solution)/shard_map/ppermute | solution.py:449
  0.7 20.5 %collective-permute-start.3 = (bf16[640,1024]{1,0:T(8,128)(2,1)}, bf16[640,1024]{1,0:T(8,128)(2,1)S(1)}, u32[]{:S(2)}, u32[]{:S(2)}) collective-permute-start(bf16[640,1024]{1,0:T(8,128)(2,1)} %refs_11_.2), channel_id=1, source_target_pairs={{0,1},{1,0},{2,3},{3,2},{4,5},{5,4},{6,7},{7,6},{8,9},{9,8},{10,11... | collective-permute-start | bytes 3932168 | tf_op jit(solution)/shard_map/ppermute | solution.py:449
  1.2 20.1 %collective-permute-start.4 = (bf16[1024,640]{1,0:T(8,128)(2,1)}, bf16[1024,640]{1,0:T(8,128)(2,1)}, u32[]{:S(2)}, u32[]{:S(2)}) collective-permute-start(bf16[1024,640]{1,0:T(8,128)(2,1)} %refs_13_.2), channel_id=1, source_target_pairs={{0,1},{1,0},{2,3},{3,2},{4,5},{5,4},{6,7},{7,6},{8,9},{9,8},{10,11... | collective-permute-start | bytes 3932168 | tf_op jit(solution)/shard_map/ppermute | solution.py:449
  1.3 8.1 %collective-permute-start = (bf16[640,512]{1,0:T(8,128)(2,1)}, bf16[640,512]{1,0:T(8,128)(2,1)S(1)}, u32[]{:S(2)}, u32[]{:S(2)}) collective-permute-start(bf16[640,512]{1,0:T(8,128)(2,1)} %refs_11_.3), channel_id=1, source_target_pairs={{0,1},{1,0},{2,3},{3,2},{4,5},{5,4},{6,7},{7,6},{8,9},{9,8},{10,11... | collective-permute-start | bytes 1966088 | tf_op jit(solution)/shard_map/ppermute | solution.py:449
  1.7 19.5 %collective-permute-start.1 = (bf16[512,640]{1,0:T(8,128)(2,1)}, bf16[512,640]{1,0:T(8,128)(2,1)}, u32[]{:S(2)}, u32[]{:S(2)}) collective-permute-start(bf16[512,640]{1,0:T(8,128)(2,1)} %refs_7_.1), channel_id=1, source_target_pairs={{0,1},{1,0},{2,3},{3,2},{4,5},{5,4},{6,7},{7,6},{8,9},{9,8},{10,11... | collective-permute-start | bytes 1966088 | tf_op jit(solution)/shard_map/ppermute | solution.py:449
  9.4 0.8 copy-start.16
  21.3 1.1 copy-start.14
  21.3 1.5 copy-start.15
  75.4 8.0 %collective-permute-start.5 = (bf16[640,1024]{1,0:T(8,128)(2,1)S(1)}, bf16[640,1024]{1,0:T(8,128)(2,1)S(1)}, u32[]{:S(2)}, u32[]{:S(2)}) collective-permute-start(bf16[640,1024]{1,0:T(8,128)(2,1)S(1)} %convolution_convert_fusion.2), channel_id=1, source_target_pairs={{0,1},{1,0},{2,3},{3,2},{4,5},{5,4},{6,7},{7,6},{8,9},{9,8},{10,11... | collective-permute-start | bytes 3932168 | tf_op jit(solution)/shard_map/ppermute | solution.py:449
  75.9 4.1 %copy-start.23 = (bf16[1024,1024]{1,0:T(8,128)(2,1)S(1)}, bf16[1024,1024]{1,0:T(8,128)(2,1)}, u32[]{:S(2)}) copy-start(bf16[1024,1024]{1,0:T(8,128)(2,1)} %get-tuple-element.96) | copy-start | bytes 6291460
  75.9 4.1 %copy-start.24 = (bf16[1024,640]{1,0:T(8,128)(2,1)S(1)}, bf16[1024,640]{1,0:T(8,128)(2,1)}, u32[]{:S(2)}) copy-start(bf16[1024,640]{1,0:T(8,128)(2,1)} %get-tuple-element.95) | copy-start | bytes 3932164
  79.9 9.3 %collective-permute-start.6 = (bf16[1024,640]{1,0:T(8,128)(2,1)S(1)}, bf16[1024,640]{1,0:T(8,128)(2,1)S(1)}, u32[]{:S(2)}, u32[]{:S(2)}) collective-permute-start(bf16[1024,640]{1,0:T(8,128)(2,1)S(1)} %convolution_convert_fusion.1), channel_id=1, source_target_pairs={{0,1},{1,0},{2,3},{3,2},{4,5},{5,4},{6,7},{7,6},{8,9},{9,8},{10,11... | collective-permute-start | bytes 3932168 | tf_op jit(solution)/shard_map/ppermute | solution.py:449
  80.0 2.4 %copy-start.18 = (bf16[1024,640]{1,0:T(8,128)(2,1)S(1)}, bf16[1024,640]{1,0:T(8,128)(2,1)}, u32[]{:S(2)}) copy-start(bf16[1024,640]{1,0:T(8,128)(2,1)} %get-tuple-element.84) | copy-start | bytes 3932164
  80.0 2.4 %copy-start.20 = (bf16[1024,512]{1,0:T(8,128)(2,1)S(1)}, bf16[1024,512]{1,0:T(8,128)(2,1)}, u32[]{:S(2)}) copy-start(bf16[1024,512]{1,0:T(8,128)(2,1)} %get-tuple-element.97) | copy-start | bytes 3145732
  81.9 11.5 %collective-permute-start.7 = (bf16[1024,640]{1,0:T(8,128)(2,1)S(1)}, bf16[1024,640]{1,0:T(8,128)(2,1)S(1)}, u32[]{:S(2)}, u32[]{:S(2)}) collective-permute-start(bf16[1024,640]{1,0:T(8,128)(2,1)S(1)} %convolution_convert_fusion), channel_id=1, source_target_pairs={{0,1},{1,0},{2,3},{3,2},{4,5},{5,4},{6,7},{7,6},{8,9},{9,8},{10,11... | collective-permute-start | bytes 3932168 | tf_op jit(solution)/shard_map/ppermute | solution.py:449
  82.4 1.6 copy-start.25
  82.4 1.9 copy-start.26
  83.3 14.3 %collective-permute-start.8 = (bf16[640,512]{1,0:T(8,128)(2,1)S(1)}, bf16[640,512]{1,0:T(8,128)(2,1)S(1)}, u32[]{:S(2)}, u32[]{:S(2)}) collective-permute-start(bf16[640,512]{1,0:T(8,128)(2,1)S(1)} %convolution_convert_fusion.4), channel_id=1, source_target_pairs={{0,1},{1,0},{2,3},{3,2},{4,5},{5,4},{6,7},{7,6},{8,9},{9,8},{10,11... | collective-permute-start | bytes 1966088 | tf_op jit(solution)/shard_map/ppermute | solution.py:449
  84.4 4.8 %copy-start.22 = (bf16[1024,1024]{1,0:T(8,128)(2,1)S(1)}, bf16[1024,1024]{1,0:T(8,128)(2,1)}, u32[]{:S(2)}) copy-start(bf16[1024,1024]{1,0:T(8,128)(2,1)} %get-tuple-element.99) | copy-start | bytes 6291460
  85.9 5.1 %copy-start = (bf16[640,1024]{1,0:T(8,128)(2,1)}, bf16[640,1024]{1,0:T(8,128)(2,1)S(1)}, u32[]{:S(2)}) copy-start(bf16[640,1024]{1,0:T(8,128)(2,1)S(1)} %add_convert_fusion.2) | copy-start | bytes 3932164
  86.9 30.0 %collective-permute-start.9 = (bf16[8,40,1024]{2,1,0:T(8,128)(2,1)}, bf16[8,40,1024]{2,1,0:T(8,128)(2,1)S(1)}, u32[]{:S(2)}, u32[]{:S(2)}) collective-permute-start(bf16[8,40,1024]{2,1,0:T(8,128)(2,1)} %dynamic-slice_bitcast_fusion), channel_id=1, source_target_pairs={{0,2},{2,0},{4,6},{6,4},{8,10},{10,8},{12,14},{14,12},{16,18},{18,... | collective-permute-start | bytes 1966088 | tf_op jit(solution)/shard_map/ppermute | solution.py:724
  89.2 4.2 %copy-start.21 = (bf16[1024,1024]{1,0:T(8,128)(2,1)S(1)}, bf16[1024,1024]{1,0:T(8,128)(2,1)}, u32[]{:S(2)}) copy-start(bf16[1024,1024]{1,0:T(8,128)(2,1)} %get-tuple-element.100) | copy-start | bytes 6291460
  91.1 4.2 %copy-start.1 = (bf16[1024,640]{1,0:T(8,128)(2,1)}, bf16[1024,640]{1,0:T(8,128)(2,1)S(1)}, u32[]{:S(2)}) copy-start(bf16[1024,640]{1,0:T(8,128)(2,1)S(1)} %add_convert_fusion.1) | copy-start | bytes 3932164
  92.1 24.7 %collective-permute-start.10 = (bf16[8,64,640]{2,1,0:T(8,128)(2,1)}, bf16[8,64,640]{2,1,0:T(8,128)(2,1)S(1)}, u32[]{:S(2)}, u32[]{:S(2)}) collective-permute-start(bf16[8,64,640]{2,1,0:T(8,128)(2,1)} %bitcast.7), channel_id=1, source_target_pairs={{0,4},{2,6},{4,0},{6,2},{8,12},{10,14},{12,8},{14,10},{16,20},{18,... | collective-permute-start | bytes 1966088 | tf_op jit(solution)/shard_map/ppermute | solution.py:724
  95.3 3.2 %copy-start.2 = (bf16[1024,640]{1,0:T(8,128)(2,1)}, bf16[1024,640]{1,0:T(8,128)(2,1)S(1)}, u32[]{:S(2)}) copy-start(bf16[1024,640]{1,0:T(8,128)(2,1)S(1)} %add_convert_fusion) | copy-start | bytes 3932164
  95.3 2.3 %copy-start.19 = (bf16[1024,512]{1,0:T(8,128)(2,1)S(1)}, bf16[1024,512]{1,0:T(8,128)(2,1)}, u32[]{:S(2)}) copy-start(bf16[1024,512]{1,0:T(8,128)(2,1)} %get-tuple-element.101) | copy-start | bytes 3145732
  96.3 20.6 %collective-permute-start.11 = (bf16[8,64,640]{2,1,0:T(8,128)(2,1)}, bf16[8,64,640]{2,1,0:T(8,128)(2,1)S(1)}, u32[]{:S(2)}, u32[]{:S(2)}) collective-permute-start(bf16[8,64,640]{2,1,0:T(8,128)(2,1)} %bitcast.9), channel_id=1, source_target_pairs={{0,8},{2,10},{4,12},{6,14},{8,0},{10,2},{12,4},{14,6},{16,24},{18,... | collective-permute-start | bytes 1966088 | tf_op jit(solution)/shard_map/ppermute | solution.py:724
  98.5 18.4 %copy-start.3 = (bf16[640,512]{1,0:T(8,128)(2,1)}, bf16[640,512]{1,0:T(8,128)(2,1)S(1)}, u32[]{:S(2)}) copy-start(bf16[640,512]{1,0:T(8,128)(2,1)S(1)} %fusion) | copy-start | bytes 1966084
  98.5 18.3 %collective-permute-start.12 = (bf16[8,40,512]{2,1,0:T(8,128)(2,1)S(1)}, bf16[8,40,512]{2,1,0:T(8,128)(2,1)S(1)}, u32[]{:S(2)}, u32[]{:S(2)}) collective-permute-start(bf16[8,40,512]{2,1,0:T(8,128)(2,1)S(1)} %dynamic-slice_bitcast_fusion.1), channel_id=1, source_target_pairs={{0,2},{2,0},{4,6},{6,4},{8,10},{10,8},{12,14},{14,12},{16,18},{18,... | collective-permute-start | bytes 983048 | tf_op jit(solution)/shard_map/ppermute | solution.py:724
  116.8 7.0 %copy-start.8 = (bf16[8,40,512]{2,1,0:T(8,128)(2,1)}, bf16[8,40,512]{2,1,0:T(8,128)(2,1)S(1)}, u32[]{:S(2)}) copy-start(bf16[8,40,512]{2,1,0:T(8,128)(2,1)S(1)} %collective-permute-done.12.refs_7_) | copy-start | bytes 983044
  116.8 7.0 %copy-start.6 = (bf16[8,64,640]{2,1,0:T(8,128)(2,1)}, bf16[8,64,640]{2,1,0:T(8,128)(2,1)S(1)}, u32[]{:S(2)}) copy-start(bf16[8,64,640]{2,1,0:T(8,128)(2,1)S(1)} %collective-permute-done.11.refs_5_) | copy-start | bytes 1966084
  116.9 7.0 %copy-start.5 = (bf16[8,64,640]{2,1,0:T(8,128)(2,1)}, bf16[8,64,640]{2,1,0:T(8,128)(2,1)S(1)}, u32[]{:S(2)}) copy-start(bf16[8,64,640]{2,1,0:T(8,128)(2,1)S(1)} %collective-permute-done.10.refs_3_) | copy-start | bytes 1966084
  116.9 7.0 %copy-start.4 = (bf16[8,40,1024]{2,1,0:T(8,128)(2,1)}, bf16[8,40,1024]{2,1,0:T(8,128)(2,1)S(1)}, u32[]{:S(2)}) copy-start(bf16[8,40,1024]{2,1,0:T(8,128)(2,1)S(1)} %collective-permute-done.9.refs_1_) | copy-start | bytes 1966084
  116.9 7.0 %collective-permute-start.13 = (bf16[512,512]{1,0:T(8,128)(2,1)}, bf16[512,512]{1,0:T(8,128)(2,1)}, u32[]{:S(2)}, u32[]{:S(2)}) collective-permute-start(bf16[512,512]{1,0:T(8,128)(2,1)} %get-tuple-element.117), channel_id=1, source_target_pairs={{1,0},{3,2},{5,4},{7,6},{9,8},{11,10},{13,12},{15,14},{17,16},{19,... | collective-permute-start | bytes 1572872 | tf_op jit(solution)/shard_map/ppermute | solution.py:787
  123.9 12.7 %collective-permute-start.14 = (bf16[512,640]{1,0:T(8,128)(2,1)S(1)}, bf16[512,640]{1,0:T(8,128)(2,1)S(1)}, u32[]{:S(2)}, u32[]{:S(2)}) collective-permute-start(bf16[512,640]{1,0:T(8,128)(2,1)S(1)} %convolution_convert_fusion.3), channel_id=1, source_target_pairs={{0,1},{1,0},{2,3},{3,2},{4,5},{5,4},{6,7},{7,6},{8,9},{9,8},{10,11... | collective-permute-start | bytes 1966088 | tf_op jit(solution)/shard_map/ppermute | solution.py:449
  123.9 12.6 %copy-start.17 = (bf16[1024,640]{1,0:T(8,128)(2,1)S(1)}, bf16[1024,640]{1,0:T(8,128)(2,1)}, u32[]{:S(2)}) copy-start(bf16[1024,640]{1,0:T(8,128)(2,1)} %get-tuple-element.113.refs_15_) | copy-start | bytes 3932164
  190.9 5.1 %copy-start.7 = (f32[16,16,640]{2,1,0:T(8,128)S(1)}, f32[16,16,640]{2,1,0:T(8,128)}, u32[]{:S(2)}) copy-start(f32[16,16,640]{2,1,0:T(8,128)} %get-tuple-element.134) | copy-start | bytes 1966084
  193.8 3.3 %copy-start.13 = (f32[32,640]{1,0:T(8,128)S(1)}, f32[32,640]{1,0:T(8,128)}, u32[]{:S(2)}) copy-start(f32[32,640]{1,0:T(8,128)} %get-tuple-element.132) | copy-start | bytes 245764
  193.8 3.9 %copy-start.12 = (f32[40,512]{1,0:T(8,128)S(1)}, f32[40,512]{1,0:T(8,128)}, u32[]{:S(2)}) copy-start(f32[40,512]{1,0:T(8,128)} %get-tuple-element.135) | copy-start | bytes 245764
  193.8 4.6 %copy-start.11 = (f32[64,640]{1,0:T(8,128)S(1)}, f32[64,640]{1,0:T(8,128)}, u32[]{:S(2)}) copy-start(f32[64,640]{1,0:T(8,128)} %get-tuple-element.136) | copy-start | bytes 491524
  196.0 3.0 %copy-start.10 = (f32[64,640]{1,0:T(8,128)S(1)}, f32[64,640]{1,0:T(8,128)}, u32[]{:S(2)}) copy-start(f32[64,640]{1,0:T(8,128)} %get-tuple-element.137) | copy-start | bytes 491524
  196.0 3.7 %copy-start.9 = (f32[40,1024]{1,0:T(8,128)S(1)}, f32[40,1024]{1,0:T(8,128)}, u32[]{:S(2)}) copy-start(f32[40,1024]{1,0:T(8,128)} %get-tuple-element.138) | copy-start | bytes 491524

commit v4 on v3

--- a/solution.py
+++ b/solution.py
@@ -267,39 +267,6 @@
         dv_out[...] = dv[BLOCK:, :]
 
 
-def input_back_kernel(x, gmid, dk_own, dv_own, back, kl, cos, sin, rows8,
-                      qr_o, qr_x, wq_o, wq_x, wk, wv, nb, gin_out, kv_out, gains, gain_k, kv_acc):
-    g_in, gk = gain_refs(rows8, 0, 5)
-    i = pl.program_id(0)
-    last = pl.num_programs(0) - 1
-    tail = (i == last).astype(F32)
-    dk = dk_own[...] + tail * back[:, :HEAD_WIDTH].astype(F32)
-    dv = dv_own[...] + tail * back[:, HEAD_WIDTH:].astype(F32)
-    dkn = rotate(dk, cos[...], sin[...], -1)
-    k_hat, k_inv = rms_stats(kl[...])
-    kraw = rms_back(k_hat, k_inv, gk[...], dkn).astype(BF)
-    vraw = dv.astype(BF)
-    kv_w = tn(jnp.concatenate([kraw, vraw], axis=1), nb[...])
-
-    @pl.when(i == 0)
-    def _():
-        kv_acc[...] = jnp.zeros_like(kv_acc)
-
-    kv_acc[...] += kv_w
-    kv_out[...] = kv_acc[...].astype(BF)
-    gn = nt(kraw, wk[...]) + nt(vraw, wv[...]) + nt(qr_o[...], wq_o[...]) + nt(qr_x[...], wq_x[...])
-    hat, inv = rms_stats(x[0])
-    gin_out[...] = gmid[...] + rms_back(hat, inv, g_in[...], gn)
-
-    @pl.when(i == 0)
-    def _():
-        gains[...] = jnp.zeros_like(gains)
-        gain_k[...] = jnp.zeros_like(gain_k)
-
-    gains[...] += jnp.sum(gn * hat, axis=0, keepdims=True)
-    gain_k[...] += jnp.sum(dkn * k_hat, axis=0, keepdims=True)
-
-
 def whole(shape):
     return pl.BlockSpec(shape, lambda *_: (0,) * len(shape), pipeline_mode=pl.Buffered(1))
 
@@ -416,35 +383,6 @@
     )(seg_ext, q_o, q_x, k, v, ga_o, ga_x, lse, delta, ql_o, ql_x, cos, sin, rows8)
 
 
-def input_back(first_row, x3, gmid, dk, dv, back, kl, cos, sin, rows8, qr_o, qr_x, wq_o, wq_x, wk, wv, nb):
-    depth = x3.shape[2]
-    own, part = qr_o.shape
-    n = BLOCK
-    kern = lambda me, *refs: input_back_kernel(*refs)
-    return pl.pallas_call(
-        kern,
-        grid_spec=pltpu.PrefetchScalarGridSpec(
-            num_scalar_prefetch=1,
-            grid=(own // n,),
-            in_specs=[pl.BlockSpec((1, n, depth), lambda i, me: (0, me[0] // n + i, 0)), rows_of(n, depth),
-                      rows_of(n, HEAD_WIDTH), rows_of(n, HEAD_WIDTH), whole(back.shape),
-                      rows_of(n, HEAD_WIDTH), rows_of(n, LANES), rows_of(n, LANES),
-                      whole(rows8.shape), rows_of(n, part), rows_of(n, part),
-                      whole(wq_o.shape), whole(wq_x.shape), whole(wk.shape), whole(wv.shape), rows_of(n, depth)],
-            out_specs=[rows_of(n, depth), pl.BlockSpec((2 * HEAD_WIDTH, depth), lambda i, *_: (0, 0)),
-                       pl.BlockSpec((1, depth), lambda i, *_: (0, 0)),
-                       pl.BlockSpec((1, HEAD_WIDTH), lambda i, *_: (0, 0))],
-            scratch_shapes=[pltpu.VMEM((2 * HEAD_WIDTH, depth), F32)],
-        ),
-        out_shape=[sds((own, depth), F32), sds((2 * HEAD_WIDTH, depth), BF),
-                   sds((1, depth), F32), sds((1, HEAD_WIDTH), F32)],
-        cost_estimate=cost(8),
-        compiler_params=params(),
-        name="input_back",
-    )(first_row, x3, gmid, dk, dv, back, kl, cos, sin, rows8,
-      qr_o, qr_x, wq_o, wq_x, wk, wv, nb)
-
-
 def swap(value, n_tensor):
     return lax.ppermute(value, "tensor", [(t, n_tensor - 1 - t) for t in range(n_tensor)])
 
@@ -474,15 +412,20 @@
     return index
 
 
-def reduce_kernel(items, kv_groups, n_bits, *refs):
+def finish_kernel(items, kv_groups, n_bits, *refs):
     n_items = len(items)
     kv_order = sum(kv_groups, ())
     refs = list(refs)
     take = lambda count: [refs.pop(0) for _ in range(count)]
-    ins = [take(2 if given else 1) for _, given in items]
-    kv_in, g_block, g_in, g_q, g_k = take(5)
+    ins = [take(2) for _, given in items if given]
+    front, rows8, g_block, g_q = take(4)
+    far = take(14)
     outs = take(n_items)
-    k_out, v_out, gain_out = take(3)
+    k_out, v_out, gain_out, gin_far = take(4)
+    near = take(14)
+    local_sems = refs.pop(0)
+    front_got, kraw, vraw, kv_in, query_sent, query_got, query, gin, g_in, g_k = take(10)
+    ins.append([query])
     recvs, curs = [], []
     for order, given in items:
         first = 1 if given else 0
@@ -565,21 +508,58 @@
         lax.fori_loop(0, half, body, 0)
         start(n, s + 1)
 
-    kv_copies = [send(kv_in.at[1 - core], kv_core, {"tensor": 1 - core})]
+    other_core = {"tensor": 1 - core}
+    own, depth = gin.shape
+    sources = list(far)
+    sources[0] = far[0].at[0, pl.ds(pl.multiple_of(core * own, own), own), :]
+    names = ("x", "gmid", "wq_o", "wq_x", "wk", "wv", "dk", "dv", "kl", "cos", "sin", "qr_o", "qr_x", "nb")
+    fetch = {name: pltpu.make_async_copy(s, d, local_sems.at[k])
+             for k, (name, s, d) in enumerate(zip(names, sources, near))}
+    buf = dict(zip(names, near))
+    for name in ("nb", "qr_x", "dk", "dv", "kl", "cos", "sin", "qr_o", "wk", "wv", "wq_o", "wq_x", "x", "gmid"):
+        fetch[name].start()
+    front_copy = send(front, front_got, other_core)
     for n in range(n_items):
-        if not items[n][1]:
-            start(n, 0)
-    gain_own[0][...] = jnp.zeros_like(gain_own[0])
-    gain_own[0][0:3, :] = g_block[0:3, :]
-    gain_own[0][3:4, :] = g_in[...]
-    gain_own[0][4:5, :HEAD_WIDTH] = g_q[...]
-    gain_own[0][5:6, :HEAD_WIDTH] = g_k[...]
-
+        if items[n][1]:
+            finish(n, 0)
+    fetch["nb"].wait()
+    fetch["qr_x"].wait()
+    query_sent[...] = tn(buf["qr_x"][...], buf["nb"][...]).astype(BF)
+    query_copy = send(query_sent, query_got, other_core)
+    for name in ("dk", "dv", "kl", "cos", "sin"):
+        fetch[name].wait()
+    front_copy.wait_recv()
+    gk_row, gin_row = rows8[5:6, :HEAD_WIDTH], rows8[0:1, :]
+    g_k[...] = jnp.zeros_like(g_k)
+    g_in[...] = jnp.zeros_like(g_in)
+    blocks = own // BLOCK
+
+    def kv_rows(i, carry):
+        at = pl.ds(pl.multiple_of(i * BLOCK, BLOCK), BLOCK)
+        tail = ((i == blocks - 1) & (core == 0)).astype(F32)
+        dk = buf["dk"][at, :] + tail * front_got[:, :HEAD_WIDTH].astype(F32)
+        dv = buf["dv"][at, :] + tail * front_got[:, HEAD_WIDTH:].astype(F32)
+        dkn = rotate(dk, buf["cos"][at, :], buf["sin"][at, :], -1)
+        k_hat, k_inv = rms_stats(buf["kl"][at, :])
+        kraw[at, :] = rms_back(k_hat, k_inv, gk_row, dkn).astype(BF)
+        vraw[at, :] = dv.astype(BF)
+        g_k[...] += jnp.sum(dkn * k_hat, axis=0, keepdims=True)
+        return carry
+
+    lax.fori_loop(0, blocks, kv_rows, 0)
+    n_chunk, rows_k = kv_in.shape[1:3]
+    for t, raw in enumerate((kraw, vraw)):
+        kv_in[t] = tn(raw[...], buf["nb"][...]).astype(BF).reshape(n_chunk, rows_k, depth)
+    kv_copies = [send(kv_in.at[1 - core], kv_core, other_core)]
+    fetch["qr_o"].wait()
+    query_copy.wait_recv()
+    own_query = tn(buf["qr_o"][...], buf["nb"][...]) + query_got[...].astype(F32)
+    query[...] = own_query.astype(BF).reshape(query.shape)
+    start(n_items - 1, 0)
     def gain_start(s):
         device = {"tensor": 1 - core} if s == 0 else {"dp": flipped((s - 1,))}
         return send(gain_own[s], gain_got[s], device)
 
-    gain_copies = [gain_start(0)]
     kv_copies[0].wait_recv()
 
     def kv_first(j, carry):
@@ -608,9 +588,27 @@
     for k, b in enumerate(kv_order):
         spot = spot + bit_of(me, b) * 2 ** (n_bits - 1 - k)
     kv_copies = kv_start(0)
-    for n in range(n_items):
-        if items[n][1]:
-            finish(n, 0)
+    for name in ("wk", "wv", "wq_o", "wq_x", "x", "gmid"):
+        fetch[name].wait()
+
+    def input_rows(i, carry):
+        at = pl.ds(pl.multiple_of(i * QB, QB), QB)
+        gn = nt(kraw[at, :], buf["wk"][...]) + nt(vraw[at, :], buf["wv"][...])
+        gn = gn + nt(buf["qr_o"][at, :], buf["wq_o"][...]) + nt(buf["qr_x"][at, :], buf["wq_x"][...])
+        hat, inv = rms_stats(buf["x"][at, :])
+        gin[at, :] = buf["gmid"][at, :] + rms_back(hat, inv, gin_row, gn)
+        g_in[...] += jnp.sum(gn * hat, axis=0, keepdims=True)
+        return carry
+
+    lax.fori_loop(0, own // QB, input_rows, 0)
+    gin_copy = pltpu.make_async_copy(gin, gin_far, local_sems.at[len(names)])
+    gin_copy.start()
+    gain_own[0][...] = jnp.zeros_like(gain_own[0])
+    gain_own[0][0:3, :] = g_block[0:3, :]
+    gain_own[0][3:4, :] = g_in[...]
+    gain_own[0][4:5, :HEAD_WIDTH] = g_q[...]
+    gain_own[0][5:6, :HEAD_WIDTH] = g_k[...]
+    gain_copies = [gain_start(0)]
     todo = [(n, s) for s in range(n_bits) for n in range(-1, n_items) if s or n < 0 or not items[n][1]]
     todo = todo + [(-1, n_bits)]
     todo.sort(key=lambda e: e[1] - (1 if e[0] >= 0 and items[e[0]][1] else 0))
@@ -675,49 +673,59 @@
         return carry
 
     lax.fori_loop(0, 2**n_bits, unpack, 0)
+    gin_copy.wait()
     for copy in sent:
         copy.wait_send()
 
 
-def reduce_all(n_dp, items, kv, kv_order, g_block, g_in, g_q, g_k):
+def finish_all(n_dp, items, order, kv_order, front, rows8, g_block, g_q, far):
     n_bits = len(kv_order)
+    own, part = far[11].shape
+    depth = far[1].shape[1]
     groups = tuple(tuple(kv_order[k : k + 2]) for k in range(0, n_bits, 2))
-    spec = []
-    operands = []
-    scratch = []
-    outs = []
-    copies = 0
-    for value, got, order in items:
-        n, c, width = value.shape
-        given = got is not None
-        spec.append((tuple(order), given))
-        operands += [value, got] if given else [value]
+    spec, operands, outs, comm = [], [], [], []
+    copies = 3
+    shapes = [value.shape for value, _, _ in items] + [(n_dp, part // n_dp, depth)]
+    for k, (n, c, width) in enumerate(shapes):
+        given = k < len(items)
+        spec.append((tuple(items[k][2] if given else order), given))
+        if given:
+            operands += [items[k][0], items[k][1]]
         outs.append(sds((c, width), F32))
         first = 1 if given else 0
-        scratch += [pltpu.VMEM((2 ** (n_bits - s - 1), c, width), BF) for s in range(first, n_bits)]
-        scratch += [pltpu.VMEM((2 ** (n_bits - s), c, width), BF) for s in range(1, n_bits)]
+        comm += [pltpu.VMEM((2 ** (n_bits - s - 1), c, width), BF) for s in range(first, n_bits)]
+        comm += [pltpu.VMEM((2 ** (n_bits - s), c, width), BF) for s in range(1, n_bits)]
         copies += n_bits - 1 + (0 if given else n // 2)
-    _, n, c, width = kv.shape
-    scratch += [pltpu.VMEM((n, c, width), BF)]
+    n, c, width = n_dp, HEAD_WIDTH // n_dp, depth
+    comm += [pltpu.VMEM((n, c, width), BF)]
     sizes = [2 ** (n_bits - sum(len(x) for x in groups[:g])) for g in range(len(groups) + 1)]
-    scratch += [pltpu.VMEM((2 ** len(groups[g]) - 1, sizes[g + 1], c, width), BF) for g in range(len(groups))]
-    scratch += [pltpu.VMEM((sizes[g], c, width), BF) for g in range(len(groups))]
-    scratch += [pltpu.VMEM((2, n, c, width), BF)]
-    scratch += [pltpu.VMEM((8, width), F32) for _ in range(2 * (n_bits + 1))]
+    comm += [pltpu.VMEM((2 ** len(groups[g]) - 1, sizes[g + 1], c, width), BF) for g in range(len(groups))]
+    comm += [pltpu.VMEM((sizes[g], c, width), BF) for g in range(len(groups))]
+    comm += [pltpu.VMEM((2, n, c, width), BF)]
+    comm += [pltpu.VMEM((8, width), F32) for _ in range(2 * (n_bits + 1))]
     copies += 2 + 2 * sum(2 ** len(g) - 1 for g in groups) + n_bits + 1
-    scratch += [pltpu.SemaphoreType.DMA((copies,)), pltpu.SemaphoreType.DMA((copies,))]
-    outs += [sds(kv.shape[1:], F32), sds(kv.shape[1:], F32), sds((8, width), F32)]
+    comm += [pltpu.SemaphoreType.DMA((copies,)), pltpu.SemaphoreType.DMA((copies,))]
+    outs += [sds((n, c, width), F32), sds((n, c, width), F32), sds((8, width), F32), sds((own, depth), F32)]
+    near = [pltpu.VMEM((own, depth), F32)] + [pltpu.VMEM(a.shape, a.dtype) for a in far[1:]]
+    scratch = near + [
+        pltpu.SemaphoreType.DMA((len(far) + 1,)),
+        pltpu.VMEM(front.shape, BF), pltpu.VMEM((own, HEAD_WIDTH), BF), pltpu.VMEM((own, HEAD_WIDTH), BF),
+        pltpu.VMEM((2, n, c, width), BF), pltpu.VMEM((part, depth), BF), pltpu.VMEM((part, depth), BF),
+        pltpu.VMEM((n_dp, part // n_dp, depth), BF), pltpu.VMEM((own, depth), F32), pltpu.VMEM((1, depth), F32),
+        pltpu.VMEM((1, HEAD_WIDTH), F32),
+    ] + comm
     vmem = pl.BlockSpec(memory_space=pltpu.VMEM)
-    operands += [kv, g_block, g_in, g_q, g_k]
+    anywhere = pl.BlockSpec(memory_space=pl.ANY)
+    operands += [front, rows8, g_block, g_q]
     return pl.pallas_call(
-        functools.partial(reduce_kernel, tuple(spec), groups, n_bits),
+        functools.partial(finish_kernel, tuple(spec), groups, n_bits),
         out_shape=outs,
-        in_specs=[vmem] * len(operands),
-        out_specs=[vmem] * len(outs),
+        in_specs=[vmem] * len(operands) + [anywhere] * len(far),
+        out_specs=[vmem] * (len(outs) - 1) + [anywhere],
         scratch_shapes=scratch,
         compiler_params=pltpu.CompilerParams(collective_id=0, has_side_effects=True, vmem_limit_bytes=VMEM_LIMIT),
-        name="reduce_all",
-    )(*operands)
+        name="finish_all",
+    )(*operands, *far)
 
 
 def hop(value, b, n_dp):
@@ -784,17 +792,10 @@
         seg_ext, q_o, q_x, k, v, ga_o, ga_x, lse, delta, ql_o, ql_x, cos, sin, rows8)
     front, qr_x, *arrived = lax.optimization_barrier((front, qr_x, *(got for _, got in state)))
     state = [(value, got) for (value, _), got in zip(state, arrived)]
-    back = lax.ppermute(front, "tensor", [(t, t - 1) for t in range(1, n_tensor)])
-    query_sent = tn(qr_x, nb).astype(BF)
-    query_got = swap(query_sent, n_tensor)
-    grad_input, kv, gain_in, gain_k = input_back(
-        first_row, residual_in, after(gmid, query_sent), dk, dv, back, kl, cos, sin, rows8, qr_o, qr_x,
-        w_query, wq_x, w_key, w_value, nb)
-    query = chunks((tn(after(qr_o, gain_k), nb) + query_got.astype(F32)).astype(BF))
-    kv = kv.reshape(2, n_dp, HEAD_WIDTH // n_dp, depth)
     items = [(value, got, order) for (value, got), order in zip(state, orders)]
-    *shares, k_sum, v_sum, gain_sum = reduce_all(
-        n_dp, items + [(query, None, plain)], kv, plain, gains, gain_in, gain_q, gain_k)
+    far = (residual_in, gmid, w_query, wq_x, w_key, w_value, dk, dv, kl, cos, sin, qr_o, qr_x, nb)
+    *shares, k_sum, v_sum, gain_sum, grad_input = finish_all(
+        n_dp, items, plain, plain, front, rows8, gains, gain_q, far)
     s_down, s_gate, s_up, s_out, s_query = shares
     k_sum = k_sum.reshape(HEAD_WIDTH, depth)
     v_sum = v_sum.reshape(HEAD_WIDTH, depth)

time: 201 us -> 189 us (0.940)
  Pallas kernels: 142 us -> 136 us
  matrix products: 22.1 us -> 16.4 us
  starting transfers between devices: 11.9 us -> 7.58 us
  local copies, waits for them, and re-layouts: 21.8 us -> 25.9 us
    pallas_call x2 -> x1, Pallas kernels: 63.9 us -> 57.9 us  [finish_all(): pl.pallas_call(functools.partial(finish_kernel, tuple(spec), groups, n_bi...]
    dot_general x10 -> x8, matrix products: 22.1 us -> 16.4 us  [tn(): lax.dot_general(a, b, (((0,), (0,)), ((), ())), preferred_element_type=F32)]
    ppermute x1 -> x0, starting transfers between devices: 4.26 us -> none  [on_device(): lax.ppermute(front, 'tensor', [(t, t - 1) for t in range(1, n_tensor)])]
    unnamed x59 -> x58, local copies, waits for them, and re-layouts: 6.56 us -> 9.4 us
  transfers between devices with their start and end apart: 15 -> 13, of which waited for: 0 -> 0; matrix products, arithmetic and copies ran while one was open for 13% -> 12% of each run, Pallas kernels for 21% -> 15%
where the time goes in v4:
time: 189 us; the launch traced here: 188 us
  Pallas kernels  136 us (72%)
  local copies, waits for them, and re-layouts  25.9 us (14%)
  matrix products  16.4 us (9%)
  starting transfers between devices  7.58 us (4%)
    pallas_call x1, Pallas kernels, finish_all(): pl.pallas_call(functools.partial(finish_kernel, tuple(spec), groups, n_bi...  57.9 us
    pallas_call x1, Pallas kernels, block_pass(): pl.pallas_call(kern, grid_spec=pltpu.PrefetchScalarGridSpec(num_scalar_pr...  49.2 us
    pallas_call x1, Pallas kernels, attn_back(): pl.pallas_call(attn_back_kernel, grid=(own // n,), in_specs=[whole(seg_ex...  18 us
    dot_general x8, matrix products, tn(): lax.dot_general(a, b, (((0,), (0,)), ((), ())), preferred_element_type=F32)  16.4 us
    pallas_call x1, Pallas kernels, project(): pl.pallas_call(project_kernel, grid_spec=pltpu.PrefetchScalarGridSpec(num...  11.1 us
    unnamed x58, local copies, waits for them, and re-layouts  9.4 us
    ppermute x4, starting transfers between devices, hop(): return lax.ppermute(value, 'dp', [(i, i ^ 2 ** b) for i in range(n_dp)])  5.13 us
  transfers between devices with their start and end apart: 13, of which 0 were waited for; matrix products, arithmetic and copies ran while one was open for 12% of the time, Pallas kernels for 15%

profile of v4, /device:TPU:1, one launch (start us, length us, event | category | flops | bytes accessed | tf_op | source)
XLA Modules:
  0.0 188.4 jit_solution(390555288135251494)
XLA Ops:
  0.6 0.1 collective-permute-start.2
  0.7 0.5 collective-permute-start.3
  1.2 0.1 collective-permute-start.4
  1.3 0.4 collective-permute-start
  1.7 0.1 collective-permute-start.1
  1.8 0.8 pad_dynamic-slice_fusion
  2.6 0.6 broadcast_in_dim.14.seg.refs_2_
  3.2 0.7 pad.8
  3.9 0.7 pad.9
  4.6 0.7 stack.24
  5.2 0.7 stack.25
  5.9 0.7 stack.26
  6.6 0.7 stack.27
  7.3 0.6 stack.31.rows8.refs_15_.refs_9_
  8.0 1.4 convert_reduce_fusion
  9.4 0.8 copy-done.5
  10.2 11.1 %project.1 = (bf16[1024,512]{1,0:T(8,128)(2,1)}, bf16[1024,512]{1,0:T(8,128)(2,1)}, f32[1024,512]{1,0:T(8,128)}, f32[1024,512]{1,0:T(8,128)}, bf16[1536,256]{1,0...) custom-call(s32[1]{0:T(128)} %bitcast.me, ...), custom_call_target="tpu_custom_call" | custom-call | flops 6000000000 | bytes 6000000 | tf_op jit(solution)/shard_map/project/pallas_call | solution.py:299
  21.3 0.0 collective-permute-done.1.refs_8_
  21.3 0.0 collective-permute-done.3.refs_12_
  21.3 0.0 collective-permute-done.4.refs_14_
  21.3 1.0 copy-done.15
  22.4 0.5 copy-done.16
  22.8 49.2 %block.1 = (f32[1024,640]{1,0:T(8,128)}, f32[1024,640]{1,0:T(8,128)}, bf16[1024,512]{1,0:T(8,128)(2,1)}, bf16[1024,512]{1,0:T(8,128)(2,1)}, bf16[1024,512]{1,0:T...) custom-call(s32[1]{0:T(128)} %bitcast.me, ...), custom_call_target="tpu_custom_call" | custom-call | flops 40000000000 | bytes 40000000 | tf_op jit(solution)/shard_map/block/pallas_call | solution.py:337
  72.0 3.5 %convolution_convert_fusion.2 = bf16[640,1024]{1,0:T(8,128)(2,1)S(1)} fusion(bf16[1024,640]{1,0:T(8,128)(2,1)} %get-tuple-element.77, bf16[1024,1024]{1,0:T(8,128)(2,1)} %get-tuple-element.83), kind=kOutput, calls=%fused_computation.5 | convolution fusion | flops 1342832640 | bytes 4718592 | tf_op jit(solution)/shard_map/dot_general | solution.py:35
  75.5 0.5 collective-permute-start.5
  76.0 3.9 %convolution_convert_fusion.1 = bf16[1024,640]{1,0:T(8,128)(2,1)S(1)} fusion(bf16[1024,1024]{1,0:T(8,128)(2,1)} %get-tuple-element.84, bf16[1024,640]{1,0:T(8,128)(2,1)} %get-tuple-element.85), kind=kOutput, calls=%fused_computation.4 | convolution fusion | flops 1342832640 | bytes 4718592 | tf_op jit(solution)/shard_map/dot_general | solution.py:35
  80.0 0.1 collective-permute-start.6
  80.1 1.9 convolution_convert_fusion
  82.0 0.5 collective-permute-start.7
  82.5 0.9 convolution_convert_fusion.3
  83.4 0.1 collective-permute-start.8
  83.5 0.6 copy-done.24
  84.1 0.4 copy-done.25
  84.4 1.6 add_convert_fusion.2
  86.0 1.0 dynamic-slice_bitcast_fusion
  87.0 2.3 %collective-permute-start.9 = (bf16[8,40,1024]{2,1,0:T(8,128)(2,1)}, bf16[8,40,1024]{2,1,0:T(8,128)(2,1)S(1)}, u32[]{:S(2)}, u32[]{:S(2)}) collective-permute-start(bf16[8,40,1024]{2,1,0:T(8,128)(2,1)} %dynamic-slice_bitcast_fusion), channel_id=1, source_target_pairs={{0,2},{2,0},{4,6},{6,4},{8,10},{10,8},{12,14},{14,12},{16,18},{18,... | collective-permute-start | bytes 1966088 | tf_op jit(solution)/shard_map/ppermute | solution.py:732
  89.3 0.0 collective-permute-done.6
  89.3 1.9 add_convert_fusion.1
  91.2 1.0 constant_dynamic-slice_fusion.1
  92.2 1.2 collective-permute-start.10
  93.5 1.9 add_convert_fusion
  95.4 1.0 constant_dynamic-slice_fusion
  96.4 1.3 collective-permute-start.11
  97.7 0.9 fusion
  98.6 0.3 collective-permute-start.12
  98.9 18.0 %attn_back.1 = (bf16[1024,512]{1,0:T(8,128)(2,1)}, bf16[1024,512]{1,0:T(8,128)(2,1)}, f32[1024,256]{1,0:T(8,128)}, f32[1024,256]{1,0:T(8,128)}, bf16[512,512]{1,0:T(8,128)(2,1)}, /*index=5*/f32[1,256]{1,0:T(1,128)}) custom-call(s32[1,1536]{1,0:T(1,128)} %broadcast_in_dim.14.seg.refs_2_, bf16[1024,512]{1,0:T(8,128)(2,1)} %get-tuple-element.72.refs_3_.q_o, ...), custom_call_target="tpu_custom_call" | custom-call | flops 20000000000 | bytes 20000000 | tf_op jit(solution)/shard_map/attn_back/pallas_call | solution.py:369
  116.9 0.0 collective-permute-done.11.refs_5_
  117.0 0.0 collective-permute-done.10.refs_3_
  117.0 0.0 copy-start.6
  117.0 0.7 copy-done.9
  117.7 0.2 copy-done.8
  117.9 0.2 copy-done.7
  118.1 0.2 copy-done.6
  118.3 57.9 %finish_all.1 = (f32[40,1024]{1,0:T(8,128)}, f32[64,640]{1,0:T(8,128)}, f32[64,640]{1,0:T(8,128)}, f32[40,512]{1,0:T(8,128)}, f32[32,640]{1,0:T(8,128)}, /*index...) custom-call(bf16[16,40,1024]{2,1,0:T(8,128)(2,1)} %bitcast.55, ...), custom_call_target="tpu_custom_call" | custom-call | tf_op jit(solution)/shard_map/finish_all/pallas_call | solution.py:720
  176.2 1.5 slice_reduce_fusion
  177.7 1.3 fusion.1
  179.1 2.3 %copy.42 = f32[256,640]{0,1:T(8,128)} copy(f32[256,640]{1,0:T(8,128)} %bitcast.66) | data formatting | bytes 1310720 | tf_op jit(solution)/shard_map/reshape | solution.py:800
  181.4 2.2 %copy.43 = f32[256,640]{0,1:T(8,128)} copy(f32[256,640]{1,0:T(8,128)} %bitcast.65) | data formatting | bytes 1310720 | tf_op jit(solution)/shard_map/reshape | solution.py:801
  183.6 1.5 copy.54
  185.1 0.6 copy.55
  185.7 0.6 copy.56
  186.3 0.7 copy.57
  187.0 0.7 copy.58
  187.7 0.7 copy.59
  (53 shorter events, 0.1 us)
Async XLA Ops:
  0.6 20.6 %collective-permute-start.2 = (bf16[640,1024]{1,0:T(8,128)(2,1)}, bf16[640,1024]{1,0:T(8,128)(2,1)S(1)}, u32[]{:S(2)}, u32[]{:S(2)}) collective-permute-start(bf16[640,1024]{1,0:T(8,128)(2,1)} %refs_9_.1), channel_id=1, source_target_pairs={{0,1},{1,0},{2,3},{3,2},{4,5},{5,4},{6,7},{7,6},{8,9},{9,8},{10,11... | collective-permute-start | bytes 3932168 | tf_op jit(solution)/shard_map/ppermute | solution.py:387
  0.7 20.6 %collective-permute-start.3 = (bf16[640,1024]{1,0:T(8,128)(2,1)}, bf16[640,1024]{1,0:T(8,128)(2,1)S(1)}, u32[]{:S(2)}, u32[]{:S(2)}) collective-permute-start(bf16[640,1024]{1,0:T(8,128)(2,1)} %refs_11_.1), channel_id=1, source_target_pairs={{0,1},{1,0},{2,3},{3,2},{4,5},{5,4},{6,7},{7,6},{8,9},{9,8},{10,11... | collective-permute-start | bytes 3932168 | tf_op jit(solution)/shard_map/ppermute | solution.py:387
  1.2 20.1 %collective-permute-start.4 = (bf16[1024,640]{1,0:T(8,128)(2,1)}, bf16[1024,640]{1,0:T(8,128)(2,1)}, u32[]{:S(2)}, u32[]{:S(2)}) collective-permute-start(bf16[1024,640]{1,0:T(8,128)(2,1)} %refs_13_.1), channel_id=1, source_target_pairs={{0,1},{1,0},{2,3},{3,2},{4,5},{5,4},{6,7},{7,6},{8,9},{9,8},{10,11... | collective-permute-start | bytes 3932168 | tf_op jit(solution)/shard_map/ppermute | solution.py:387
  1.3 8.1 %collective-permute-start = (bf16[640,512]{1,0:T(8,128)(2,1)}, bf16[640,512]{1,0:T(8,128)(2,1)S(1)}, u32[]{:S(2)}, u32[]{:S(2)}) collective-permute-start(bf16[640,512]{1,0:T(8,128)(2,1)} %refs_14_.1), channel_id=1, source_target_pairs={{0,1},{1,0},{2,3},{3,2},{4,5},{5,4},{6,7},{7,6},{8,9},{9,8},{10,11... | collective-permute-start | bytes 1966088 | tf_op jit(solution)/shard_map/ppermute | solution.py:387
  1.7 19.5 %collective-permute-start.1 = (bf16[512,640]{1,0:T(8,128)(2,1)}, bf16[512,640]{1,0:T(8,128)(2,1)}, u32[]{:S(2)}, u32[]{:S(2)}) collective-permute-start(bf16[512,640]{1,0:T(8,128)(2,1)} %refs_7_.1), channel_id=1, source_target_pairs={{0,1},{1,0},{2,3},{3,2},{4,5},{5,4},{6,7},{7,6},{8,9},{9,8},{10,11... | collective-permute-start | bytes 1966088 | tf_op jit(solution)/shard_map/ppermute | solution.py:387
  9.4 0.8 copy-start.5
  21.3 1.1 copy-start.15
  21.3 1.5 copy-start.16
  75.5 8.0 %collective-permute-start.5 = (bf16[640,1024]{1,0:T(8,128)(2,1)S(1)}, bf16[640,1024]{1,0:T(8,128)(2,1)S(1)}, u32[]{:S(2)}, u32[]{:S(2)}) collective-permute-start(bf16[640,1024]{1,0:T(8,128)(2,1)S(1)} %convolution_convert_fusion.2), channel_id=1, source_target_pairs={{0,1},{1,0},{2,3},{3,2},{4,5},{5,4},{6,7},{7,6},{8,9},{9,8},{10,11... | collective-permute-start | bytes 3932168 | tf_op jit(solution)/shard_map/ppermute | solution.py:387
  76.0 4.1 %copy-start.22 = (bf16[1024,1024]{1,0:T(8,128)(2,1)S(1)}, bf16[1024,1024]{1,0:T(8,128)(2,1)}, u32[]{:S(2)}) copy-start(bf16[1024,1024]{1,0:T(8,128)(2,1)} %get-tuple-element.86) | copy-start | bytes 6291460
  76.0 4.1 %copy-start.23 = (bf16[1024,640]{1,0:T(8,128)(2,1)S(1)}, bf16[1024,640]{1,0:T(8,128)(2,1)}, u32[]{:S(2)}) copy-start(bf16[1024,640]{1,0:T(8,128)(2,1)} %get-tuple-element.85) | copy-start | bytes 3932164
  80.0 9.4 %collective-permute-start.6 = (bf16[1024,640]{1,0:T(8,128)(2,1)S(1)}, bf16[1024,640]{1,0:T(8,128)(2,1)S(1)}, u32[]{:S(2)}, u32[]{:S(2)}) collective-permute-start(bf16[1024,640]{1,0:T(8,128)(2,1)S(1)} %convolution_convert_fusion.1), channel_id=1, source_target_pairs={{0,1},{1,0},{2,3},{3,2},{4,5},{5,4},{6,7},{7,6},{8,9},{9,8},{10,11... | collective-permute-start | bytes 3932168 | tf_op jit(solution)/shard_map/ppermute | solution.py:387
  80.1 2.4 %copy-start.17 = (bf16[1024,640]{1,0:T(8,128)(2,1)S(1)}, bf16[1024,640]{1,0:T(8,128)(2,1)}, u32[]{:S(2)}) copy-start(bf16[1024,640]{1,0:T(8,128)(2,1)} %get-tuple-element.79) | copy-start | bytes 3932164
  80.1 2.4 %copy-start.19 = (bf16[1024,512]{1,0:T(8,128)(2,1)S(1)}, bf16[1024,512]{1,0:T(8,128)(2,1)}, u32[]{:S(2)}) copy-start(bf16[1024,512]{1,0:T(8,128)(2,1)} %get-tuple-element.87) | copy-start | bytes 3145732
  82.0 11.5 %collective-permute-start.7 = (bf16[1024,640]{1,0:T(8,128)(2,1)S(1)}, bf16[1024,640]{1,0:T(8,128)(2,1)S(1)}, u32[]{:S(2)}, u32[]{:S(2)}) collective-permute-start(bf16[1024,640]{1,0:T(8,128)(2,1)S(1)} %convolution_convert_fusion), channel_id=1, source_target_pairs={{0,1},{1,0},{2,3},{3,2},{4,5},{5,4},{6,7},{7,6},{8,9},{9,8},{10,11... | collective-permute-start | bytes 3932168 | tf_op jit(solution)/shard_map/ppermute | solution.py:387
  82.5 1.6 copy-start.24
  82.5 1.9 %copy-start.25 = (bf16[1024,640]{1,0:T(8,128)(2,1)S(1)}, bf16[1024,640]{1,0:T(8,128)(2,1)}, u32[]{:S(2)}) copy-start(bf16[1024,640]{1,0:T(8,128)(2,1)} %get-tuple-element.77) | copy-start | bytes 3932164
  83.4 14.3 %collective-permute-start.8 = (bf16[640,512]{1,0:T(8,128)(2,1)S(1)}, bf16[640,512]{1,0:T(8,128)(2,1)S(1)}, u32[]{:S(2)}, u32[]{:S(2)}) collective-permute-start(bf16[640,512]{1,0:T(8,128)(2,1)S(1)} %convolution_convert_fusion.3), channel_id=1, source_target_pairs={{0,1},{1,0},{2,3},{3,2},{4,5},{5,4},{6,7},{7,6},{8,9},{9,8},{10,11... | collective-permute-start | bytes 1966088 | tf_op jit(solution)/shard_map/ppermute | solution.py:387
  84.4 4.9 %copy-start.21 = (bf16[1024,1024]{1,0:T(8,128)(2,1)S(1)}, bf16[1024,1024]{1,0:T(8,128)(2,1)}, u32[]{:S(2)}) copy-start(bf16[1024,1024]{1,0:T(8,128)(2,1)} %get-tuple-element.93) | copy-start | bytes 6291460
  86.0 5.2 %copy-start = (bf16[640,1024]{1,0:T(8,128)(2,1)}, bf16[640,1024]{1,0:T(8,128)(2,1)S(1)}, u32[]{:S(2)}) copy-start(bf16[640,1024]{1,0:T(8,128)(2,1)S(1)} %add_convert_fusion.2) | copy-start | bytes 3932164
  87.0 29.9 %collective-permute-start.9 = (bf16[8,40,1024]{2,1,0:T(8,128)(2,1)}, bf16[8,40,1024]{2,1,0:T(8,128)(2,1)S(1)}, u32[]{:S(2)}, u32[]{:S(2)}) collective-permute-start(bf16[8,40,1024]{2,1,0:T(8,128)(2,1)} %dynamic-slice_bitcast_fusion), channel_id=1, source_target_pairs={{0,2},{2,0},{4,6},{6,4},{8,10},{10,8},{12,14},{14,12},{16,18},{18,... | collective-permute-start | bytes 1966088 | tf_op jit(solution)/shard_map/ppermute | solution.py:732
  89.3 4.2 %copy-start.20 = (bf16[1024,1024]{1,0:T(8,128)(2,1)S(1)}, bf16[1024,1024]{1,0:T(8,128)(2,1)}, u32[]{:S(2)}) copy-start(bf16[1024,1024]{1,0:T(8,128)(2,1)} %get-tuple-element.94) | copy-start | bytes 6291460
  91.2 4.1 %copy-start.1 = (bf16[1024,640]{1,0:T(8,128)(2,1)}, bf16[1024,640]{1,0:T(8,128)(2,1)S(1)}, u32[]{:S(2)}) copy-start(bf16[1024,640]{1,0:T(8,128)(2,1)S(1)} %add_convert_fusion.1) | copy-start | bytes 3932164
  92.2 24.7 %collective-permute-start.10 = (bf16[8,64,640]{2,1,0:T(8,128)(2,1)}, bf16[8,64,640]{2,1,0:T(8,128)(2,1)S(1)}, u32[]{:S(2)}, u32[]{:S(2)}) collective-permute-start(bf16[8,64,640]{2,1,0:T(8,128)(2,1)} %bitcast.8), channel_id=1, source_target_pairs={{0,4},{2,6},{4,0},{6,2},{8,12},{10,14},{12,8},{14,10},{16,20},{18,... | collective-permute-start | bytes 1966088 | tf_op jit(solution)/shard_map/ppermute | solution.py:732
  95.4 3.2 %copy-start.2 = (bf16[1024,640]{1,0:T(8,128)(2,1)}, bf16[1024,640]{1,0:T(8,128)(2,1)S(1)}, u32[]{:S(2)}) copy-start(bf16[1024,640]{1,0:T(8,128)(2,1)S(1)} %add_convert_fusion) | copy-start | bytes 3932164
  95.4 2.3 %copy-start.18 = (bf16[1024,512]{1,0:T(8,128)(2,1)S(1)}, bf16[1024,512]{1,0:T(8,128)(2,1)}, u32[]{:S(2)}) copy-start(bf16[1024,512]{1,0:T(8,128)(2,1)} %get-tuple-element.95) | copy-start | bytes 3145732
  96.4 20.6 %collective-permute-start.11 = (bf16[8,64,640]{2,1,0:T(8,128)(2,1)}, bf16[8,64,640]{2,1,0:T(8,128)(2,1)S(1)}, u32[]{:S(2)}, u32[]{:S(2)}) collective-permute-start(bf16[8,64,640]{2,1,0:T(8,128)(2,1)} %bitcast.10), channel_id=1, source_target_pairs={{0,8},{2,10},{4,12},{6,14},{8,0},{10,2},{12,4},{14,6},{16,24},{18,... | collective-permute-start | bytes 1966088 | tf_op jit(solution)/shard_map/ppermute | solution.py:732
  98.5 18.4 %copy-start.4 = (bf16[640,512]{1,0:T(8,128)(2,1)}, bf16[640,512]{1,0:T(8,128)(2,1)S(1)}, u32[]{:S(2)}) copy-start(bf16[640,512]{1,0:T(8,128)(2,1)S(1)} %fusion) | copy-start | bytes 1966084
  98.6 18.3 %collective-permute-start.12 = (bf16[8,40,512]{2,1,0:T(8,128)(2,1)S(1)}, bf16[8,40,512]{2,1,0:T(8,128)(2,1)S(1)}, u32[]{:S(2)}, u32[]{:S(2)}) collective-permute-start(bf16[8,40,512]{2,1,0:T(8,128)(2,1)S(1)} %dynamic-slice_bitcast_fusion.1), channel_id=1, source_target_pairs={{0,2},{2,0},{4,6},{6,4},{8,10},{10,8},{12,14},{14,12},{16,18},{18,... | collective-permute-start | bytes 983048 | tf_op jit(solution)/shard_map/ppermute | solution.py:732
  116.9 0.8 copy-start.9
  117.0 1.0 copy-start.8
  117.0 1.1 copy-start.7
  117.0 1.3 copy-start.6
  179.1 4.5 %copy-start.3 = (f32[1024,640]{1,0:T(8,128)S(1)}, f32[1024,640]{1,0:T(8,128)}, u32[]{:S(2)}) copy-start(f32[1024,640]{1,0:T(8,128)} %get-tuple-element.120) | copy-start | bytes 7864324
  183.5 1.5 copy-start.14
  183.5 2.2 %copy-start.13 = (f32[40,512]{1,0:T(8,128)S(1)}, f32[40,512]{1,0:T(8,128)}, u32[]{:S(2)}) copy-start(f32[40,512]{1,0:T(8,128)} %get-tuple-element.125) | copy-start | bytes 245764
  183.5 2.8 %copy-start.12 = (f32[64,640]{1,0:T(8,128)S(1)}, f32[64,640]{1,0:T(8,128)}, u32[]{:S(2)}) copy-start(f32[64,640]{1,0:T(8,128)} %get-tuple-element.126) | copy-start | bytes 491524
  183.6 3.5 %copy-start.11 = (f32[64,640]{1,0:T(8,128)S(1)}, f32[64,640]{1,0:T(8,128)}, u32[]{:S(2)}) copy-start(f32[64,640]{1,0:T(8,128)} %get-tuple-element.127) | copy-start | bytes 491524
  183.6 4.1 %copy-start.10 = (f32[40,1024]{1,0:T(8,128)S(1)}, f32[40,1024]{1,0:T(8,128)}, u32[]{:S(2)}) copy-start(f32[40,1024]{1,0:T(8,128)} %get-tuple-element.128) | copy-start | bytes 491524

commit v5 on v4

--- a/solution.py
+++ b/solution.py
@@ -212,59 +212,46 @@
     gains[2:3, :] += jnp.sum(gmid * hat_attn, axis=0, keepdims=True)
 
 
-def attn_back_kernel(seg, q_o, q_x, k, v, ga_o, ga_x, lse, delta, ql_o, ql_x, cos, sin, rows8,
-                     qr_o, qr_x, dk_out, dv_out, front, gain, dk, dv):
-    (gq,) = gain_refs(rows8, 4)
-    i = pl.program_id(0)
-    rows = q_o.shape[0]
+def attn_rows(i, seg, buf, lse, delta, gq, qr_o, qr_x, dk, dv, gain):
+    rows = QB
     base = pl.multiple_of(i * rows, rows)
-
-    @pl.when(i == 0)
-    def _():
-        dk[...] = jnp.zeros_like(dk)
-        dv[...] = jnp.zeros_like(dv)
-        gain[...] = jnp.zeros_like(gain)
-
-    k_win = k[pl.ds(base, WIN), :]
-    v_win = v[pl.ds(base, WIN), :]
+    mine = pl.ds(base, rows)
+    k_win = buf["k"][pl.ds(base, WIN), :]
+    v_win = buf["v"][pl.ds(base, WIN), :]
     seg_k = column_of(seg[:, pl.ds(base, WIN)])[:, :1]
     seg_q = seg[:, pl.ds(base + BLOCK, rows)]
     lane = lax.broadcasted_iota(jnp.int32, (WIN, rows), 1)
     sub = lax.broadcasted_iota(jnp.int32, (WIN, rows), 0)
     mask = (seg_q == seg_k) & (sub <= lane + (WIN - rows))
+    cos = buf["cos"][mine, :]
+    sin = buf["sin"][mine, :]
     dk_sum = None
     dv_sum = None
     g_sum = None
-    heads = q_o.shape[1] // HEAD_WIDTH
+    heads = qr_o.shape[1] // HEAD_WIDTH
     for n in range(2 * heads):
-        q, ga, ql, qraw = ((q_o, ga_o, ql_o, qr_o), (q_x, ga_x, ql_x, qr_x))[n // heads]
+        side = "ox"[n // heads]
+        qraw = (qr_o, qr_x)[n // heads]
         h = n % heads
         cols = slice(h * HEAD_WIDTH, (h + 1) * HEAD_WIDTH)
-        qh = q[:, cols]
-        gh = ga[:, cols]
+        qh = buf["q_" + side][mine, cols]
+        gh = buf["ga_" + side][mine, cols]
         s = jnp.where(mask, nt(k_win, qh), -jnp.inf)
-        p = jnp.exp(s - lse[n : n + 1, :])
-        ds = (p * (nt(v_win, gh) - delta[n : n + 1, :])).astype(BF)
+        p = jnp.exp(s - lse[n : n + 1, mine])
+        ds = (p * (nt(v_win, gh) - delta[n : n + 1, mine])).astype(BF)
         dq = tn(ds, k_win) * SCORE_SCALE
         a = nn(ds, qh)
         b = nn(p.astype(BF), gh)
         dk_sum = a if dk_sum is None else dk_sum + a
         dv_sum = b if dv_sum is None else dv_sum + b
-        dqn = rotate(dq, cos[...], sin[...], -1)
-        hat, inv = rms_stats(ql[:, cols])
+        dqn = rotate(dq, cos, sin, -1)
+        hat, inv = rms_stats(buf["ql_" + side][mine, cols])
         g = jnp.sum(dqn * hat, axis=0, keepdims=True)
         g_sum = g if g_sum is None else g_sum + g
-        qraw[:, cols] = rms_back(hat, inv, gq[...], dqn).astype(BF)
+        qraw[mine, cols] = rms_back(hat, inv, gq, dqn).astype(BF)
     dk[pl.ds(base, WIN), :] += dk_sum
     dv[pl.ds(base, WIN), :] += dv_sum
     gain[...] += g_sum
-
-    @pl.when(i == pl.num_programs(0) - 1)
-    def _():
-        front[:, :HEAD_WIDTH] = dk[:BLOCK, :].astype(BF)
-        front[:, HEAD_WIDTH:] = dv[:BLOCK, :].astype(BF)
-        dk_out[...] = dk[BLOCK:, :]
-        dv_out[...] = dv[BLOCK:, :]
 
 
 def whole(shape):
@@ -360,29 +347,6 @@
     )(first_row, x3, up3, seg_ext, q_o, q_x, k, v, *weights, rows8)
 
 
-def attn_back(seg_ext, q_o, q_x, k, v, ga_o, ga_x, lse, delta, ql_o, ql_x, cos, sin, rows8):
-    own, part = q_o.shape
-    n = QB
-    ext = k.shape[0]
-    fixed = lambda shape: pl.BlockSpec(shape, lambda i: (0, 0))
-    stat = pl.BlockSpec((8, n), lambda i: (0, i))
-    return pl.pallas_call(
-        attn_back_kernel,
-        grid=(own // n,),
-        in_specs=[whole(seg_ext.shape), rows_of(n, part), rows_of(n, part), whole(k.shape), whole(v.shape),
-                  rows_of(n, part), rows_of(n, part), stat, stat, rows_of(n, part), rows_of(n, part),
-                  rows_of(n, LANES), rows_of(n, LANES), whole(rows8.shape)],
-        out_specs=[rows_of(n, part), rows_of(n, part), fixed((own, HEAD_WIDTH)), fixed((own, HEAD_WIDTH)),
-                   fixed((BLOCK, 2 * HEAD_WIDTH)), fixed((1, HEAD_WIDTH))],
-        out_shape=[sds((own, part), BF), sds((own, part), BF), sds((own, HEAD_WIDTH), F32),
-                   sds((own, HEAD_WIDTH), F32), sds((BLOCK, 2 * HEAD_WIDTH), BF), sds((1, HEAD_WIDTH), F32)],
-        scratch_shapes=[pltpu.VMEM((ext, HEAD_WIDTH), F32), pltpu.VMEM((ext, HEAD_WIDTH), F32)],
-        compiler_params=params(),
-        cost_estimate=cost(20),
-        name="attn_back",
-    )(seg_ext, q_o, q_x, k, v, ga_o, ga_x, lse, delta, ql_o, ql_x, cos, sin, rows8)
-
-
 def swap(value, n_tensor):
     return lax.ppermute(value, "tensor", [(t, n_tensor - 1 - t) for t in range(n_tensor)])
 
@@ -396,10 +360,6 @@
     turned = plain[1:] + plain[:1]
     lead = (plain[2],) + plain[:2] + plain[3:] if n_bits > 2 else plain[::-1]
     return plain, turned, lead
-
-
-def drop_bit(index, b):
-    return lax.div(index, 2 ** (b + 1)) * 2**b + lax.rem(index, 2**b)
 
 
 def natural_index(me, j, fixed, free):
@@ -412,24 +372,28 @@
     return index
 
 
+NAMES = ("x", "gmid", "wq_o", "wq_x", "wk", "wv", "kl", "cos", "sin", "nb", "k", "v", "q_o", "q_x", "ga_o", "ga_x",
+         "ql_o", "ql_x")
+
+
 def finish_kernel(items, kv_groups, n_bits, *refs):
     n_items = len(items)
     kv_order = sum(kv_groups, ())
     refs = list(refs)
     take = lambda count: [refs.pop(0) for _ in range(count)]
-    ins = [take(2) for _, given in items if given]
-    front, rows8, g_block, g_q = take(4)
-    far = take(14)
+    ins = [take(1) for _, early in items if early]
+    seg, lse, delta, rows8, g_block = take(5)
+    far = take(len(NAMES))
     outs = take(n_items)
     k_out, v_out, gain_out, gin_far = take(4)
-    near = take(14)
+    near = take(len(NAMES))
     local_sems = refs.pop(0)
-    front_got, kraw, vraw, kv_in, query_sent, query_got, query, gin, g_in, g_k = take(10)
+    (front, front_got, dk_all, dv_all, qr_o, qr_x, kraw, vraw, kv_in, query_sent, query_got, query,
+     g_in, g_k, g_q) = take(15)
     ins.append([query])
     recvs, curs = [], []
-    for order, given in items:
-        first = 1 if given else 0
-        recvs.append({s: refs.pop(0) for s in range(first, n_bits)})
+    for _ in items:
+        recvs.append({s: refs.pop(0) for s in range(n_bits)})
         curs.append({s: refs.pop(0) for s in range(1, n_bits)})
     kv_core = refs.pop(0)
     kv_recv = take(len(kv_groups))
@@ -482,12 +446,11 @@
             flying[n] = [send(curs[n][s].at[pl.ds(away, half)], recvs[n][s], device)]
 
     def finish(n, s):
-        order, given = items[n]
+        order, _ = items[n]
         half = 2 ** (n_bits - s - 1)
-        for copy in flying.pop(n, ()):
+        for copy in flying.pop(n):
             copy.wait_recv()
-        outside = given and s == 0
-        got = ins[n][1] if outside else recvs[n][s]
+        got = recvs[n][s]
         held = curs[n][s] if s else ins[n][0]
 
         def total_at(j):
@@ -495,7 +458,7 @@
                 index = bit_of(me, order[s]) * half + j
             else:
                 index = natural_index(me, j, ((order[0], False),), order[1:])
-            return held[index].astype(F32) + got[drop_bit(index, order[0]) if outside else j].astype(F32)
+            return held[index].astype(F32) + got[j].astype(F32)
 
         if s == n_bits - 1:
             outs[n][...] = total_at(0)
@@ -509,25 +472,43 @@
         start(n, s + 1)
 
     other_core = {"tensor": 1 - core}
-    own, depth = gin.shape
+    own, depth = near[0].shape
     sources = list(far)
     sources[0] = far[0].at[0, pl.ds(pl.multiple_of(core * own, own), own), :]
-    names = ("x", "gmid", "wq_o", "wq_x", "wk", "wv", "dk", "dv", "kl", "cos", "sin", "qr_o", "qr_x", "nb")
+    buf = dict(zip(NAMES, near))
     fetch = {name: pltpu.make_async_copy(s, d, local_sems.at[k])
-             for k, (name, s, d) in enumerate(zip(names, sources, near))}
-    buf = dict(zip(names, near))
-    for name in ("nb", "qr_x", "dk", "dv", "kl", "cos", "sin", "qr_o", "wk", "wv", "wq_o", "wq_x", "x", "gmid"):
+             for k, (name, s, d) in enumerate(zip(NAMES, sources, near))}
+    first_use = ("k", "v", "q_o", "ga_o", "cos", "sin", "ql_o", "q_x", "ga_x", "ql_x")
+    second_use = ("nb", "kl", "wk", "wv", "wq_o", "wq_x", "x", "gmid")
+    for name in first_use:
         fetch[name].start()
+    for n in range(n_items):
+        if items[n][1]:
+            start(n, 0)
+    for name in second_use:
+        fetch[name].start()
+    dk_all[...] = jnp.zeros_like(dk_all)
+    dv_all[...] = jnp.zeros_like(dv_all)
+    g_q[...] = jnp.zeros_like(g_q)
+    gq_row = rows8[4:5, :HEAD_WIDTH]
+    for name in first_use:
+        fetch[name].wait()
+
+    def attn_body(i, carry):
+        attn_rows(i, seg, buf, lse, delta, gq_row, qr_o, qr_x, dk_all, dv_all, g_q)
+        return carry
+
+    lax.fori_loop(0, own // QB, attn_body, 0)
+    front[:, :HEAD_WIDTH] = dk_all[:BLOCK, :].astype(BF)
+    front[:, HEAD_WIDTH:] = dv_all[:BLOCK, :].astype(BF)
     front_copy = send(front, front_got, other_core)
+    fetch["nb"].wait()
+    query_sent[...] = tn(qr_x[...], buf["nb"][...]).astype(BF)
+    query_copy = send(query_sent, query_got, other_core)
     for n in range(n_items):
         if items[n][1]:
             finish(n, 0)
-    fetch["nb"].wait()
-    fetch["qr_x"].wait()
-    query_sent[...] = tn(buf["qr_x"][...], buf["nb"][...]).astype(BF)
-    query_copy = send(query_sent, query_got, other_core)
-    for name in ("dk", "dv", "kl", "cos", "sin"):
-        fetch[name].wait()
+    fetch["kl"].wait()
     front_copy.wait_recv()
     gk_row, gin_row = rows8[5:6, :HEAD_WIDTH], rows8[0:1, :]
     g_k[...] = jnp.zeros_like(g_k)
@@ -537,8 +518,9 @@
     def kv_rows(i, carry):
         at = pl.ds(pl.multiple_of(i * BLOCK, BLOCK), BLOCK)
         tail = ((i == blocks - 1) & (core == 0)).astype(F32)
-        dk = buf["dk"][at, :] + tail * front_got[:, :HEAD_WIDTH].astype(F32)
-        dv = buf["dv"][at, :] + tail * front_got[:, HEAD_WIDTH:].astype(F32)
+        later = pl.ds(pl.multiple_of((i + 1) * BLOCK, BLOCK), BLOCK)
+        dk = dk_all[later, :] + tail * front_got[:, :HEAD_WIDTH].astype(F32)
+        dv = dv_all[later, :] + tail * front_got[:, HEAD_WIDTH:].astype(F32)
         dkn = rotate(dk, buf["cos"][at, :], buf["sin"][at, :], -1)
         k_hat, k_inv = rms_stats(buf["kl"][at, :])
         kraw[at, :] = rms_back(k_hat, k_inv, gk_row, dkn).astype(BF)
@@ -551,9 +533,8 @@
     for t, raw in enumerate((kraw, vraw)):
         kv_in[t] = tn(raw[...], buf["nb"][...]).astype(BF).reshape(n_chunk, rows_k, depth)
     kv_copies = [send(kv_in.at[1 - core], kv_core, other_core)]
-    fetch["qr_o"].wait()
     query_copy.wait_recv()
-    own_query = tn(buf["qr_o"][...], buf["nb"][...]) + query_got[...].astype(F32)
+    own_query = tn(qr_o[...], buf["nb"][...]) + query_got[...].astype(F32)
     query[...] = own_query.astype(BF).reshape(query.shape)
     start(n_items - 1, 0)
     def gain_start(s):
@@ -594,14 +575,14 @@
     def input_rows(i, carry):
         at = pl.ds(pl.multiple_of(i * QB, QB), QB)
         gn = nt(kraw[at, :], buf["wk"][...]) + nt(vraw[at, :], buf["wv"][...])
-        gn = gn + nt(buf["qr_o"][at, :], buf["wq_o"][...]) + nt(buf["qr_x"][at, :], buf["wq_x"][...])
+        gn = gn + nt(qr_o[at, :], buf["wq_o"][...]) + nt(qr_x[at, :], buf["wq_x"][...])
         hat, inv = rms_stats(buf["x"][at, :])
-        gin[at, :] = buf["gmid"][at, :] + rms_back(hat, inv, gin_row, gn)
+        buf["x"][at, :] = buf["gmid"][at, :] + rms_back(hat, inv, gin_row, gn)
         g_in[...] += jnp.sum(gn * hat, axis=0, keepdims=True)
         return carry
 
     lax.fori_loop(0, own // QB, input_rows, 0)
-    gin_copy = pltpu.make_async_copy(gin, gin_far, local_sems.at[len(names)])
+    gin_copy = pltpu.make_async_copy(buf["x"], gin_far, local_sems.at[len(NAMES)])
     gin_copy.start()
     gain_own[0][...] = jnp.zeros_like(gain_own[0])
     gain_own[0][0:3, :] = g_block[0:3, :]
@@ -678,24 +659,24 @@
         copy.wait_send()
 
 
-def finish_all(n_dp, items, order, kv_order, front, rows8, g_block, g_q, far):
+def finish_all(n_dp, items, order, kv_order, small, far):
     n_bits = len(kv_order)
-    own, part = far[11].shape
+    own, part = far[12].shape
+    ext = far[10].shape[0]
     depth = far[1].shape[1]
     groups = tuple(tuple(kv_order[k : k + 2]) for k in range(0, n_bits, 2))
     spec, operands, outs, comm = [], [], [], []
     copies = 3
-    shapes = [value.shape for value, _, _ in items] + [(n_dp, part // n_dp, depth)]
+    shapes = [value.shape for value, _ in items] + [(n_dp, part // n_dp, depth)]
     for k, (n, c, width) in enumerate(shapes):
-        given = k < len(items)
-        spec.append((tuple(items[k][2] if given else order), given))
-        if given:
-            operands += [items[k][0], items[k][1]]
+        early = k < len(items)
+        spec.append((tuple(items[k][1] if early else order), early))
+        if early:
+            operands.append(items[k][0])
         outs.append(sds((c, width), F32))
-        first = 1 if given else 0
-        comm += [pltpu.VMEM((2 ** (n_bits - s - 1), c, width), BF) for s in range(first, n_bits)]
+        comm += [pltpu.VMEM((2 ** (n_bits - s - 1), c, width), BF) for s in range(n_bits)]
         comm += [pltpu.VMEM((2 ** (n_bits - s), c, width), BF) for s in range(1, n_bits)]
-        copies += n_bits - 1 + (0 if given else n // 2)
+        copies += n_bits - 1 + n // 2
     n, c, width = n_dp, HEAD_WIDTH // n_dp, depth
     comm += [pltpu.VMEM((n, c, width), BF)]
     sizes = [2 ** (n_bits - sum(len(x) for x in groups[:g])) for g in range(len(groups) + 1)]
@@ -709,14 +690,17 @@
     near = [pltpu.VMEM((own, depth), F32)] + [pltpu.VMEM(a.shape, a.dtype) for a in far[1:]]
     scratch = near + [
         pltpu.SemaphoreType.DMA((len(far) + 1,)),
-        pltpu.VMEM(front.shape, BF), pltpu.VMEM((own, HEAD_WIDTH), BF), pltpu.VMEM((own, HEAD_WIDTH), BF),
+        pltpu.VMEM((BLOCK, 2 * HEAD_WIDTH), BF), pltpu.VMEM((BLOCK, 2 * HEAD_WIDTH), BF),
+        pltpu.VMEM((ext, HEAD_WIDTH), F32), pltpu.VMEM((ext, HEAD_WIDTH), F32),
+        pltpu.VMEM((own, part), BF), pltpu.VMEM((own, part), BF),
+        pltpu.VMEM((own, HEAD_WIDTH), BF), pltpu.VMEM((own, HEAD_WIDTH), BF),
         pltpu.VMEM((2, n, c, width), BF), pltpu.VMEM((part, depth), BF), pltpu.VMEM((part, depth), BF),
-        pltpu.VMEM((n_dp, part // n_dp, depth), BF), pltpu.VMEM((own, depth), F32), pltpu.VMEM((1, depth), F32),
-        pltpu.VMEM((1, HEAD_WIDTH), F32),
+        pltpu.VMEM((n_dp, part // n_dp, depth), BF), pltpu.VMEM((1, depth), F32),
+        pltpu.VMEM((1, HEAD_WIDTH), F32), pltpu.VMEM((1, HEAD_WIDTH), F32),
     ] + comm
     vmem = pl.BlockSpec(memory_space=pltpu.VMEM)
     anywhere = pl.BlockSpec(memory_space=pl.ANY)
-    operands += [front, rows8, g_block, g_q]
+    operands += list(small)
     return pl.pallas_call(
         functools.partial(finish_kernel, tuple(spec), groups, n_bits),
         out_shape=outs,
@@ -728,20 +712,8 @@
     )(*operands, *far)
 
 
-def hop(value, b, n_dp):
-    return lax.ppermute(value, "dp", [(i, i ^ 2**b) for i in range(n_dp)])
-
-
 def after(value, *others):
     return lax.optimization_barrier((value,) + others)[0]
-
-
-def first_hop(value, b, n_dp):
-    n, c, width = value.shape
-    away = 1 - bit_of(lax.axis_index("dp"), b)
-    view = value.reshape(n // 2 ** (b + 1), 2, 2**b, c, width)
-    sent = lax.dynamic_index_in_dim(view, away, 1, keepdims=False).reshape(n // 2, c, width)
-    return hop(sent, b, n_dp), sent
 
 
 def on_device(n_dp, n_tensor, residual_in, cotangent, segment_ids, gain_attn_in, w_query, w_key, w_value,
@@ -769,33 +741,21 @@
     n_bits = n_dp.bit_length() - 1
     plain, turned, lead = bit_orders(n_bits)
     chunks = lambda value: value.reshape(n_dp, value.shape[0] // n_dp, value.shape[1])
-    spot = lax.axis_index("dp").astype(jnp.int32).reshape(1)
 
     pairs = [(gff, act_x, act_o, plain), (mid_b, gg_x, gg_o, turned), (mid_b, gu_x, gu_o, lead), (gas, af_x, af_o, plain)]
     grad = lambda left, units: tn(left, units) if left is not mid_b else tn(units, left)
-    orders = [order for *_, order in pairs]
     gots = []
     last = ()
     for left, units, _, _ in pairs:
         sent = grad(left, after(units, *last)).astype(BF)
         last = (sent,)
         gots.append(swap(sent, n_tensor))
-    state = []
+    items = []
     for (left, _, units, order), got in zip(pairs, gots):
-        value = chunks((grad(left, after(units, *last)) + got.astype(F32)).astype(BF))
-        arrived, away = first_hop(value, order[0], n_dp)
-        last = (away,)
-        state.append((value, arrived))
-
-    ga_o = after(ga_o, *last)
-    qr_o, qr_x, dk, dv, front, gain_q = attn_back(
-        seg_ext, q_o, q_x, k, v, ga_o, ga_x, lse, delta, ql_o, ql_x, cos, sin, rows8)
-    front, qr_x, *arrived = lax.optimization_barrier((front, qr_x, *(got for _, got in state)))
-    state = [(value, got) for (value, _), got in zip(state, arrived)]
-    items = [(value, got, order) for (value, got), order in zip(state, orders)]
-    far = (residual_in, gmid, w_query, wq_x, w_key, w_value, dk, dv, kl, cos, sin, qr_o, qr_x, nb)
+        items.append((chunks((grad(left, after(units, *last)) + got.astype(F32)).astype(BF)), order))
+    far = (residual_in, gmid, w_query, wq_x, w_key, w_value, kl, cos, sin, nb, k, v, q_o, q_x, ga_o, ga_x, ql_o, ql_x)
     *shares, k_sum, v_sum, gain_sum, grad_input = finish_all(
-        n_dp, items, plain, plain, front, rows8, gains, gain_q, far)
+        n_dp, items, plain, plain, (seg_ext, lse, delta, rows8, gains), far)
     s_down, s_gate, s_up, s_out, s_query = shares
     k_sum = k_sum.reshape(HEAD_WIDTH, depth)
     v_sum = v_sum.reshape(HEAD_WIDTH, depth)

time: 189 us -> 187 us (0.989)
  local copies, waits for them, and re-layouts: 25.9 us -> 20.6 us
  starting transfers between devices: 7.58 us -> 2.32 us
  Pallas kernels: 136 us -> 141 us
  matrix products: 16.4 us -> 18.5 us
  waiting for transfers between devices: 0.03 us -> 2.08 us
    pallas_call x1, Pallas kernels: 57.9 us -> 80.6 us  [finish_all(): pl.pallas_call(functools.partial(finish_kernel, tuple(spec), groups, n_bi...]
    pallas_call x1 -> x0, Pallas kernels: 18 us -> none  [attn_back(): pl.pallas_call(attn_back_kernel, grid=(own // n,), in_specs=[whole(seg_ex...]
    ppermute x4 -> x0, starting transfers between devices: 5.13 us -> none  [hop(): return lax.ppermute(value, 'dp', [(i, i ^ 2 ** b) for i in range(n_dp)])]
    unnamed x58 -> x44, local copies, waits for them, and re-layouts: 9.4 us -> 7.15 us
    dot_general x8, matrix products: 16.4 us -> 18.5 us  [tn(): lax.dot_general(a, b, (((0,), (0,)), ((), ())), preferred_element_type=F32)]
    ppermute x9, waiting for transfers between devices: 0.02 us -> 2.08 us  [swap(): lax.ppermute(value, 'tensor', [(t, n_tensor - 1 - t) for t in range(n_ten...]
    dynamic_slice x2 -> x0, local copies, waits for them, and re-layouts: 1.96 us -> none  [first_hop(): lax.dynamic_index_in_dim(view, away, 1, keepdims=False)]
  transfers between devices with their start and end apart: 13 -> 9, of which waited for: 0 -> 1; matrix products, arithmetic and copies ran while one was open for 12% -> 9% of each run, Pallas kernels for 15% -> 6%
where the time goes in v5:
time: 187 us
  Pallas kernels  141 us (75%)
  local copies, waits for them, and re-layouts  20.6 us (11%)
  matrix products  18.5 us (10%)
  starting transfers between devices  2.32 us (1%)
  waiting for transfers between devices  2.08 us (1%)
    pallas_call x1, Pallas kernels, finish_all(): pl.pallas_call(functools.partial(finish_kernel, tuple(spec), groups, n_bi...  80.6 us
    pallas_call x1, Pallas kernels, block_pass(): pl.pallas_call(kern, grid_spec=pltpu.PrefetchScalarGridSpec(num_scalar_pr...  49.2 us
    dot_general x8, matrix products, tn(): lax.dot_general(a, b, (((0,), (0,)), ((), ())), preferred_element_type=F32)  18.5 us
    pallas_call x1, Pallas kernels, project(): pl.pallas_call(project_kernel, grid_spec=pltpu.PrefetchScalarGridSpec(num...  11 us
    unnamed x44, local copies, waits for them, and re-layouts  7.15 us
  transfers between devices with their start and end apart: 9, of which 1 were waited for; matrix products, arithmetic and copies ran while one was open for 9% of the time, Pallas kernels for 6%

profile of v5, /device:TPU:1, one launch (start us, length us, event | category | flops | bytes accessed | tf_op | source)
XLA Modules:
  0.0 186.6 jit_solution(3864725643683744004)
XLA Ops:
  0.6 0.1 collective-permute-start.2
  0.7 0.5 collective-permute-start.3
  1.2 0.1 collective-permute-start.4
  1.3 0.4 collective-permute-start
  1.7 0.1 collective-permute-start.1
  1.8 0.7 stack.24
  2.5 0.7 stack.25
  3.2 0.7 stack.26
  3.9 0.7 stack.27
  4.6 0.7 pad.8
  5.3 0.7 pad.9
  5.9 0.8 pad_dynamic-slice_fusion
  6.7 0.6 broadcast_in_dim.14.seg.refs_2_.refs_4_
  7.3 0.6 stack.31.rows8.refs_15_.refs_7_
  8.0 1.4 convert_reduce_fusion
  9.4 0.0 collective-permute-done.wq_x.refs_12_
  9.4 0.8 copy-done.1
  10.2 11.0 %project.1 = (bf16[1024,512]{1,0:T(8,128)(2,1)}, bf16[1024,512]{1,0:T(8,128)(2,1)}, f32[1024,512]{1,0:T(8,128)}, f32[1024,512]{1,0:T(8,128)}, bf16[1536,256]{1,0...) custom-call(s32[1]{0:T(128)} %bitcast.me, ...), custom_call_target="tpu_custom_call" | custom-call | flops 6000000000 | bytes 6000000 | tf_op jit(solution)/shard_map/project/pallas_call | solution.py:286
  21.2 0.0 collective-permute-done.1.refs_8_
  21.2 0.0 collective-permute-done.2.refs_10_
  21.2 0.0 copy-start.7
  21.2 0.0 collective-permute-done.3.refs_12_
  21.2 0.0 copy-start.8
  21.2 0.0 collective-permute-done.4.refs_14_
  21.3 1.1 copy-done.7
  22.3 0.4 copy-done.8
  22.7 49.2 %block.1 = (f32[1024,640]{1,0:T(8,128)}, f32[1024,640]{1,0:T(8,128)}, bf16[1024,512]{1,0:T(8,128)(2,1)}, bf16[1024,512]{1,0:T(8,128)(2,1)}, bf16[1024,512]{1,0:T...) custom-call(s32[1]{0:T(128)} %bitcast.me, ...), custom_call_target="tpu_custom_call" | custom-call | flops 40000000000 | bytes 40000000 | tf_op jit(solution)/shard_map/block/pallas_call | solution.py:324
  71.9 0.0 copy-start.15
  71.9 3.7 %convolution_convert_fusion.2 = bf16[640,1024]{1,0:T(8,128)(2,1)S(1)} fusion(bf16[1024,640]{1,0:T(8,128)(2,1)} %get-tuple-element.64, bf16[1024,1024]{1,0:T(8,128)(2,1)} %get-tuple-element.70), kind=kOutput, calls=%fused_computation.5 | convolution fusion | flops 1342832640 | bytes 4718592 | tf_op jit(solution)/shard_map/dot_general | solution.py:35
  75.6 1.9 %convolution_convert_fusion.1 = bf16[1024,640]{1,0:T(8,128)(2,1)S(1)} fusion(bf16[1024,1024]{1,0:T(8,128)(2,1)S(1)} %copy-done.15, bf16[1024,640]{1,0:T(8,128)(2,1)S(1)} %copy-done.16), kind=kOutput, calls=%fused_computation.4 | convolution fusion | flops 1342832640 | bytes 4718592 | tf_op jit(solution)/shard_map/dot_general | solution.py:35
  77.5 0.0 copy-done.14
  77.5 0.0 copy-start.9
  77.5 0.0 copy-start.11
  77.5 1.9 %convolution_convert_fusion = bf16[1024,640]{1,0:T(8,128)(2,1)S(1)} fusion(bf16[1024,1024]{1,0:T(8,128)(2,1)S(1)} %copy-done.14, bf16[1024,640]{1,0:T(8,128)(2,1)S(1)} %copy-done.16), kind=kOutput, calls=%fused_computation.3 | convolution fusion | flops 1342832640 | bytes 4718592 | tf_op jit(solution)/shard_map/dot_general | solution.py:35
  79.4 0.5 collective-permute-start.7
  79.9 0.0 copy-done.11
  79.9 0.9 convolution_convert_fusion.3
  80.8 0.1 collective-permute-start.8
  80.9 0.4 collective-permute-start.6
  81.4 0.1 collective-permute-start.5
  81.5 2.1 %collective-permute-done.8 = bf16[640,512]{1,0:T(8,128)(2,1)S(1)} collective-permute-done((bf16[640,512]{1,0:T(8,128)(2,1)S(1)}, bf16[640,512]{1,0:T(8,128)(2,1)S(1)}, u32[]{:S(2)}, u32[]{:S(2)}) %collective-permute-start.8) | collective-permute-done | bytes 655392 | tf_op jit(solution)/shard_map/ppermute | solution.py:351
  83.5 0.0 copy-done.10
  83.5 1.7 fusion
  85.2 0.0 collective-permute-done.7
  85.3 2.9 %add_convert_fusion = bf16[1024,640]{1,0:T(8,128)(2,1)} fusion(bf16[1024,640]{1,0:T(8,128)(2,1)S(1)} %collective-permute-done.7, bf16[1024,1024]{1,0:T(8,128)(2,1)S(1)} %copy-done.13, bf16[1024,640]{1,0:T(8,128)(2,1)S(1)} %copy-done.16), kind=kOutput, calls=%fused_computation | convolution fusion | flops 1344143360 | bytes 6029312 | tf_op jit(solution)/shard_map/dot_general | solution.py:35
  88.2 0.0 collective-permute-done.6
  88.2 3.0 %add_convert_fusion.1 = bf16[1024,640]{1,0:T(8,128)(2,1)} fusion(bf16[1024,640]{1,0:T(8,128)(2,1)S(1)} %collective-permute-done.6, bf16[1024,1024]{1,0:T(8,128)(2,1)S(1)} %copy-done.12, bf16[1024,640]{1,0:T(8,128)(2,1)S(1)} %copy-done.16), kind=kOutput, calls=%fused_computation.1 | convolution fusion | flops 1344143360 | bytes 6029312 | tf_op jit(solution)/shard_map/dot_general | solution.py:35
  91.2 0.0 collective-permute-done.5
  91.2 0.0 copy-done.17
  91.2 2.7 %add_convert_fusion.2 = bf16[640,1024]{1,0:T(8,128)(2,1)} fusion(bf16[640,1024]{1,0:T(8,128)(2,1)S(1)} %collective-permute-done.5, bf16[1024,640]{1,0:T(8,128)(2,1)S(1)} %copy-done.18, bf16[1024,1024]{1,0:T(8,128)(2,1)S(1)} %copy-done.17), kind=kOutput, calls=%fused_computation.2 | convolution fusion | flops 1344143360 | bytes 6029312 | tf_op jit(solution)/shard_map/dot_general | solution.py:35
  93.8 80.6 %finish_all.1 = (f32[40,1024]{1,0:T(8,128)}, f32[64,640]{1,0:T(8,128)}, f32[64,640]{1,0:T(8,128)}, f32[40,512]{1,0:T(8,128)}, f32[32,640]{1,0:T(8,128)}, /*index...) custom-call(bf16[16,40,1024]{2,1,0:T(8,128)(2,1)} %bitcast.39, ...), custom_call_target="tpu_custom_call" | custom-call | tf_op jit(solution)/shard_map/finish_all/pallas_call | solution.py:704
  174.5 1.3 fusion.1
  175.8 1.5 slice_reduce_fusion
  177.3 2.3 %copy.34 = f32[256,640]{0,1:T(8,128)} copy(f32[256,640]{1,0:T(8,128)} %bitcast.43) | data formatting | bytes 1310720 | tf_op jit(solution)/shard_map/reshape | solution.py:760
  179.6 2.2 %copy.35 = f32[256,640]{0,1:T(8,128)} copy(f32[256,640]{1,0:T(8,128)} %bitcast.42) | data formatting | bytes 1310720 | tf_op jit(solution)/shard_map/reshape | solution.py:761
  181.8 0.0 copy-start.3
  181.8 0.0 copy-start.2
  181.8 1.5 copy.42
  183.3 0.6 copy.43
  183.9 0.6 copy.44
  184.6 0.0 copy-done.4
  184.6 0.7 copy.45
  185.3 0.7 copy.46
  185.9 0.7 copy.47
  (26 shorter events, 0.1 us)
Async XLA Ops:
  0.6 20.6 %collective-permute-start.2 = (bf16[640,1024]{1,0:T(8,128)(2,1)}, bf16[640,1024]{1,0:T(8,128)(2,1)S(1)}, u32[]{:S(2)}, u32[]{:S(2)}) collective-permute-start(bf16[640,1024]{1,0:T(8,128)(2,1)} %refs_9_.2), channel_id=1, source_target_pairs={{0,1},{1,0},{2,3},{3,2},{4,5},{5,4},{6,7},{7,6},{8,9},{9,8},{10,11... | collective-permute-start | bytes 3932168 | tf_op jit(solution)/shard_map/ppermute | solution.py:351
  0.7 20.5 %collective-permute-start.3 = (bf16[640,1024]{1,0:T(8,128)(2,1)}, bf16[640,1024]{1,0:T(8,128)(2,1)S(1)}, u32[]{:S(2)}, u32[]{:S(2)}) collective-permute-start(bf16[640,1024]{1,0:T(8,128)(2,1)} %refs_11_.2), channel_id=1, source_target_pairs={{0,1},{1,0},{2,3},{3,2},{4,5},{5,4},{6,7},{7,6},{8,9},{9,8},{10,11... | collective-permute-start | bytes 3932168 | tf_op jit(solution)/shard_map/ppermute | solution.py:351
  1.2 20.0 %collective-permute-start.4 = (bf16[1024,640]{1,0:T(8,128)(2,1)}, bf16[1024,640]{1,0:T(8,128)(2,1)}, u32[]{:S(2)}, u32[]{:S(2)}) collective-permute-start(bf16[1024,640]{1,0:T(8,128)(2,1)} %refs_13_.2), channel_id=1, source_target_pairs={{0,1},{1,0},{2,3},{3,2},{4,5},{5,4},{6,7},{7,6},{8,9},{9,8},{10,11... | collective-permute-start | bytes 3932168 | tf_op jit(solution)/shard_map/ppermute | solution.py:351
  1.3 8.1 %collective-permute-start = (bf16[640,512]{1,0:T(8,128)(2,1)}, bf16[640,512]{1,0:T(8,128)(2,1)S(1)}, u32[]{:S(2)}, u32[]{:S(2)}) collective-permute-start(bf16[640,512]{1,0:T(8,128)(2,1)} %refs_11_.3), channel_id=1, source_target_pairs={{0,1},{1,0},{2,3},{3,2},{4,5},{5,4},{6,7},{7,6},{8,9},{9,8},{10,11... | collective-permute-start | bytes 1966088 | tf_op jit(solution)/shard_map/ppermute | solution.py:351
  1.7 19.5 %collective-permute-start.1 = (bf16[512,640]{1,0:T(8,128)(2,1)}, bf16[512,640]{1,0:T(8,128)(2,1)}, u32[]{:S(2)}, u32[]{:S(2)}) collective-permute-start(bf16[512,640]{1,0:T(8,128)(2,1)} %refs_7_.1), channel_id=1, source_target_pairs={{0,1},{1,0},{2,3},{3,2},{4,5},{5,4},{6,7},{7,6},{8,9},{9,8},{10,11... | collective-permute-start | bytes 1966088 | tf_op jit(solution)/shard_map/ppermute | solution.py:351
  9.4 0.8 copy-start.1
  21.2 1.1 copy-start.7
  21.2 1.5 copy-start.8
  71.9 3.7 %copy-start.15 = (bf16[1024,1024]{1,0:T(8,128)(2,1)S(1)}, bf16[1024,1024]{1,0:T(8,128)(2,1)}, u32[]{:S(2)}) copy-start(bf16[1024,1024]{1,0:T(8,128)(2,1)} %get-tuple-element.71) | copy-start | bytes 6291460
  71.9 3.7 %copy-start.16 = (bf16[1024,640]{1,0:T(8,128)(2,1)S(1)}, bf16[1024,640]{1,0:T(8,128)(2,1)}, u32[]{:S(2)}) copy-start(bf16[1024,640]{1,0:T(8,128)(2,1)} %get-tuple-element.72) | copy-start | bytes 3932164
  75.6 1.9 %copy-start.14 = (bf16[1024,1024]{1,0:T(8,128)(2,1)S(1)}, bf16[1024,1024]{1,0:T(8,128)(2,1)}, u32[]{:S(2)}) copy-start(bf16[1024,1024]{1,0:T(8,128)(2,1)} %get-tuple-element.73) | copy-start | bytes 6291460
  77.5 2.4 %copy-start.9 = (bf16[1024,640]{1,0:T(8,128)(2,1)S(1)}, bf16[1024,640]{1,0:T(8,128)(2,1)}, u32[]{:S(2)}) copy-start(bf16[1024,640]{1,0:T(8,128)(2,1)} %get-tuple-element.66) | copy-start | bytes 3932164
  77.5 2.4 %copy-start.11 = (bf16[1024,512]{1,0:T(8,128)(2,1)S(1)}, bf16[1024,512]{1,0:T(8,128)(2,1)}, u32[]{:S(2)}) copy-start(bf16[1024,512]{1,0:T(8,128)(2,1)} %get-tuple-element.74) | copy-start | bytes 3145732
  79.4 5.8 %collective-permute-start.7 = (bf16[1024,640]{1,0:T(8,128)(2,1)S(1)}, bf16[1024,640]{1,0:T(8,128)(2,1)S(1)}, u32[]{:S(2)}, u32[]{:S(2)}) collective-permute-start(bf16[1024,640]{1,0:T(8,128)(2,1)S(1)} %convolution_convert_fusion), channel_id=1, source_target_pairs={{0,1},{1,0},{2,3},{3,2},{4,5},{5,4},{6,7},{7,6},{8,9},{9,8},{10,11... | collective-permute-start | bytes 3932168 | tf_op jit(solution)/shard_map/ppermute | solution.py:351
  79.9 3.6 %copy-start.10 = (bf16[1024,512]{1,0:T(8,128)(2,1)S(1)}, bf16[1024,512]{1,0:T(8,128)(2,1)}, u32[]{:S(2)}) copy-start(bf16[1024,512]{1,0:T(8,128)(2,1)} %get-tuple-element.81) | copy-start | bytes 3145732
  80.8 2.7 %collective-permute-start.8 = (bf16[640,512]{1,0:T(8,128)(2,1)S(1)}, bf16[640,512]{1,0:T(8,128)(2,1)S(1)}, u32[]{:S(2)}, u32[]{:S(2)}) collective-permute-start(bf16[640,512]{1,0:T(8,128)(2,1)S(1)} %convolution_convert_fusion.3), channel_id=1, source_target_pairs={{0,1},{1,0},{2,3},{3,2},{4,5},{5,4},{6,7},{7,6},{8,9},{9,8},{10,11... | collective-permute-start | bytes 1966088 | tf_op jit(solution)/shard_map/ppermute | solution.py:351
  80.9 7.3 %collective-permute-start.6 = (bf16[1024,640]{1,0:T(8,128)(2,1)S(1)}, bf16[1024,640]{1,0:T(8,128)(2,1)S(1)}, u32[]{:S(2)}, u32[]{:S(2)}) collective-permute-start(bf16[1024,640]{1,0:T(8,128)(2,1)S(1)} %convolution_convert_fusion.1), channel_id=1, source_target_pairs={{0,1},{1,0},{2,3},{3,2},{4,5},{5,4},{6,7},{7,6},{8,9},{9,8},{10,11... | collective-permute-start | bytes 3932168 | tf_op jit(solution)/shard_map/ppermute | solution.py:351
  81.4 9.8 %collective-permute-start.5 = (bf16[640,1024]{1,0:T(8,128)(2,1)S(1)}, bf16[640,1024]{1,0:T(8,128)(2,1)S(1)}, u32[]{:S(2)}, u32[]{:S(2)}) collective-permute-start(bf16[640,1024]{1,0:T(8,128)(2,1)S(1)} %convolution_convert_fusion.2), channel_id=1, source_target_pairs={{0,1},{1,0},{2,3},{3,2},{4,5},{5,4},{6,7},{7,6},{8,9},{9,8},{10,11... | collective-permute-start | bytes 3932168 | tf_op jit(solution)/shard_map/ppermute | solution.py:351
  81.4 3.8 %copy-start.13 = (bf16[1024,1024]{1,0:T(8,128)(2,1)S(1)}, bf16[1024,1024]{1,0:T(8,128)(2,1)}, u32[]{:S(2)}) copy-start(bf16[1024,1024]{1,0:T(8,128)(2,1)} %get-tuple-element.79) | copy-start | bytes 6291460
  85.2 2.9 %copy-start.12 = (bf16[1024,1024]{1,0:T(8,128)(2,1)S(1)}, bf16[1024,1024]{1,0:T(8,128)(2,1)}, u32[]{:S(2)}) copy-start(bf16[1024,1024]{1,0:T(8,128)(2,1)} %get-tuple-element.77) | copy-start | bytes 6291460
  88.2 3.0 %copy-start.17 = (bf16[1024,1024]{1,0:T(8,128)(2,1)S(1)}, bf16[1024,1024]{1,0:T(8,128)(2,1)}, u32[]{:S(2)}) copy-start(bf16[1024,1024]{1,0:T(8,128)(2,1)} %get-tuple-element.75) | copy-start | bytes 6291460
  88.2 3.0 %copy-start.18 = (bf16[1024,640]{1,0:T(8,128)(2,1)S(1)}, bf16[1024,640]{1,0:T(8,128)(2,1)}, u32[]{:S(2)}) copy-start(bf16[1024,640]{1,0:T(8,128)(2,1)} %get-tuple-element.64) | copy-start | bytes 3932164
  177.3 4.5 %copy-start = (f32[1024,640]{1,0:T(8,128)S(1)}, f32[1024,640]{1,0:T(8,128)}, u32[]{:S(2)}) copy-start(f32[1024,640]{1,0:T(8,128)} %get-tuple-element.94) | copy-start | bytes 7864324
  181.8 1.5 copy-start.6
  181.8 2.2 %copy-start.5 = (f32[40,512]{1,0:T(8,128)S(1)}, f32[40,512]{1,0:T(8,128)}, u32[]{:S(2)}) copy-start(f32[40,512]{1,0:T(8,128)} %get-tuple-element.99) | copy-start | bytes 245764
  181.8 2.8 %copy-start.4 = (f32[64,640]{1,0:T(8,128)S(1)}, f32[64,640]{1,0:T(8,128)}, u32[]{:S(2)}) copy-start(f32[64,640]{1,0:T(8,128)} %get-tuple-element.100) | copy-start | bytes 491524
  181.8 3.5 %copy-start.3 = (f32[64,640]{1,0:T(8,128)S(1)}, f32[64,640]{1,0:T(8,128)}, u32[]{:S(2)}) copy-start(f32[64,640]{1,0:T(8,128)} %get-tuple-element.101) | copy-start | bytes 491524
  181.8 4.1 %copy-start.2 = (f32[40,1024]{1,0:T(8,128)S(1)}, f32[40,1024]{1,0:T(8,128)}, u32[]{:S(2)}) copy-start(f32[40,1024]{1,0:T(8,128)} %get-tuple-element.102) | copy-start | bytes 491524

commit v6 on v5

--- a/solution.py
+++ b/solution.py
@@ -70,19 +70,28 @@
     return np.concatenate(parts, axis=1)
 
 
-def project_kernel(me, x, seg, starts, table, rows8, wq_o, wq_x, wk, wv,
-                   q_o, q_x, ql_o, ql_x, k_out, v_out, kl_out, nb_out, cos_out, sin_out):
-    g_in, gq, gk = gain_refs(rows8, 0, 4, 5)
+def project_kernel(me, x, seg, table, g1, g2, g3, g4, g5, g6, wq_o, wq_x, wk, wv,
+                   q_o, q_x, ql_o, ql_x, k_out, v_out, kl_out, nb_out, cos_out, sin_out, seg_out, rows8):
     i = pl.program_id(0)
     rows = x.shape[1]
+
+    @pl.when(i == 0)
+    def _():
+        rows8[...] = jnp.zeros_like(rows8)
+        for r, g in enumerate((g1, g2, g3, g4, g5, g6)):
+            rows8[r : r + 1, : g.shape[0]] = g[...].reshape(1, g.shape[0])
+
+    g_in, gq, gk = gain_refs(rows8, 0, 4, 5)
     hat, _ = rms_stats(x[0])
     nb = (hat * g_in[...]).astype(BF)
     nb_out[...] = nb
-    seg_col = column_of(seg[...])
-    lane = lax.broadcasted_iota(jnp.int32, (rows, LANES), 1)
-    start = jnp.sum(jnp.where(seg_col == lane, starts[...], 0.0), axis=1, keepdims=True)
-    row = lax.broadcasted_iota(jnp.int32, (rows, 1), 0) + me[0] + (i - 1) * rows
-    pos = row - start.astype(jnp.int32)
+    base = me[0] + (i - 1) * rows
+    seg_row = seg[:, pl.ds(pl.multiple_of(jnp.maximum(base, 0), rows), rows)]
+    seg_row = jnp.where(base < 0, -1, seg_row)
+    seg_out[...] = seg_row
+    before = (seg[...] < column_of(seg_row)[:, :1]).astype(F32)
+    start = jnp.sum(before, axis=1, keepdims=True)
+    pos = lax.broadcasted_iota(jnp.int32, (rows, 1), 0) + base - start.astype(jnp.int32)
     hot = (lax.broadcasted_iota(jnp.int32, (rows, BLOCK), 1) == pos).astype(F32).astype(BF)
     cs = nn(hot, table[...])
     cos = cs[:, :LANES] + cs[:, LANES : 2 * LANES]
@@ -276,10 +285,9 @@
     return jax.ShapeDtypeStruct(shape, dtype)
 
 
-def project(first_row, x3, seg_ext, starts, table, rows8, wq_o, wq_x, wk, wv):
+def project(first_row, own, x3, seg, table, gain_list, wq_o, wq_x, wk, wv):
     depth = x3.shape[2]
-    ext = seg_ext.shape[1]
-    own = ext - BLOCK
+    ext = own + BLOCK
     part = wq_o.shape[1]
     n = BLOCK
     me_block = lambda i, me: (0, jnp.maximum(me[0] // n + i - 1, 0), 0)
@@ -290,27 +298,28 @@
             grid=(ext // n,),
             in_specs=[
                 pl.BlockSpec((1, n, depth), me_block),
-                pl.BlockSpec((1, n), lambda i, *_: (0, i)),
-                whole((1, LANES)),
+                whole(seg.shape),
                 whole(table.shape),
-                whole(rows8.shape),
+                *[whole(g.shape) for g in gain_list],
                 whole(wq_o.shape), whole(wq_x.shape), whole(wk.shape), whole(wv.shape),
             ],
             out_specs=[
                 rows_of(n, part, 1), rows_of(n, part, 1), rows_of(n, part, 1), rows_of(n, part, 1),
                 rows_of(n, HEAD_WIDTH), rows_of(n, HEAD_WIDTH), rows_of(n, HEAD_WIDTH, 1),
                 rows_of(n, depth, 1), rows_of(n, LANES, 1), rows_of(n, LANES, 1),
+                pl.BlockSpec((1, n), lambda i, *_: (0, i)), pl.BlockSpec((8, depth), lambda i, *_: (0, 0)),
             ],
         ),
         out_shape=[
             sds((own, part), BF), sds((own, part), BF), sds((own, part), F32), sds((own, part), F32),
             sds((ext, HEAD_WIDTH), BF), sds((ext, HEAD_WIDTH), BF), sds((own, HEAD_WIDTH), F32),
             sds((own, depth), BF), sds((own, LANES), F32), sds((own, LANES), F32),
+            sds((1, ext), jnp.int32), sds((8, depth), F32),
         ],
         compiler_params=params(),
         cost_estimate=cost(6),
         name="project",
-    )(first_row, x3, seg_ext, starts, table, rows8, wq_o, wq_x, wk, wv)
+    )(first_row, x3, seg, table, *gain_list, wq_o, wq_x, wk, wv)
 
 
 def block_pass(first_row, x3, up3, seg_ext, q_o, q_x, k, v, weights, rows8):
@@ -399,8 +408,9 @@
     kv_recv = take(len(kv_groups))
     kv_cur = take(len(kv_groups))
     kv_all = refs.pop(0)
-    gain_own = take(n_bits + 1)
-    gain_got = take(n_bits + 1)
+    kv_wide = refs.pop(0)
+    gain_own = take(len(kv_groups) + 1)
+    gain_got = take(len(kv_groups) + 1)
     send_sems, recv_sems = take(2)
 
     me = lax.axis_index("dp")
@@ -505,9 +515,6 @@
     fetch["nb"].wait()
     query_sent[...] = tn(qr_x[...], buf["nb"][...]).astype(BF)
     query_copy = send(query_sent, query_got, other_core)
-    for n in range(n_items):
-        if items[n][1]:
-            finish(n, 0)
     fetch["kl"].wait()
     front_copy.wait_recv()
     gk_row, gin_row = rows8[5:6, :HEAD_WIDTH], rows8[0:1, :]
@@ -537,10 +544,6 @@
     own_query = tn(qr_o[...], buf["nb"][...]) + query_got[...].astype(F32)
     query[...] = own_query.astype(BF).reshape(query.shape)
     start(n_items - 1, 0)
-    def gain_start(s):
-        device = {"tensor": 1 - core} if s == 0 else {"dp": flipped((s - 1,))}
-        return send(gain_own[s], gain_got[s], device)
-
     kv_copies[0].wait_recv()
 
     def kv_first(j, carry):
@@ -569,6 +572,9 @@
     for k, b in enumerate(kv_order):
         spot = spot + bit_of(me, b) * 2 ** (n_bits - 1 - k)
     kv_copies = kv_start(0)
+    for n in range(n_items):
+        if items[n][1]:
+            finish(n, 0)
     for name in ("wk", "wv", "wq_o", "wq_x", "x", "gmid"):
         fetch[name].wait()
 
@@ -581,33 +587,52 @@
         g_in[...] += jnp.sum(gn * hat, axis=0, keepdims=True)
         return carry
 
-    lax.fori_loop(0, own // QB, input_rows, 0)
+    gain_copies = []
+
+    def gain_start(s):
+        if s == 0:
+            gain_copies.append([send(gain_own[0], gain_got[0].at[0], other_core)])
+        else:
+            gain_copies.append([send(gain_own[s], gain_got[s].at[c], {"dp": flipped(m)})
+                                for c, m in enumerate(subsets(kv_groups[s - 1]))])
+
+    def gain_step():
+        s = len(gain_copies) - 1
+        total = gain_own[s][...]
+        for c, copy in enumerate(gain_copies[s]):
+            copy.wait_recv()
+            total = total + gain_got[s][c]
+        if s == len(kv_groups):
+            gain_out[...] = total
+            return True
+        gain_own[s + 1][...] = total
+        gain_start(s + 1)
+        return False
+
+    half_rows = own // QB // 2
+
+    def fill_first():
+        lax.fori_loop(0, half_rows, input_rows, 0)
+
+    def fill_second():
+        lax.fori_loop(half_rows, own // QB, input_rows, 0)
+        gain_own[0][...] = jnp.zeros_like(gain_own[0])
+        gain_own[0][0:3, :] = g_block[0:3, :]
+        gain_own[0][3:4, :] = g_in[...]
+        gain_own[0][4:5, :HEAD_WIDTH] = g_q[...]
+        gain_own[0][5:6, :HEAD_WIDTH] = g_k[...]
+        gain_start(0)
+
     gin_copy = pltpu.make_async_copy(buf["x"], gin_far, local_sems.at[len(NAMES)])
-    gin_copy.start()
-    gain_own[0][...] = jnp.zeros_like(gain_own[0])
-    gain_own[0][0:3, :] = g_block[0:3, :]
-    gain_own[0][3:4, :] = g_in[...]
-    gain_own[0][4:5, :HEAD_WIDTH] = g_q[...]
-    gain_own[0][5:6, :HEAD_WIDTH] = g_k[...]
-    gain_copies = [gain_start(0)]
-    todo = [(n, s) for s in range(n_bits) for n in range(-1, n_items) if s or n < 0 or not items[n][1]]
-    todo = todo + [(-1, n_bits)]
-    todo.sort(key=lambda e: e[1] - (1 if e[0] >= 0 and items[e[0]][1] else 0))
+    fills = [fill_first, fill_second, gin_copy.start]
+    rank = lambda e: e[1] - (1 if items[e[0]][1] else 0)
+    todo = [(n, s) for s in range(n_bits) for n in range(n_items) if s or not items[n][1]]
+    todo.sort(key=rank)
 
     def advance():
-        rank = lambda e: e[1] - (1 if e[0] >= 0 and items[e[0]][1] else 0)
         now = rank(todo[0]) if todo else 0
         while todo and rank(todo[0]) == now:
-            n, s = todo.pop(0)
-            if n >= 0:
-                finish(n, s)
-                continue
-            gain_copies[s].wait_recv()
-            if s == n_bits:
-                gain_out[...] = gain_own[s][...] + gain_got[s][...]
-            else:
-                gain_own[s + 1][...] = gain_own[s][...] + gain_got[s][...]
-                gain_copies.append(gain_start(s + 1))
+            finish(*todo.pop(0))
 
     for g in range(len(kv_groups)):
         rest = rest_of(g)
@@ -629,9 +654,12 @@
 
             lax.fori_loop(0, rest, kv_body, 0)
             kv_copies = kv_start(g + 1)
+            if len(fills) > 2:
+                fills.pop(0)()
+            advance()
         else:
             kv_all[core, spot] = kv_total(0)
-        advance()
+    gains_done = False
     for g in reversed(range(len(kv_groups))):
         size = rest_of(g)
         begin = 0
@@ -639,21 +667,31 @@
             begin = begin + bit_of(me, b) * 2 ** (n_bits - 1 - k)
         region = kv_all.at[core, pl.ds(begin, size)]
         copies = [send(region, region, {"dp": flipped(m)}) for m in subsets(kv_groups[g])]
+        while len(fills) > 1:
+            fills.pop(0)()
+        if fills:
+            fills.pop(0)()
+        elif not gains_done:
+            gains_done = gain_step()
         advance()
         for copy in copies:
             copy.wait_recv()
-    copy = send(kv_all.at[core], kv_all.at[core], {"tensor": 1 - core})
+    copy = send(kv_all.at[core], kv_all.at[core], other_core)
     while todo:
         advance()
+    while not gains_done:
+        gains_done = gain_step()
     copy.wait_recv()
 
     def unpack(j, carry):
         index = natural_index(me, j, (), kv_order)
-        k_out[index] = kv_all[0, j].astype(F32)
-        v_out[index] = kv_all[1, j].astype(F32)
+        for t in range(2):
+            kv_wide[t, index] = kv_all[t, j].astype(F32)
         return carry
 
     lax.fori_loop(0, 2**n_bits, unpack, 0)
+    for t, out in enumerate((k_out, v_out)):
+        out[...] = jnp.transpose(kv_wide[t].reshape(HEAD_WIDTH, depth))
     gin_copy.wait()
     for copy in sent:
         copy.wait_send()
@@ -683,10 +721,12 @@
     comm += [pltpu.VMEM((2 ** len(groups[g]) - 1, sizes[g + 1], c, width), BF) for g in range(len(groups))]
     comm += [pltpu.VMEM((sizes[g], c, width), BF) for g in range(len(groups))]
     comm += [pltpu.VMEM((2, n, c, width), BF)]
-    comm += [pltpu.VMEM((8, width), F32) for _ in range(2 * (n_bits + 1))]
-    copies += 2 + 2 * sum(2 ** len(g) - 1 for g in groups) + n_bits + 1
+    comm += [pltpu.VMEM((2, n, c, width), F32)]
+    comm += [pltpu.VMEM((8, width), F32) for _ in range(len(groups) + 1)]
+    comm += [pltpu.VMEM((1, 8, width), F32)] + [pltpu.VMEM((2 ** len(g) - 1, 8, width), F32) for g in groups]
+    copies += 3 + 3 * sum(2 ** len(g) - 1 for g in groups)
     comm += [pltpu.SemaphoreType.DMA((copies,)), pltpu.SemaphoreType.DMA((copies,))]
-    outs += [sds((n, c, width), F32), sds((n, c, width), F32), sds((8, width), F32), sds((own, depth), F32)]
+    outs += [sds((width, HEAD_WIDTH), F32), sds((width, HEAD_WIDTH), F32), sds((8, width), F32), sds((own, depth), F32)]
     near = [pltpu.VMEM((own, depth), F32)] + [pltpu.VMEM(a.shape, a.dtype) for a in far[1:]]
     scratch = near + [
         pltpu.SemaphoreType.DMA((len(far) + 1,)),
@@ -722,17 +762,11 @@
     own = tokens // n_tensor
     me = lax.axis_index("tensor")
     first_row = (me * own).astype(jnp.int32).reshape(1)
-    seg = segment_ids[0]
-    seg_pad = jnp.concatenate([jnp.full((BLOCK,), -1, jnp.int32), seg])
-    seg_ext = lax.dynamic_slice_in_dim(seg_pad, me * own, own + BLOCK, 0)[None]
-    starts = jnp.sum((seg[None, :] < jnp.arange(LANES, dtype=jnp.int32)[:, None]).astype(F32), axis=1)[None]
-    fill = lambda g: jnp.pad(g, (0, depth - g.shape[0]))
-    rows8 = jnp.stack([gain_attn_in, gain_attn_out, gain_ff_in, gain_ff_out, fill(gain_query), fill(gain_key),
-                       jnp.zeros_like(gain_attn_in), jnp.zeros_like(gain_attn_in)])
     wq_x, wo_x, wg_x, wu_x, wd_x = (swap(w, n_tensor) for w in (w_query, w_out, w_gate, w_up, w_down))
     table = jnp.asarray(rope_table())
-    q_o, q_x, ql_o, ql_x, k, v, kl, nb, cos, sin = project(
-        first_row, residual_in, seg_ext, starts, table, rows8, w_query, wq_x, w_key, w_value)
+    gain_list = (gain_attn_in, gain_attn_out, gain_ff_in, gain_ff_out, gain_query, gain_key)
+    q_o, q_x, ql_o, ql_x, k, v, kl, nb, cos, sin, seg_ext, rows8 = project(
+        first_row, own, residual_in, segment_ids, table, gain_list, w_query, wq_x, w_key, w_value)
     weights = (w_out, wo_x, w_gate, wg_x, w_up, wu_x, w_down, wd_x)
     (output, gmid, ga_o, ga_x, af_o, af_x, lse, delta, mid_b, gff, gas,
      act_o, act_x, gg_o, gg_x, gu_o, gu_x, gains) = block_pass(
@@ -757,10 +791,8 @@
     *shares, k_sum, v_sum, gain_sum, grad_input = finish_all(
         n_dp, items, plain, plain, (seg_ext, lse, delta, rows8, gains), far)
     s_down, s_gate, s_up, s_out, s_query = shares
-    k_sum = k_sum.reshape(HEAD_WIDTH, depth)
-    v_sum = v_sum.reshape(HEAD_WIDTH, depth)
     return (
-        output[None], grad_input[None], gain_sum[3], s_query.T, k_sum.T, v_sum.T,
+        output[None], grad_input[None], gain_sum[3], s_query.T, k_sum, v_sum,
         gain_sum[4, :HEAD_WIDTH], gain_sum[5, :HEAD_WIDTH],
         s_out.T, gain_sum[2], gain_sum[1], s_gate.T, s_up.T, s_down.T, gain_sum[0],
     )

time: 187 us -> 181 us (0.968)
  local copies, waits for them, and re-layouts: 20.6 us -> 13.6 us
  waiting for transfers between devices: 2.08 us -> 8.86 us
  Pallas kernels: 141 us -> 135 us
    ppermute x9, waiting for transfers between devices: 2.08 us -> 8.86 us  [swap(): lax.ppermute(value, 'tensor', [(t, n_tensor - 1 - t) for t in range(n_ten...]
    pallas_call x1, Pallas kernels: 80.6 us -> 74 us  [finish_all(): pl.pallas_call(functools.partial(finish_kernel, tuple(spec), groups, n_bi...]
    reshape x2 -> x0, local copies, waits for them, and re-layouts: 4.47 us -> none  [the longest x1 2.31 us: on_device(): k_sum = k_sum.reshape(HEAD_WIDTH, depth)]
    unnamed x44 -> x48, local copies, waits for them, and re-layouts: 7.15 us -> 10.8 us
    another operation x8 -> x0, local copies, waits for them, and re-layouts: 3.41 us -> none  [on_device(): jnp.stack([gain_attn_in, gain_attn_out, gain_ff_in, gain_ff_out, fill(gai...]
  transfers between devices with their start and end apart: 9 -> 9, of which waited for: 1 -> 2; matrix products, arithmetic and copies ran while one was open for 9% -> 5% of each run, Pallas kernels for 6% -> 7%
where the time goes in v6:
time: 181 us; the launch traced here: 180 us
  Pallas kernels  135 us (75%)
  matrix products  18.6 us (10%)
  local copies, waits for them, and re-layouts  13.6 us (8%)
  waiting for transfers between devices  8.86 us (5%)
  starting transfers between devices  2.32 us (1%)
    pallas_call x1, Pallas kernels, finish_all(): pl.pallas_call(functools.partial(finish_kernel, tuple(spec), groups, n_bi...  74 us
    pallas_call x1, Pallas kernels, block_pass(): pl.pallas_call(kern, grid_spec=pltpu.PrefetchScalarGridSpec(num_scalar_pr...  49.2 us
    dot_general x8, matrix products, tn(): lax.dot_general(a, b, (((0,), (0,)), ((), ())), preferred_element_type=F32)  18.6 us
    pallas_call x1, Pallas kernels, project(): pl.pallas_call(project_kernel, grid_spec=pltpu.PrefetchScalarGridSpec(num...  12.2 us
    unnamed x48, local copies, waits for them, and re-layouts  10.8 us
    ppermute x9, waiting for transfers between devices, swap(): lax.ppermute(value, 'tensor', [(t, n_tensor - 1 - t) for t in range(n_ten...  8.86 us
  transfers between devices with their start and end apart: 9, of which 2 were waited for; matrix products, arithmetic and copies ran while one was open for 5% of the time, Pallas kernels for 7%

profile of v6, /device:TPU:1, one launch (start us, length us, event | category | flops | bytes accessed | tf_op | source)
XLA Modules:
  0.0 179.5 jit_solution(3459102733413343205)
XLA Ops:
  0.6 0.1 collective-permute-start.2
  0.7 0.5 collective-permute-start.3
  1.2 0.1 collective-permute-start.4
  1.3 0.4 collective-permute-start
  1.7 0.1 collective-permute-start.1
  1.8 6.8 %collective-permute-done.wq_x.refs_12_ = bf16[640,512]{1,0:T(8,128)(2,1)S(1)} collective-permute-done((bf16[640,512]{1,0:T(8,128)(2,1)}, bf16[640,512]{1,0:T(8,128)(2,1)S(1)}, u32[]{:S(2)}, u32[]{:S(2)}) %collective-permute-start) | collective-permute-done | bytes 655392 | tf_op jit(solution)/shard_map/ppermute | solution.py:360
  8.6 0.8 copy-done
  9.5 12.2 %project.1 = (bf16[1024,512]{1,0:T(8,128)(2,1)}, bf16[1024,512]{1,0:T(8,128)(2,1)}, f32[1024,512]{1,0:T(8,128)}, f32[1024,512]{1,0:T(8,128)}, bf16[1536,256]{1,0...) custom-call(s32[1]{0:T(128)} %bitcast.me, ...), custom_call_target="tpu_custom_call" | custom-call | flops 6000000000 | bytes 6000000 | tf_op jit(solution)/shard_map/project/pallas_call | solution.py:294
  21.6 0.0 collective-permute-done.1.refs_8_
  21.7 0.0 collective-permute-done.2.refs_10_
  21.7 0.0 copy-start.8
  21.7 0.0 collective-permute-done.3.refs_12_
  21.7 0.0 copy-start.9
  21.7 0.0 collective-permute-done.4.refs_14_
  21.7 1.1 copy-done.8
  22.8 0.4 copy-done.9
  23.2 49.2 %block.1 = (f32[1024,640]{1,0:T(8,128)}, f32[1024,640]{1,0:T(8,128)}, bf16[1024,512]{1,0:T(8,128)(2,1)}, bf16[1024,512]{1,0:T(8,128)(2,1)}, bf16[1024,512]{1,0:T...) custom-call(s32[1]{0:T(128)} %bitcast.me, ...), custom_call_target="tpu_custom_call" | custom-call | flops 40000000000 | bytes 40000000 | tf_op jit(solution)/shard_map/block/pallas_call | solution.py:333
  72.3 0.0 copy-start.16
  72.4 0.0 copy-start.17
  72.4 3.7 %convolution_convert_fusion.2 = bf16[640,1024]{1,0:T(8,128)(2,1)S(1)} fusion(bf16[1024,640]{1,0:T(8,128)(2,1)} %get-tuple-element.68, bf16[1024,1024]{1,0:T(8,128)(2,1)} %get-tuple-element.74), kind=kOutput, calls=%fused_computation.5 | convolution fusion | flops 1342832640 | bytes 4718592 | tf_op jit(solution)/shard_map/dot_general | solution.py:35
  76.1 0.0 copy-done.16
  76.1 0.0 copy-done.17
  76.1 0.0 copy-start.15
  76.1 1.9 %convolution_convert_fusion.1 = bf16[1024,640]{1,0:T(8,128)(2,1)S(1)} fusion(bf16[1024,1024]{1,0:T(8,128)(2,1)S(1)} %copy-done.16, bf16[1024,640]{1,0:T(8,128)(2,1)S(1)} %copy-done.17), kind=kOutput, calls=%fused_computation.4 | convolution fusion | flops 1342832640 | bytes 4718592 | tf_op jit(solution)/shard_map/dot_general | solution.py:35
  78.0 0.0 copy-done.15
  78.0 0.0 copy-start.10
  78.0 0.0 copy-start.12
  78.0 1.9 %convolution_convert_fusion = bf16[1024,640]{1,0:T(8,128)(2,1)S(1)} fusion(bf16[1024,1024]{1,0:T(8,128)(2,1)S(1)} %copy-done.15, bf16[1024,640]{1,0:T(8,128)(2,1)S(1)} %copy-done.17), kind=kOutput, calls=%fused_computation.3 | convolution fusion | flops 1342832640 | bytes 4718592 | tf_op jit(solution)/shard_map/dot_general | solution.py:35
  79.9 0.2 collective-permute-start.7
  80.1 0.0 copy-done.10
  80.1 0.0 copy-done.12
  80.1 0.9 convolution_convert_fusion.3
  81.0 0.4 collective-permute-start.8
  81.4 0.2 collective-permute-start.6
  81.5 0.4 collective-permute-start.5
  81.9 2.0 %collective-permute-done.8 = bf16[640,512]{1,0:T(8,128)(2,1)S(1)} collective-permute-done((bf16[640,512]{1,0:T(8,128)(2,1)S(1)}, bf16[640,512]{1,0:T(8,128)(2,1)S(1)}, u32[]{:S(2)}, u32[]{:S(2)}) %collective-permute-start.8) | collective-permute-done | bytes 655392 | tf_op jit(solution)/shard_map/ppermute | solution.py:360
  83.9 0.0 copy-done.11
  83.9 1.7 fusion
  85.6 0.0 collective-permute-done.7
  85.6 0.0 copy-done.14
  85.6 2.9 %add_convert_fusion = bf16[1024,640]{1,0:T(8,128)(2,1)} fusion(bf16[1024,640]{1,0:T(8,128)(2,1)S(1)} %collective-permute-done.7, bf16[1024,1024]{1,0:T(8,128)(2,1)S(1)} %copy-done.14, bf16[1024,640]{1,0:T(8,128)(2,1)S(1)} %copy-done.17), kind=kOutput, calls=%fused_computation | convolution fusion | flops 1344143360 | bytes 6029312 | tf_op jit(solution)/shard_map/dot_general | solution.py:35
  88.6 0.0 collective-permute-done.6
  88.6 0.0 copy-done.13
  88.6 3.0 %add_convert_fusion.1 = bf16[1024,640]{1,0:T(8,128)(2,1)} fusion(bf16[1024,640]{1,0:T(8,128)(2,1)S(1)} %collective-permute-done.6, bf16[1024,1024]{1,0:T(8,128)(2,1)S(1)} %copy-done.13, bf16[1024,640]{1,0:T(8,128)(2,1)S(1)} %copy-done.17), kind=kOutput, calls=%fused_computation.1 | convolution fusion | flops 1344143360 | bytes 6029312 | tf_op jit(solution)/shard_map/dot_general | solution.py:35
  91.6 0.0 collective-permute-done.5
  91.6 0.0 copy-done.18
  91.6 0.0 copy-done.19
  91.6 2.6 %add_convert_fusion.2 = bf16[640,1024]{1,0:T(8,128)(2,1)} fusion(bf16[640,1024]{1,0:T(8,128)(2,1)S(1)} %collective-permute-done.5, bf16[1024,640]{1,0:T(8,128)(2,1)S(1)} %copy-done.19, bf16[1024,1024]{1,0:T(8,128)(2,1)S(1)} %copy-done.18), kind=kOutput, calls=%fused_computation.2 | convolution fusion | flops 1344143360 | bytes 6029312 | tf_op jit(solution)/shard_map/dot_general | solution.py:35
  94.2 74.0 %finish_all.1 = (f32[40,1024]{1,0:T(8,128)}, f32[64,640]{1,0:T(8,128)}, f32[64,640]{1,0:T(8,128)}, f32[40,512]{1,0:T(8,128)}, f32[32,640]{1,0:T(8,128)}, /*index...) custom-call(bf16[16,40,1024]{2,1,0:T(8,128)(2,1)} %bitcast.33, ...), custom_call_target="tpu_custom_call" | custom-call | tf_op jit(solution)/shard_map/finish_all/pallas_call | solution.py:744
  168.2 1.3 fusion.1
  169.6 1.5 slice_reduce_fusion
  171.1 3.5 %copy.40 = f32[1,1024,640]{2,1,0:T(8,128)} copy(f32[1,1024,640]{2,1,0:T(8,128)} %bitcast.30) | data formatting | bytes 5242880
  174.5 0.0 copy-done.7
  174.5 0.6 copy.41
  175.2 0.0 copy-done.2
  175.2 0.8 copy.42
  176.0 0.0 copy-done.1
  176.0 0.8 copy.43
  176.9 0.0 copy-done.6
  176.9 0.6 copy.44
  177.5 0.7 copy.45
  178.2 0.0 copy-done.4
  178.2 0.7 copy.46
  178.9 0.7 copy.47
  (15 shorter events, 0.0 us)
Async XLA Ops:
  0.6 21.0 %collective-permute-start.2 = (bf16[640,1024]{1,0:T(8,128)(2,1)}, bf16[640,1024]{1,0:T(8,128)(2,1)S(1)}, u32[]{:S(2)}, u32[]{:S(2)}) collective-permute-start(bf16[640,1024]{1,0:T(8,128)(2,1)} %refs_9_.2), channel_id=1, source_target_pairs={{0,1},{1,0},{2,3},{3,2},{4,5},{5,4},{6,7},{7,6},{8,9},{9,8},{10,11... | collective-permute-start | bytes 3932168 | tf_op jit(solution)/shard_map/ppermute | solution.py:360
  0.7 21.0 %collective-permute-start.3 = (bf16[640,1024]{1,0:T(8,128)(2,1)}, bf16[640,1024]{1,0:T(8,128)(2,1)S(1)}, u32[]{:S(2)}, u32[]{:S(2)}) collective-permute-start(bf16[640,1024]{1,0:T(8,128)(2,1)} %refs_11_.2), channel_id=1, source_target_pairs={{0,1},{1,0},{2,3},{3,2},{4,5},{5,4},{6,7},{7,6},{8,9},{9,8},{10,11... | collective-permute-start | bytes 3932168 | tf_op jit(solution)/shard_map/ppermute | solution.py:360
  1.2 20.5 %collective-permute-start.4 = (bf16[1024,640]{1,0:T(8,128)(2,1)}, bf16[1024,640]{1,0:T(8,128)(2,1)}, u32[]{:S(2)}, u32[]{:S(2)}) collective-permute-start(bf16[1024,640]{1,0:T(8,128)(2,1)} %refs_13_.2), channel_id=1, source_target_pairs={{0,1},{1,0},{2,3},{3,2},{4,5},{5,4},{6,7},{7,6},{8,9},{9,8},{10,11... | collective-permute-start | bytes 3932168 | tf_op jit(solution)/shard_map/ppermute | solution.py:360
  1.3 7.3 %collective-permute-start = (bf16[640,512]{1,0:T(8,128)(2,1)}, bf16[640,512]{1,0:T(8,128)(2,1)S(1)}, u32[]{:S(2)}, u32[]{:S(2)}) collective-permute-start(bf16[640,512]{1,0:T(8,128)(2,1)} %refs_11_.3), channel_id=1, source_target_pairs={{0,1},{1,0},{2,3},{3,2},{4,5},{5,4},{6,7},{7,6},{8,9},{9,8},{10,11... | collective-permute-start | bytes 1966088 | tf_op jit(solution)/shard_map/ppermute | solution.py:360
  1.7 19.9 %collective-permute-start.1 = (bf16[512,640]{1,0:T(8,128)(2,1)}, bf16[512,640]{1,0:T(8,128)(2,1)}, u32[]{:S(2)}, u32[]{:S(2)}) collective-permute-start(bf16[512,640]{1,0:T(8,128)(2,1)} %refs_7_.1), channel_id=1, source_target_pairs={{0,1},{1,0},{2,3},{3,2},{4,5},{5,4},{6,7},{7,6},{8,9},{9,8},{10,11... | collective-permute-start | bytes 1966088 | tf_op jit(solution)/shard_map/ppermute | solution.py:360
  8.6 0.8 copy-start
  21.7 1.1 copy-start.8
  21.7 1.5 copy-start.9
  72.3 3.7 %copy-start.16 = (bf16[1024,1024]{1,0:T(8,128)(2,1)S(1)}, bf16[1024,1024]{1,0:T(8,128)(2,1)}, u32[]{:S(2)}) copy-start(bf16[1024,1024]{1,0:T(8,128)(2,1)} %get-tuple-element.75) | copy-start | bytes 6291460
  72.4 3.7 %copy-start.17 = (bf16[1024,640]{1,0:T(8,128)(2,1)S(1)}, bf16[1024,640]{1,0:T(8,128)(2,1)}, u32[]{:S(2)}) copy-start(bf16[1024,640]{1,0:T(8,128)(2,1)} %get-tuple-element.76) | copy-start | bytes 3932164
  76.1 1.9 %copy-start.15 = (bf16[1024,1024]{1,0:T(8,128)(2,1)S(1)}, bf16[1024,1024]{1,0:T(8,128)(2,1)}, u32[]{:S(2)}) copy-start(bf16[1024,1024]{1,0:T(8,128)(2,1)} %get-tuple-element.77) | copy-start | bytes 6291460
  78.0 2.1 %copy-start.10 = (bf16[1024,640]{1,0:T(8,128)(2,1)S(1)}, bf16[1024,640]{1,0:T(8,128)(2,1)}, u32[]{:S(2)}) copy-start(bf16[1024,640]{1,0:T(8,128)(2,1)} %get-tuple-element.70) | copy-start | bytes 3932164
  78.0 2.1 %copy-start.12 = (bf16[1024,512]{1,0:T(8,128)(2,1)S(1)}, bf16[1024,512]{1,0:T(8,128)(2,1)}, u32[]{:S(2)}) copy-start(bf16[1024,512]{1,0:T(8,128)(2,1)} %get-tuple-element.78) | copy-start | bytes 3145732
  79.9 5.8 %collective-permute-start.7 = (bf16[1024,640]{1,0:T(8,128)(2,1)S(1)}, bf16[1024,640]{1,0:T(8,128)(2,1)S(1)}, u32[]{:S(2)}, u32[]{:S(2)}) collective-permute-start(bf16[1024,640]{1,0:T(8,128)(2,1)S(1)} %convolution_convert_fusion), channel_id=1, source_target_pairs={{0,1},{1,0},{2,3},{3,2},{4,5},{5,4},{6,7},{7,6},{8,9},{9,8},{10,11... | collective-permute-start | bytes 3932168 | tf_op jit(solution)/shard_map/ppermute | solution.py:360
  80.1 3.8 %copy-start.11 = (bf16[1024,512]{1,0:T(8,128)(2,1)S(1)}, bf16[1024,512]{1,0:T(8,128)(2,1)}, u32[]{:S(2)}) copy-start(bf16[1024,512]{1,0:T(8,128)(2,1)} %get-tuple-element.85) | copy-start | bytes 3145732
  81.0 2.9 %collective-permute-start.8 = (bf16[640,512]{1,0:T(8,128)(2,1)S(1)}, bf16[640,512]{1,0:T(8,128)(2,1)S(1)}, u32[]{:S(2)}, u32[]{:S(2)}) collective-permute-start(bf16[640,512]{1,0:T(8,128)(2,1)S(1)} %convolution_convert_fusion.3), channel_id=1, source_target_pairs={{0,1},{1,0},{2,3},{3,2},{4,5},{5,4},{6,7},{7,6},{8,9},{9,8},{10,11... | collective-permute-start | bytes 1966088 | tf_op jit(solution)/shard_map/ppermute | solution.py:360
  81.4 7.2 %collective-permute-start.6 = (bf16[1024,640]{1,0:T(8,128)(2,1)S(1)}, bf16[1024,640]{1,0:T(8,128)(2,1)S(1)}, u32[]{:S(2)}, u32[]{:S(2)}) collective-permute-start(bf16[1024,640]{1,0:T(8,128)(2,1)S(1)} %convolution_convert_fusion.1), channel_id=1, source_target_pairs={{0,1},{1,0},{2,3},{3,2},{4,5},{5,4},{6,7},{7,6},{8,9},{9,8},{10,11... | collective-permute-start | bytes 3932168 | tf_op jit(solution)/shard_map/ppermute | solution.py:360
  81.5 10.0 %collective-permute-start.5 = (bf16[640,1024]{1,0:T(8,128)(2,1)S(1)}, bf16[640,1024]{1,0:T(8,128)(2,1)S(1)}, u32[]{:S(2)}, u32[]{:S(2)}) collective-permute-start(bf16[640,1024]{1,0:T(8,128)(2,1)S(1)} %convolution_convert_fusion.2), channel_id=1, source_target_pairs={{0,1},{1,0},{2,3},{3,2},{4,5},{5,4},{6,7},{7,6},{8,9},{9,8},{10,11... | collective-permute-start | bytes 3932168 | tf_op jit(solution)/shard_map/ppermute | solution.py:360
  81.9 3.8 %copy-start.14 = (bf16[1024,1024]{1,0:T(8,128)(2,1)S(1)}, bf16[1024,1024]{1,0:T(8,128)(2,1)}, u32[]{:S(2)}) copy-start(bf16[1024,1024]{1,0:T(8,128)(2,1)} %get-tuple-element.83) | copy-start | bytes 6291460
  85.6 3.0 %copy-start.13 = (bf16[1024,1024]{1,0:T(8,128)(2,1)S(1)}, bf16[1024,1024]{1,0:T(8,128)(2,1)}, u32[]{:S(2)}) copy-start(bf16[1024,1024]{1,0:T(8,128)(2,1)} %get-tuple-element.81) | copy-start | bytes 6291460
  88.6 3.0 %copy-start.18 = (bf16[1024,1024]{1,0:T(8,128)(2,1)S(1)}, bf16[1024,1024]{1,0:T(8,128)(2,1)}, u32[]{:S(2)}) copy-start(bf16[1024,1024]{1,0:T(8,128)(2,1)} %get-tuple-element.79) | copy-start | bytes 6291460
  88.6 3.0 %copy-start.19 = (bf16[1024,640]{1,0:T(8,128)(2,1)S(1)}, bf16[1024,640]{1,0:T(8,128)(2,1)}, u32[]{:S(2)}) copy-start(bf16[1024,640]{1,0:T(8,128)(2,1)} %get-tuple-element.68) | copy-start | bytes 3932164
  171.1 3.5 %copy-start.7 = (f32[32,640]{1,0:T(8,128)S(1)}, f32[32,640]{1,0:T(8,128)}, u32[]{:S(2)}) copy-start(f32[32,640]{1,0:T(8,128)} %get-tuple-element.100) | copy-start | bytes 245764
  171.1 4.1 %copy-start.2 = (f32[640,256]{1,0:T(8,128)S(1)}, f32[640,256]{1,0:T(8,128)}, u32[]{:S(2)}) copy-start(f32[640,256]{1,0:T(8,128)} %get-tuple-element.132) | copy-start | bytes 1966084
  174.5 1.5 copy-start.1
  175.2 1.7 copy-start.6
  175.2 2.3 %copy-start.5 = (f32[64,640]{1,0:T(8,128)S(1)}, f32[64,640]{1,0:T(8,128)}, u32[]{:S(2)}) copy-start(f32[64,640]{1,0:T(8,128)} %get-tuple-element.104) | copy-start | bytes 491524
  175.2 3.0 %copy-start.4 = (f32[64,640]{1,0:T(8,128)S(1)}, f32[64,640]{1,0:T(8,128)}, u32[]{:S(2)}) copy-start(f32[64,640]{1,0:T(8,128)} %get-tuple-element.105) | copy-start | bytes 491524
  176.0 2.8 %copy-start.3 = (f32[40,1024]{1,0:T(8,128)S(1)}, f32[40,1024]{1,0:T(8,128)}, u32[]{:S(2)}) copy-start(f32[40,1024]{1,0:T(8,128)} %get-tuple-element.106) | copy-start | bytes 491524

commit v7 on v6

--- a/solution.py
+++ b/solution.py
@@ -396,7 +396,7 @@
     outs = take(n_items)
     k_out, v_out, gain_out, gin_far = take(4)
     near = take(len(NAMES))
-    local_sems = refs.pop(0)
+    local_sems, part_sems = take(2)
     (front, front_got, dk_all, dv_all, qr_o, qr_x, kraw, vraw, kv_in, query_sent, query_got, query,
      g_in, g_k, g_q) = take(15)
     ins.append([query])
@@ -488,10 +488,20 @@
     buf = dict(zip(NAMES, near))
     fetch = {name: pltpu.make_async_copy(s, d, local_sems.at[k])
              for k, (name, s, d) in enumerate(zip(NAMES, sources, near))}
-    first_use = ("k", "v", "q_o", "ga_o", "cos", "sin", "ql_o", "q_x", "ga_x", "ql_x")
+    first_use = ("k", "v")
+    by_rows = ("q_o", "ga_o", "cos", "sin", "ql_o", "q_x", "ga_x", "ql_x")
+
+    def fetch_rows(name, i):
+        k = NAMES.index(name)
+        at = pl.ds(pl.multiple_of(i * QB, QB), QB)
+        return pltpu.make_async_copy(far[k].at[at, :], near[k].at[at, :], part_sems.at[by_rows.index(name), i])
+
     second_use = ("nb", "kl", "wk", "wv", "wq_o", "wq_x", "x", "gmid")
     for name in first_use:
         fetch[name].start()
+    for i in range(own // QB):
+        for name in by_rows:
+            fetch_rows(name, i).start()
     for n in range(n_items):
         if items[n][1]:
             start(n, 0)
@@ -505,6 +515,8 @@
         fetch[name].wait()
 
     def attn_body(i, carry):
+        for name in by_rows:
+            fetch_rows(name, i).wait()
         attn_rows(i, seg, buf, lse, delta, gq_row, qr_o, qr_x, dk_all, dv_all, g_q)
         return carry
 
@@ -729,7 +741,7 @@
     outs += [sds((width, HEAD_WIDTH), F32), sds((width, HEAD_WIDTH), F32), sds((8, width), F32), sds((own, depth), F32)]
     near = [pltpu.VMEM((own, depth), F32)] + [pltpu.VMEM(a.shape, a.dtype) for a in far[1:]]
     scratch = near + [
-        pltpu.SemaphoreType.DMA((len(far) + 1,)),
+        pltpu.SemaphoreType.DMA((len(far) + 1,)), pltpu.SemaphoreType.DMA((8, own // QB)),
         pltpu.VMEM((BLOCK, 2 * HEAD_WIDTH), BF), pltpu.VMEM((BLOCK, 2 * HEAD_WIDTH), BF),
         pltpu.VMEM((ext, HEAD_WIDTH), F32), pltpu.VMEM((ext, HEAD_WIDTH), F32),
         pltpu.VMEM((own, part), BF), pltpu.VMEM((own, part), BF),
@@ -762,7 +774,9 @@
     own = tokens // n_tensor
     me = lax.axis_index("tensor")
     first_row = (me * own).astype(jnp.int32).reshape(1)
-    wq_x, wo_x, wg_x, wu_x, wd_x = (swap(w, n_tensor) for w in (w_query, w_out, w_gate, w_up, w_down))
+    wq_x = swap(w_query, n_tensor)
+    *later, wq_x = lax.optimization_barrier((w_out, w_gate, w_up, w_down, wq_x))
+    wo_x, wg_x, wu_x, wd_x = (swap(w, n_tensor) for w in later)
     table = jnp.asarray(rope_table())
     gain_list = (gain_attn_in, gain_attn_out, gain_ff_in, gain_ff_out, gain_query, gain_key)
     q_o, q_x, ql_o, ql_x, k, v, kl, nb, cos, sin, seg_ext, rows8 = project(
@@ -786,7 +800,9 @@
         gots.append(swap(sent, n_tensor))
     items = []
     for (left, _, units, order), got in zip(pairs, gots):
-        items.append((chunks((grad(left, after(units, *last)) + got.astype(F32)).astype(BF)), order))
+        value = chunks((grad(left, after(units, *last)) + got.astype(F32)).astype(BF))
+        last = (value,)
+        items.append((value, order))
     far = (residual_in, gmid, w_query, wq_x, w_key, w_value, kl, cos, sin, nb, k, v, q_o, q_x, ga_o, ga_x, ql_o, ql_x)
     *shares, k_sum, v_sum, gain_sum, grad_input = finish_all(
         n_dp, items, plain, plain, (seg_ext, lse, delta, rows8, gains), far)

time: 181 us -> 175 us (0.967)
  waiting for transfers between devices: 8.86 us -> 2.31 us
    ppermute x9, waiting for transfers between devices: 8.86 us -> 2.31 us  [swap(): lax.ppermute(value, 'tensor', [(t, n_tensor - 1 - t) for t in range(n_ten...]
  transfers between devices with their start and end apart: 9 -> 9, of which waited for: 2 -> 1; matrix products, arithmetic and copies ran while one was open for 5% -> 8% of each run, Pallas kernels for 7% -> 7%
where the time goes in v7:
time: 175 us; the launch traced here: 173 us
  Pallas kernels  135 us (77%)
  matrix products  18.5 us (11%)
  local copies, waits for them, and re-layouts  13.4 us (8%)
  starting transfers between devices  2.38 us (1%)
  waiting for transfers between devices  2.31 us (1%)
    pallas_call x1, Pallas kernels, finish_all(): pl.pallas_call(functools.partial(finish_kernel, tuple(spec), groups, n_bi...  73.8 us
    pallas_call x1, Pallas kernels, block_pass(): pl.pallas_call(kern, grid_spec=pltpu.PrefetchScalarGridSpec(num_scalar_pr...  49.1 us
    dot_general x8, matrix products, tn(): lax.dot_general(a, b, (((0,), (0,)), ((), ())), preferred_element_type=F32)  18.5 us
    pallas_call x1, Pallas kernels, project(): pl.pallas_call(project_kernel, grid_spec=pltpu.PrefetchScalarGridSpec(num...  12.2 us
    unnamed x48, local copies, waits for them, and re-layouts  10.6 us
  transfers between devices with their start and end apart: 9, of which 1 were waited for; matrix products, arithmetic and copies ran while one was open for 8% of the time, Pallas kernels for 7%

profile of v7, /device:TPU:1, one launch (start us, length us, event | category | flops | bytes accessed | tf_op | source)
XLA Modules:
  0.0 172.6 jit_solution(5297549952927977792)
XLA Ops:
  0.6 0.1 collective-permute-start
  0.7 2.3 %collective-permute-done.wq_x.refs_12_ = bf16[640,512]{1,0:T(8,128)(2,1)S(1)} collective-permute-done((bf16[640,512]{1,0:T(8,128)(2,1)}, bf16[640,512]{1,0:T(8,128)(2,1)S(1)}, u32[]{:S(2)}, u32[]{:S(2)}) %collective-permute-start) | collective-permute-done | bytes 655392 | tf_op jit(solution)/shard_map/ppermute | solution.py:360
  3.0 0.1 collective-permute-start.2
  3.2 0.4 collective-permute-start.3
  3.5 0.1 collective-permute-start.4
  3.7 0.4 collective-permute-start.1
  4.0 0.0 copy-done
  4.0 12.2 %project.1 = (bf16[1024,512]{1,0:T(8,128)(2,1)}, bf16[1024,512]{1,0:T(8,128)(2,1)}, f32[1024,512]{1,0:T(8,128)}, f32[1024,512]{1,0:T(8,128)}, bf16[1536,256]{1,0...) custom-call(s32[1]{0:T(128)} %bitcast.me, ...), custom_call_target="tpu_custom_call" | custom-call | flops 6000000000 | bytes 6000000 | tf_op jit(solution)/shard_map/project/pallas_call | solution.py:294
  16.2 0.0 collective-permute-done.1.refs_8_
  16.2 0.0 collective-permute-done.2.refs_10_
  16.2 0.0 copy-start.8
  16.2 0.0 collective-permute-done.3.refs_12_
  16.3 0.0 copy-start.9
  16.3 0.0 collective-permute-done.4.refs_14_
  16.3 1.0 copy-done.8
  17.3 0.4 copy-done.9
  17.8 49.1 %block.1 = (f32[1024,640]{1,0:T(8,128)}, f32[1024,640]{1,0:T(8,128)}, bf16[1024,512]{1,0:T(8,128)(2,1)}, bf16[1024,512]{1,0:T(8,128)(2,1)}, bf16[1024,512]{1,0:T...) custom-call(s32[1]{0:T(128)} %bitcast.me, ...), custom_call_target="tpu_custom_call" | custom-call | flops 40000000000 | bytes 40000000 | tf_op jit(solution)/shard_map/block/pallas_call | solution.py:333
  66.9 0.0 copy-start.16
  66.9 0.0 copy-start.17
  66.9 3.7 %convolution_convert_fusion.2 = bf16[640,1024]{1,0:T(8,128)(2,1)S(1)} fusion(bf16[1024,640]{1,0:T(8,128)(2,1)} %get-tuple-element.78, bf16[1024,1024]{1,0:T(8,128)(2,1)} %get-tuple-element.84), kind=kOutput, calls=%fused_computation.5 | convolution fusion | flops 1342832640 | bytes 4718592 | tf_op jit(solution)/shard_map/dot_general | solution.py:35
  70.6 0.2 collective-permute-start.5
  70.8 0.0 copy-done.16
  70.8 0.0 copy-done.17
  70.8 0.0 copy-start.15
  70.8 1.9 %convolution_convert_fusion.1 = bf16[1024,640]{1,0:T(8,128)(2,1)S(1)} fusion(bf16[1024,1024]{1,0:T(8,128)(2,1)S(1)} %copy-done.16, bf16[1024,640]{1,0:T(8,128)(2,1)S(1)} %copy-done.17), kind=kOutput, calls=%fused_computation.4 | convolution fusion | flops 1342832640 | bytes 4718592 | tf_op jit(solution)/shard_map/dot_general | solution.py:35
  72.7 0.4 collective-permute-start.6
  73.1 0.0 copy-done.15
  73.1 1.9 %convolution_convert_fusion = bf16[1024,640]{1,0:T(8,128)(2,1)S(1)} fusion(bf16[1024,1024]{1,0:T(8,128)(2,1)S(1)} %copy-done.15, bf16[1024,640]{1,0:T(8,128)(2,1)S(1)} %copy-done.17), kind=kOutput, calls=%fused_computation.3 | convolution fusion | flops 1342832640 | bytes 4718592 | tf_op jit(solution)/shard_map/dot_general | solution.py:35
  75.0 0.2 collective-permute-start.7
  75.2 0.0 copy-done.10
  75.2 0.0 copy-done.12
  75.3 0.9 convolution_convert_fusion.3
  76.1 0.4 collective-permute-start.8
  76.5 0.0 collective-permute-done.5
  76.5 0.3 copy-done.18
  76.8 0.4 copy-done.19
  77.2 2.6 %add_convert_fusion.2 = bf16[640,1024]{1,0:T(8,128)(2,1)} fusion(bf16[640,1024]{1,0:T(8,128)(2,1)S(1)} %collective-permute-done.5, bf16[1024,640]{1,0:T(8,128)(2,1)S(1)} %copy-done.19, bf16[1024,1024]{1,0:T(8,128)(2,1)S(1)} %copy-done.18), kind=kOutput, calls=%fused_computation.2 | convolution fusion | flops 1344143360 | bytes 6029312 | tf_op jit(solution)/shard_map/dot_general | solution.py:35
  79.8 0.0 collective-permute-done.6
  79.8 0.0 copy-done.14
  79.8 3.0 %add_convert_fusion.1 = bf16[1024,640]{1,0:T(8,128)(2,1)} fusion(bf16[1024,640]{1,0:T(8,128)(2,1)S(1)} %collective-permute-done.6, bf16[1024,1024]{1,0:T(8,128)(2,1)S(1)} %copy-done.14, bf16[1024,640]{1,0:T(8,128)(2,1)S(1)} %copy-done.17), kind=kOutput, calls=%fused_computation.1 | convolution fusion | flops 1344143360 | bytes 6029312 | tf_op jit(solution)/shard_map/dot_general | solution.py:35
  82.8 0.0 collective-permute-done.7
  82.8 0.0 copy-done.13
  82.8 3.0 %add_convert_fusion = bf16[1024,640]{1,0:T(8,128)(2,1)} fusion(bf16[1024,640]{1,0:T(8,128)(2,1)S(1)} %collective-permute-done.7, bf16[1024,1024]{1,0:T(8,128)(2,1)S(1)} %copy-done.13, bf16[1024,640]{1,0:T(8,128)(2,1)S(1)} %copy-done.17), kind=kOutput, calls=%fused_computation | convolution fusion | flops 1344143360 | bytes 6029312 | tf_op jit(solution)/shard_map/dot_general | solution.py:35
  85.8 0.0 collective-permute-done.8
  85.8 0.0 copy-done.11
  85.8 1.7 fusion
  87.5 73.8 %finish_all.1 = (f32[40,1024]{1,0:T(8,128)}, f32[64,640]{1,0:T(8,128)}, f32[64,640]{1,0:T(8,128)}, f32[40,512]{1,0:T(8,128)}, f32[32,640]{1,0:T(8,128)}, /*index...) custom-call(bf16[16,40,1024]{2,1,0:T(8,128)(2,1)} %bitcast.31, ...), custom_call_target="tpu_custom_call" | custom-call | tf_op jit(solution)/shard_map/finish_all/pallas_call | solution.py:756
  161.2 1.3 fusion.1
  162.6 1.5 slice_reduce_fusion
  164.1 3.5 %copy.40 = f32[1,1024,640]{2,1,0:T(8,128)} copy(f32[1,1024,640]{2,1,0:T(8,128)} %bitcast.30) | data formatting | bytes 5242880
  167.6 0.0 copy-done.7
  167.6 0.6 copy.41
  168.2 0.0 copy-done.2
  168.2 0.8 copy.42
  169.1 0.0 copy-done.1
  169.1 0.8 copy.43
  169.9 0.0 copy-done.6
  169.9 0.6 copy.44
  170.5 0.0 copy-done.5
  170.5 0.7 copy.45
  171.2 0.0 copy-done.4
  171.2 0.7 copy.46
  171.9 0.0 copy-done.3
  171.9 0.7 copy.47
  (15 shorter events, 0.0 us)
Async XLA Ops:
  0.6 2.4 %collective-permute-start = (bf16[640,512]{1,0:T(8,128)(2,1)}, bf16[640,512]{1,0:T(8,128)(2,1)S(1)}, u32[]{:S(2)}, u32[]{:S(2)}) collective-permute-start(bf16[640,512]{1,0:T(8,128)(2,1)} %refs_11_.3), channel_id=1, source_target_pairs={{0,1},{1,0},{2,3},{3,2},{4,5},{5,4},{6,7},{7,6},{8,9},{9,8},{10,11... | collective-permute-start | bytes 1966088 | tf_op jit(solution)/shard_map/ppermute | solution.py:360
  3.0 1.0 copy-start
  3.0 13.2 %collective-permute-start.2 = (bf16[640,1024]{1,0:T(8,128)(2,1)}, bf16[640,1024]{1,0:T(8,128)(2,1)S(1)}, u32[]{:S(2)}, u32[]{:S(2)}) collective-permute-start(bf16[640,1024]{1,0:T(8,128)(2,1)} %refs_9_.2), channel_id=1, source_target_pairs={{0,1},{1,0},{2,3},{3,2},{4,5},{5,4},{6,7},{7,6},{8,9},{9,8},{10,11... | collective-permute-start | bytes 3932168 | tf_op jit(solution)/shard_map/ppermute | solution.py:360
  3.2 13.1 %collective-permute-start.3 = (bf16[640,1024]{1,0:T(8,128)(2,1)}, bf16[640,1024]{1,0:T(8,128)(2,1)S(1)}, u32[]{:S(2)}, u32[]{:S(2)}) collective-permute-start(bf16[640,1024]{1,0:T(8,128)(2,1)} %refs_11_.2), channel_id=1, source_target_pairs={{0,1},{1,0},{2,3},{3,2},{4,5},{5,4},{6,7},{7,6},{8,9},{9,8},{10,11... | collective-permute-start | bytes 3932168 | tf_op jit(solution)/shard_map/ppermute | solution.py:360
  3.5 12.7 %collective-permute-start.4 = (bf16[1024,640]{1,0:T(8,128)(2,1)}, bf16[1024,640]{1,0:T(8,128)(2,1)}, u32[]{:S(2)}, u32[]{:S(2)}) collective-permute-start(bf16[1024,640]{1,0:T(8,128)(2,1)} %refs_13_.2), channel_id=1, source_target_pairs={{0,1},{1,0},{2,3},{3,2},{4,5},{5,4},{6,7},{7,6},{8,9},{9,8},{10,11... | collective-permute-start | bytes 3932168 | tf_op jit(solution)/shard_map/ppermute | solution.py:360
  3.7 12.5 %collective-permute-start.1 = (bf16[512,640]{1,0:T(8,128)(2,1)}, bf16[512,640]{1,0:T(8,128)(2,1)}, u32[]{:S(2)}, u32[]{:S(2)}) collective-permute-start(bf16[512,640]{1,0:T(8,128)(2,1)} %refs_7_.1), channel_id=1, source_target_pairs={{0,1},{1,0},{2,3},{3,2},{4,5},{5,4},{6,7},{7,6},{8,9},{9,8},{10,11... | collective-permute-start | bytes 1966088 | tf_op jit(solution)/shard_map/ppermute | solution.py:360
  16.2 1.1 copy-start.8
  16.3 1.5 copy-start.9
  66.9 3.9 %copy-start.16 = (bf16[1024,1024]{1,0:T(8,128)(2,1)S(1)}, bf16[1024,1024]{1,0:T(8,128)(2,1)}, u32[]{:S(2)}) copy-start(bf16[1024,1024]{1,0:T(8,128)(2,1)} %get-tuple-element.85) | copy-start | bytes 6291460
  66.9 3.9 %copy-start.17 = (bf16[1024,640]{1,0:T(8,128)(2,1)S(1)}, bf16[1024,640]{1,0:T(8,128)(2,1)}, u32[]{:S(2)}) copy-start(bf16[1024,640]{1,0:T(8,128)(2,1)} %get-tuple-element.86) | copy-start | bytes 3932164
  70.6 5.9 %collective-permute-start.5 = (bf16[640,1024]{1,0:T(8,128)(2,1)S(1)}, bf16[640,1024]{1,0:T(8,128)(2,1)S(1)}, u32[]{:S(2)}, u32[]{:S(2)}) collective-permute-start(bf16[640,1024]{1,0:T(8,128)(2,1)S(1)} %convolution_convert_fusion.2), channel_id=1, source_target_pairs={{0,1},{1,0},{2,3},{3,2},{4,5},{5,4},{6,7},{7,6},{8,9},{9,8},{10,11... | collective-permute-start | bytes 3932168 | tf_op jit(solution)/shard_map/ppermute | solution.py:360
  70.8 2.3 %copy-start.15 = (bf16[1024,1024]{1,0:T(8,128)(2,1)S(1)}, bf16[1024,1024]{1,0:T(8,128)(2,1)}, u32[]{:S(2)}) copy-start(bf16[1024,1024]{1,0:T(8,128)(2,1)} %get-tuple-element.87) | copy-start | bytes 6291460
  72.7 7.1 %collective-permute-start.6 = (bf16[1024,640]{1,0:T(8,128)(2,1)S(1)}, bf16[1024,640]{1,0:T(8,128)(2,1)S(1)}, u32[]{:S(2)}, u32[]{:S(2)}) collective-permute-start(bf16[1024,640]{1,0:T(8,128)(2,1)S(1)} %convolution_convert_fusion.1), channel_id=1, source_target_pairs={{0,1},{1,0},{2,3},{3,2},{4,5},{5,4},{6,7},{7,6},{8,9},{9,8},{10,11... | collective-permute-start | bytes 3932168 | tf_op jit(solution)/shard_map/ppermute | solution.py:360
  73.1 2.1 %copy-start.10 = (bf16[1024,640]{1,0:T(8,128)(2,1)S(1)}, bf16[1024,640]{1,0:T(8,128)(2,1)}, u32[]{:S(2)}) copy-start(bf16[1024,640]{1,0:T(8,128)(2,1)} %get-tuple-element.80) | copy-start | bytes 3932164
  73.1 2.1 %copy-start.12 = (bf16[1024,512]{1,0:T(8,128)(2,1)S(1)}, bf16[1024,512]{1,0:T(8,128)(2,1)}, u32[]{:S(2)}) copy-start(bf16[1024,512]{1,0:T(8,128)(2,1)} %get-tuple-element.88) | copy-start | bytes 3145732
  75.0 7.8 %collective-permute-start.7 = (bf16[1024,640]{1,0:T(8,128)(2,1)S(1)}, bf16[1024,640]{1,0:T(8,128)(2,1)S(1)}, u32[]{:S(2)}, u32[]{:S(2)}) collective-permute-start(bf16[1024,640]{1,0:T(8,128)(2,1)S(1)} %convolution_convert_fusion), channel_id=1, source_target_pairs={{0,1},{1,0},{2,3},{3,2},{4,5},{5,4},{6,7},{7,6},{8,9},{9,8},{10,11... | collective-permute-start | bytes 3932168 | tf_op jit(solution)/shard_map/ppermute | solution.py:360
  75.2 1.6 copy-start.18
  75.2 1.9 %copy-start.19 = (bf16[1024,640]{1,0:T(8,128)(2,1)S(1)}, bf16[1024,640]{1,0:T(8,128)(2,1)}, u32[]{:S(2)}) copy-start(bf16[1024,640]{1,0:T(8,128)(2,1)} %get-tuple-element.78) | copy-start | bytes 3932164
  76.1 9.6 %collective-permute-start.8 = (bf16[640,512]{1,0:T(8,128)(2,1)S(1)}, bf16[640,512]{1,0:T(8,128)(2,1)S(1)}, u32[]{:S(2)}, u32[]{:S(2)}) collective-permute-start(bf16[640,512]{1,0:T(8,128)(2,1)S(1)} %convolution_convert_fusion.3), channel_id=1, source_target_pairs={{0,1},{1,0},{2,3},{3,2},{4,5},{5,4},{6,7},{7,6},{8,9},{9,8},{10,11... | collective-permute-start | bytes 1966088 | tf_op jit(solution)/shard_map/ppermute | solution.py:360
  76.5 3.3 %copy-start.14 = (bf16[1024,1024]{1,0:T(8,128)(2,1)S(1)}, bf16[1024,1024]{1,0:T(8,128)(2,1)}, u32[]{:S(2)}) copy-start(bf16[1024,1024]{1,0:T(8,128)(2,1)} %get-tuple-element.91) | copy-start | bytes 6291460
  79.8 3.0 %copy-start.13 = (bf16[1024,1024]{1,0:T(8,128)(2,1)S(1)}, bf16[1024,1024]{1,0:T(8,128)(2,1)}, u32[]{:S(2)}) copy-start(bf16[1024,1024]{1,0:T(8,128)(2,1)} %get-tuple-element.93) | copy-start | bytes 6291460
  82.8 3.0 %copy-start.11 = (bf16[1024,512]{1,0:T(8,128)(2,1)S(1)}, bf16[1024,512]{1,0:T(8,128)(2,1)}, u32[]{:S(2)}) copy-start(bf16[1024,512]{1,0:T(8,128)(2,1)} %get-tuple-element.95) | copy-start | bytes 3145732
  164.1 3.5 %copy-start.7 = (f32[32,640]{1,0:T(8,128)S(1)}, f32[32,640]{1,0:T(8,128)}, u32[]{:S(2)}) copy-start(f32[32,640]{1,0:T(8,128)} %get-tuple-element.110) | copy-start | bytes 245764
  164.1 4.1 %copy-start.2 = (f32[640,256]{1,0:T(8,128)S(1)}, f32[640,256]{1,0:T(8,128)}, u32[]{:S(2)}) copy-start(f32[640,256]{1,0:T(8,128)} %get-tuple-element.142) | copy-start | bytes 1966084
  167.6 1.5 copy-start.1
  168.2 1.7 copy-start.6
  168.2 2.3 %copy-start.5 = (f32[64,640]{1,0:T(8,128)S(1)}, f32[64,640]{1,0:T(8,128)}, u32[]{:S(2)}) copy-start(f32[64,640]{1,0:T(8,128)} %get-tuple-element.114) | copy-start | bytes 491524
  168.2 3.0 %copy-start.4 = (f32[64,640]{1,0:T(8,128)S(1)}, f32[64,640]{1,0:T(8,128)}, u32[]{:S(2)}) copy-start(f32[64,640]{1,0:T(8,128)} %get-tuple-element.115) | copy-start | bytes 491524
  169.1 2.8 %copy-start.3 = (f32[40,1024]{1,0:T(8,128)S(1)}, f32[40,1024]{1,0:T(8,128)}, u32[]{:S(2)}) copy-start(f32[40,1024]{1,0:T(8,128)} %get-tuple-element.116) | copy-start | bytes 491524
